TPU v7x, 8 devices: a whole 2x2x1 slice. The times are simulated.
8 devices in a mesh: part: 1 (over z), model: 2 (over y), data: 4 (over x, core).
Axes of the slice: x: 2, y: 2, z: 1, core: 2. Of those that a mesh axis runs over, the one named last changes fastest.
Arguments:
- hidden: bfloat16 [256, 1, 2560], P(('part', 'data'))
- positions: int32 [256], P(('part', 'data'))
- k_local: bfloat16 [256, 64, 4, 256], P(('part', 'data'), None, 'model')
- v_local: bfloat16 [256, 64, 4, 256], P(('part', 'data'), None, 'model')
- k_global: bfloat16 [256, 512, 4, 256], P(('part', 'data'), None, 'model')
- v_global: bfloat16 [256, 512, 4, 256], P(('part', 'data'), None, 'model')
- w_q: bfloat16 [2, 2560, 8, 256], P(None, 'data', 'model')
- w_k: bfloat16 [2, 2560, 4, 256], P(None, 'data', 'model')
- w_v: bfloat16 [2, 2560, 4, 256], P(None, 'data', 'model')
- w_o: bfloat16 [2, 8, 256, 2560], P(None, 'model', None, 'data')
- w_gate: bfloat16 [2, 2560, 10240], P(None, 'data', 'model')
- w_up: bfloat16 [2, 2560, 10240], P(None, 'data', 'model')
- w_down: bfloat16 [2, 10240, 2560], P(None, 'model', 'data')
- norm_gains: bfloat16 [2, 4, 2560], replicated
Outputs:
- output 1: bfloat16 [256, 1, 2560], P(('part', 'data'))
- output 2: bfloat16 [256, 64, 4, 256], P(('part', 'data'), None, 'model')
- output 3: bfloat16 [256, 64, 4, 256], P(('part', 'data'), None, 'model')
- output 4: bfloat16 [256, 512, 4, 256], P(('part', 'data'), None, 'model')
- output 5: bfloat16 [256, 512, 4, 256], P(('part', 'data'), None, 'model')
All inputs are finite; a program needn't handle non-finite values.
Results may differ from a plain program's by a relative error of at most 0.02.
Values are sent between devices in bfloat16 or wider.
A program may use at most 1 GiB of HBM per device.

v0:
```python
import jax
import jax.numpy as jnp
from jax import lax
from jax.sharding import PartitionSpec as P

SOFT_CAP = 50.0
NORM_EPS = 1e-6
ROPE_BASE = 10000.0

ROW_SPEC = P(("part", "data"), None, None)
POS_SPEC = P(("part", "data"))
CACHE_SPEC = P(("part", "data"), None, "model", None)
PROJ_IN_SPEC = P(None, "data", "model", None)
PROJ_OUT_SPEC = P(None, "model", None, "data")
FF_IN_SPEC = P(None, "data", "model")
FF_OUT_SPEC = P(None, "model", "data")
GAIN_SPEC = P(None, None, None)


def rms_norm(hidden, gain):
    mean_sq = jnp.mean(jnp.square(hidden), axis=-1, keepdims=True)
    return hidden * lax.rsqrt(mean_sq + NORM_EPS) * (1.0 + gain.astype(jnp.float32))


def rotary(hidden, cos_t, sin_t):
    half_dim = hidden.shape[-1] // 2
    first_half = hidden[..., :half_dim]
    second_half = hidden[..., half_dim:]
    return jnp.concatenate([first_half * cos_t - second_half * sin_t, second_half * cos_t + first_half * sin_t], axis=-1)


def rope_tables(positions, head_dim):
    inv_freq = ROPE_BASE ** (-jnp.arange(0, head_dim, 2).astype(jnp.float32) / head_dim)
    angles = positions.astype(jnp.float32)[:, None] * inv_freq[None, :]
    return jnp.cos(angles)[:, None, :], jnp.sin(angles)[:, None, :]


def attend(q_new, k_new, v_new, positions, k_cache, v_cache, is_local):
    n_rows, cache_len, kv_loc, head_dim = k_cache.shape
    group_size = q_new.shape[1] // kv_loc
    slot_ids = jnp.arange(cache_len)
    if is_local:
        slot_now = positions % cache_len
        valid_mask = ((positions[:, None] - slot_ids[None, :]) % cache_len) <= positions[:, None]
    else:
        slot_now = positions
        valid_mask = slot_ids[None, :] <= positions[:, None]
    slot_hit = (slot_ids[None, :] == slot_now[:, None])[:, :, None, None]
    k_cache = jnp.where(slot_hit, k_new[:, None], k_cache)
    v_cache = jnp.where(slot_hit, v_new[:, None], v_cache)
    q_grp = q_new.reshape(n_rows, kv_loc, group_size, head_dim)
    scores = jnp.einsum("bkgd,btkd->bkgt", q_grp, k_cache, preferred_element_type=jnp.float32)
    scores = SOFT_CAP * jnp.tanh(scores / SOFT_CAP)
    scores = jnp.where(valid_mask[:, None, None, :], scores, -1e30)
    attn_prob = jax.nn.softmax(scores, axis=-1).astype(jnp.bfloat16)
    head_out = jnp.einsum("bkgt,btkd->bkgd", attn_prob, v_cache, preferred_element_type=jnp.float32)
    return head_out.astype(jnp.bfloat16).reshape(n_rows, kv_loc * group_size, head_dim), k_cache, v_cache


def layer_block(hidden, positions, k_cache, v_cache, weights, layer, is_local):
    w_q, w_k, w_v, w_o, w_gate, w_up, w_down, norm_gains = weights
    layer_gains = norm_gains[layer]
    wq_full = lax.all_gather(w_q[layer], "data", axis=0, tiled=True)
    wk_full = lax.all_gather(w_k[layer], "data", axis=0, tiled=True)
    wv_full = lax.all_gather(w_v[layer], "data", axis=0, tiled=True)
    wo_full = lax.all_gather(w_o[layer], "data", axis=2, tiled=True)
    wg_full = lax.all_gather(w_gate[layer], "data", axis=0, tiled=True)
    wu_full = lax.all_gather(w_up[layer], "data", axis=0, tiled=True)
    wd_full = lax.all_gather(w_down[layer], "data", axis=1, tiled=True)
    residual = hidden[:, 0, :].astype(jnp.float32)
    normed = rms_norm(residual, layer_gains[0]).astype(jnp.bfloat16)
    q_proj = jnp.einsum("bd,dhk->bhk", normed, wq_full, preferred_element_type=jnp.float32)
    k_proj = jnp.einsum("bd,dhk->bhk", normed, wk_full, preferred_element_type=jnp.float32)
    v_proj = jnp.einsum("bd,dhk->bhk", normed, wv_full, preferred_element_type=jnp.float32)
    head_dim = q_proj.shape[-1]
    cos_t, sin_t = rope_tables(positions, head_dim)
    q_new = (rotary(q_proj, cos_t, sin_t) * head_dim ** -0.5).astype(jnp.bfloat16)
    k_new = rotary(k_proj, cos_t, sin_t).astype(jnp.bfloat16)
    head_out, k_cache, v_cache = attend(q_new, k_new, v_proj.astype(jnp.bfloat16), positions, k_cache, v_cache, is_local)
    attn_sum = lax.psum(jnp.einsum("bhk,hkd->bd", head_out, wo_full, preferred_element_type=jnp.float32), "model")
    mid_hidden = (residual + rms_norm(attn_sum, layer_gains[1])).astype(jnp.bfloat16)
    mid_f = mid_hidden.astype(jnp.float32)
    normed_ff = rms_norm(mid_f, layer_gains[2]).astype(jnp.bfloat16)
    gate_proj = jnp.dot(normed_ff, wg_full, preferred_element_type=jnp.float32)
    up_proj = jnp.dot(normed_ff, wu_full, preferred_element_type=jnp.float32)
    gated_act = (jax.nn.gelu(gate_proj, approximate=True) * up_proj).astype(jnp.bfloat16)
    down_sum = lax.psum(jnp.dot(gated_act, wd_full, preferred_element_type=jnp.float32), "model")
    layer_out = (mid_f + rms_norm(down_sum, layer_gains[3])).astype(jnp.bfloat16)
    return layer_out[:, None, :], k_cache, v_cache


def solution(mesh):
    def device_step(hidden, positions, k_local, v_local, k_global, v_global, w_q, w_k, w_v, w_o, w_gate, w_up, w_down, norm_gains):
        weights = (w_q, w_k, w_v, w_o, w_gate, w_up, w_down, norm_gains)
        mid_hidden, k_local, v_local = layer_block(hidden, positions, k_local, v_local, weights, 0, True)
        final, k_global, v_global = layer_block(mid_hidden, positions, k_global, v_global, weights, 1, False)
        return final, k_local, v_local, k_global, v_global

    in_specs = (ROW_SPEC, POS_SPEC, CACHE_SPEC, CACHE_SPEC, CACHE_SPEC, CACHE_SPEC, PROJ_IN_SPEC, PROJ_IN_SPEC, PROJ_IN_SPEC, PROJ_OUT_SPEC, FF_IN_SPEC, FF_IN_SPEC, FF_OUT_SPEC, GAIN_SPEC)
    out_specs = (ROW_SPEC, CACHE_SPEC, CACHE_SPEC, CACHE_SPEC, CACHE_SPEC)
    return jax.shard_map(device_step, mesh=mesh, in_specs=in_specs, out_specs=out_specs, check_vma=False)
```

profile of v0, /device:TPU:0, one launch (start us, length us, event | category | flops | bytes accessed | tf_op | source)
XLA Modules:
  0.0 1437.6 jit_solution(13349016818579141324)
XLA Ops:
  7.2 3.1 fusion.175
  11.4 1.8 fusion.176
  14.1 2.6 fusion.174
  18.1 3.5 fusion.173
  23.1 13.6 all-gather.31.cloned.1.call-done
  36.7 2.3 fusion.58
  39.2 22.1 %all-gather.33.cloned.1.call-done = bf16[1,2560,2,256]{3,1,2,0:T(8,128)(2,1)} async-done(((bf16[1,640,2,256]{3,1,2,0:T(8,128)(2,1)}), bf16[1,2560,2,256]{3,1,2,0:T(8,128)(2,1)}) %all-gather.33.cloned.1.call-update) | async-done | bytes 2621456 | tf_op jit(solution)/shard_map/all_gather | solution.py:65
  61.3 2.4 fusion.103
  63.7 11.8 broadcast_select_fusion.3
  75.5 25.5 %all-gather.29.cloned.1.call-done = bf16[1,2560,4,256]{3,1,2,0:T(8,128)(2,1)} async-done(((bf16[1,640,4,256]{3,1,2,0:T(8,128)(2,1)}), bf16[1,2560,4,256]{3,1,2,0:T(8,128)(2,1)}) %all-gather.29.cloned.1.call-update) | async-done | bytes 5242896 | tf_op jit(solution)/shard_map/all_gather | solution.py:63
  101.0 3.6 fusion.36
  104.8 3.6 fusion.178
  108.4 2.9 fusion.90
  111.4 29.2 %all-gather.35.cloned.1.call-done = bf16[1,4,256,2560]{3,2,1,0:T(8,128)(2,1)} async-done(((bf16[1,4,256,640]{3,2,1,0:T(8,128)(2,1)}), bf16[1,4,256,2560]{3,2,1,0:T(8,128)(2,1)}) %all-gather.35.cloned.1.call-update) | async-done | bytes 5242896 | tf_op jit(solution)/shard_map/all_gather | solution.py:66
  140.5 4.3 fusion.42
  144.9 10.3 fusion.171
  155.3 10.3 fusion.170
  165.7 10.7 fusion.172
  176.6 1.2 multiply_reduce_fusion.3
  177.9 1.4 fusion.118
  179.3 152.1 %all-gather.37.cloned.1.call-done = bf16[1,2560,5120]{2,1,0:T(8,128)(2,1)} async-done(((bf16[1,640,5120]{2,1,0:T(8,128)(2,1)}), bf16[1,2560,5120]{2,1,0:T(8,128)(2,1)}) %all-gather.37.cloned.1.call-update) | async-done | bytes 26214416 | tf_op jit(solution)/shard_map/all_gather | solution.py:67
  331.4 11.0 fusion.66
  342.4 149.2 %all-gather.39.cloned.1.call-done = bf16[1,2560,5120]{2,1,0:T(8,128)(2,1)} async-done(((bf16[1,640,5120]{2,1,0:T(8,128)(2,1)}), bf16[1,2560,5120]{2,1,0:T(8,128)(2,1)}) %all-gather.39.cloned.1.call-update) | async-done | bytes 26214416 | tf_op jit(solution)/shard_map/all_gather | solution.py:68
  491.6 160.6 %all-gather.41.cloned.1.call-done = bf16[1,5120,2560]{2,1,0:T(8,128)(2,1)} async-done(((bf16[1,5120,640]{2,1,0:T(8,128)(2,1)}), bf16[1,5120,2560]{2,1,0:T(8,128)(2,1)}) %all-gather.41.cloned.1.call-update) | async-done | bytes 26214416 | tf_op jit(solution)/shard_map/all_gather | solution.py:69
  652.2 21.8 %fusion.12 = f32[64,2560]{1,0:T(8,128)} fusion(bf16[1,5120,2560]{2,1,0:T(8,128)(2,1)} %all-gather.41.cloned.1.call-done, f32[64,5120]{1,0:T(8,128)S(1)} %fusion.66, bf16[1,2560,5120]{2,1,0:T(8,128)(2,1)} %all-gather.39.cloned.1.call-done, bf16[64,2560]{1,0:T(8,128)(2,1)S(1)} %get-tuple-element.18, f32[2560]{0:T(1024)S(1)} %get-tuple-element.9, ...), kind=kOutput, calls=%fused_computation.14 | convolution fusion | flops 3356753920 | bytes 54733056 | tf_op jit(solution)/shard_map/dot_general | solution.py:87
  674.0 2.0 copy.46
  676.1 2.0 copy.45
  680.4 19.4 %all-reduce.7.cloned.1.call-done = f32[64,2560]{1,0:T(8,128)} async-done(((f32[64,2560]{1,0:T(8,128)}), f32[64,2560]{1,0:T(8,128)}) %all-reduce.7.cloned.1.call-update) | async-done | bytes 655376 | tf_op jit(solution)/shard_map/psum | solution.py:87
  699.8 1.2 multiply_reduce_fusion.2
  701.1 1.4 fusion.122
  702.5 21.2 %all-gather.47.cloned.1.call-done = bf16[1,2560,2,256]{3,1,2,0:T(8,128)(2,1)} async-done(((bf16[1,640,2,256]{3,1,2,0:T(8,128)(2,1)}), bf16[1,2560,2,256]{3,1,2,0:T(8,128)(2,1)}) %all-gather.47.cloned.1.call-update) | async-done | bytes 2621456 | tf_op jit(solution)/shard_map/all_gather | solution.py:65
  723.6 2.4 fusion.106
  726.1 22.1 %all-gather.45.cloned.1.call-done = bf16[1,2560,2,256]{3,1,2,0:T(8,128)(2,1)} async-done(((bf16[1,640,2,256]{3,1,2,0:T(8,128)(2,1)}), bf16[1,2560,2,256]{3,1,2,0:T(8,128)(2,1)}) %all-gather.45.cloned.1.call-update) | async-done | bytes 2621456 | tf_op jit(solution)/shard_map/all_gather | solution.py:64
  748.2 2.3 fusion.54
  750.7 81.8 %broadcast_select_fusion.1 = (bf16[64,512,2,256]{3,2,1,0:T(2,128)(2,1)}, bf16[64,512,2,256]{3,2,1,0:T(2,128)(2,1)}) fusion(bf16[64,512,2,256]{3,2,1,0:T(2,128)(2,1)} %param.18, pred[64,512]{1,0:T(8,128)(4,1)S(1)} %get-tuple-element.48, bf16[64,2,256]{2,1,0:T(2,128)(2,1)S(1)} %copy.33, bf16[64,512,2,256]{3,2,1,0:T(2,128)(2,1)} %param.19, ...), kind=kLoop, calls=%fused_computation.3 | loop fusion | flops 33554432 | bytes 134381568 | tf_op jit(solution)/shard_map/jit(_where)/select_n | solution.py:49
  832.6 3.6 fusion.32
  836.4 18.2 %fusion.179 = (f32[64,2,2]{2,1,0:T(2,128)S(1)}, f32[64,2,2,512]{3,2,1,0:T(2,128)S(1)}) fusion(bf16[64,512,2,256]{3,2,1,0:T(2,128)(2,1)} %get-tuple-element.41, pred[64,512]{1,0:T(8,128)(4,1)S(1)} %get-tuple-element.47, f32[64,2,2,128]{3,2,1,0:T(2,128)S(1)} %copy.31, f32[64,2,2,128]{3,2,1,0:T(2,128)S(1)} %copy.30), kind=kOutput, calls=%fused_computation.182 | convolution fusion | flops 67961344 | bytes 34374656 | tf_op jit(solution)/shard_map/sub | solution.py:55
  854.6 15.1 %fusion.93 = bf16[64,2,2,256]{3,2,1,0:T(2,128)(2,1)S(1)} fusion(bf16[64,512,2,256]{3,2,1,0:T(2,128)(2,1)} %get-tuple-element.42, f32[64,2,2,512]{3,2,1,0:T(2,128)S(1)} %get-tuple-element.54, f32[64,2,2]{2,1,0:T(2,128)S(1)} %get-tuple-element.53), kind=kOutput, calls=%fused_computation.71 | convolution fusion | flops 67436544 | bytes 34210816 | tf_op jit(solution)/shard_map/bkgt,btkd->bkgd/dot_general | solution.py:56
  869.7 4.3 fusion.45
  876.2 23.8 %all-reduce.9.cloned.1.call-done = f32[64,2560]{1,0:T(8,128)} async-done(((f32[64,2560]{1,0:T(8,128)}), f32[64,2560]{1,0:T(8,128)}) %all-reduce.9.cloned.1.call-update) | async-done | bytes 655376 | tf_op jit(solution)/shard_map/psum | solution.py:80
  901.2 1.4 fusion.126
  902.6 157.4 %all-gather.51.cloned.1.call-done = bf16[1,2560,5120]{2,1,0:T(8,128)(2,1)} async-done(((bf16[1,640,5120]{2,1,0:T(8,128)(2,1)}), bf16[1,2560,5120]{2,1,0:T(8,128)(2,1)}) %all-gather.51.cloned.1.call-update) | async-done | bytes 26214416 | tf_op jit(solution)/shard_map/all_gather | solution.py:67
  1060.0 11.0 fusion.75
  1071.1 149.1 %all-gather.53.cloned.1.call-done = bf16[1,2560,5120]{2,1,0:T(8,128)(2,1)} async-done(((bf16[1,640,5120]{2,1,0:T(8,128)(2,1)}), bf16[1,2560,5120]{2,1,0:T(8,128)(2,1)}) %all-gather.53.cloned.1.call-update) | async-done | bytes 26214416 | tf_op jit(solution)/shard_map/all_gather | solution.py:68
  1220.1 159.8 %all-gather.55.cloned.1.call-done = bf16[1,5120,2560]{2,1,0:T(8,128)(2,1)} async-done(((bf16[1,5120,640]{2,1,0:T(8,128)(2,1)}), bf16[1,5120,2560]{2,1,0:T(8,128)(2,1)}) %all-gather.55.cloned.1.call-update) | async-done | bytes 26214416 | tf_op jit(solution)/shard_map/all_gather | solution.py:69
  1379.9 21.6 %fusion.6 = f32[64,2560]{1,0:T(8,128)} fusion(bf16[1,5120,2560]{2,1,0:T(8,128)(2,1)} %all-gather.55.cloned.1.call-done, f32[64,5120]{1,0:T(8,128)S(1)} %fusion.75, bf16[1,2560,5120]{2,1,0:T(8,128)(2,1)} %all-gather.53.cloned.1.call-done, bf16[64,2560]{1,0:T(8,128)(2,1)S(1)} %get-tuple-element.14, f32[2560]{0:T(1024)S(1)} %copy-done.2, f32[64]{0:T(128)S(1)} %add_rsqrt_fusion.1), kind=kOutput, calls=%fused_computation.8 | convolution fusion | flops 3356753920 | bytes 54733056 | tf_op jit(solution)/shard_map/dot_general | solution.py:87
  1401.6 25.9 %all-reduce.11.cloned.1.call-done = f32[64,2560]{1,0:T(8,128)} async-done(((f32[64,2560]{1,0:T(8,128)}), f32[64,2560]{1,0:T(8,128)}) %all-reduce.11.cloned.1.call-update) | async-done | bytes 655376 | tf_op jit(solution)/shard_map/psum | solution.py:87
  1428.7 2.0 fusion.135
  (91 shorter events, 12.9 us)
Async XLA Ops:
  7.2 4.2 copy-start.1
  7.2 29.6 %all-gather.31.cloned.1.call-start = ((), (), s32[]{:S(2)}) async-start(), calls=%async_computation.5 | async-start | bytes 3276800 | tf_op jit(solution)/shard_map/all_gather | solution.py:64
  11.3 50.0 %all-gather.33.cloned.1.call-start = ((), (), s32[]{:S(2)}) async-start(), calls=%async_computation.6 | async-start | bytes 3276800 | tf_op jit(solution)/shard_map/all_gather | solution.py:65
  14.1 86.9 %all-gather.29.cloned.1.call-start = ((), (), s32[]{:S(2)}) async-start(), calls=%async_computation.4 | async-start | bytes 6553600 | tf_op jit(solution)/shard_map/all_gather | solution.py:63
  18.0 3.7 copy-start.3
  18.0 4.5 copy-start
  18.0 4.7 copy-start.6
  18.0 122.5 %all-gather.35.cloned.1.call-start = ((), (), s32[]{:S(2)}) async-start(), calls=%async_computation.7 | async-start | bytes 6553600 | tf_op jit(solution)/shard_map/all_gather | solution.py:66
  21.6 155.0 %all-reduce.5.cloned.1.call-start = ((), (), s32[]{:S(2)}) async-start(), calls=%async_computation | async-start | bytes 1310720 | tf_op jit(solution)/shard_map/psum | solution.py:80
  144.9 186.5 %all-gather.37.cloned.1.call-start = ((), (), s32[]{:S(2)}) async-start(), calls=%async_computation.8 | async-start | bytes 32768000 | tf_op jit(solution)/shard_map/all_gather | solution.py:67
  155.3 336.3 %all-gather.39.cloned.1.call-start = ((), (), s32[]{:S(2)}) async-start(), calls=%async_computation.9 | async-start | bytes 32768000 | tf_op jit(solution)/shard_map/all_gather | solution.py:68
  165.7 486.5 %all-gather.41.cloned.1.call-start = ((), (), s32[]{:S(2)}) async-start(), calls=%async_computation.10 | async-start | bytes 32768000 | tf_op jit(solution)/shard_map/all_gather | solution.py:69
  176.4 523.4 %all-reduce.7.cloned.1.call-start = ((), (), s32[]{:S(2)}) async-start(), calls=%async_computation.1 | async-start | bytes 1310720 | tf_op jit(solution)/shard_map/psum | solution.py:87
  674.0 49.7 %all-gather.47.cloned.1.call-start = ((), (), s32[]{:S(2)}) async-start(), calls=%async_computation.13 | async-start | bytes 3276800 | tf_op jit(solution)/shard_map/all_gather | solution.py:65
  676.1 72.1 %all-gather.45.cloned.1.call-start = ((), (), s32[]{:S(2)}) async-start(), calls=%async_computation.12 | async-start | bytes 3276800 | tf_op jit(solution)/shard_map/all_gather | solution.py:64
  678.2 154.4 %all-gather.43.cloned.1.call-start = ((), (), s32[]{:S(2)}) async-start(), calls=%async_computation.11 | async-start | bytes 6553600 | tf_op jit(solution)/shard_map/all_gather | solution.py:63
  679.5 190.3 %all-gather.49.cloned.1.call-start = ((), (), s32[]{:S(2)}) async-start(), calls=%async_computation.14 | async-start | bytes 6553600 | tf_op jit(solution)/shard_map/all_gather | solution.py:66
  680.2 219.7 %all-reduce.9.cloned.1.call-start = ((), (), s32[]{:S(2)}) async-start(), calls=%async_computation.2 | async-start | bytes 1310720 | tf_op jit(solution)/shard_map/psum | solution.py:80
  874.1 185.9 %all-gather.51.cloned.1.call-start = ((), (), s32[]{:S(2)}) async-start(), calls=%async_computation.15 | async-start | bytes 32768000 | tf_op jit(solution)/shard_map/all_gather | solution.py:67
  874.7 345.4 %all-gather.53.cloned.1.call-start = ((), (), s32[]{:S(2)}) async-start(), calls=%async_computation.16 | async-start | bytes 32768000 | tf_op jit(solution)/shard_map/all_gather | solution.py:68
  875.3 25.9 %copy-start.5 = (f32[2560]{0:T(1024)S(1)}, f32[2560]{0:T(1024)}, u32[]{:S(2)}) copy-start(f32[2560]{0:T(1024)} %get-tuple-element.6) | copy-start | bytes 30724
  875.3 504.7 %all-gather.55.cloned.1.call-start = ((), (), s32[]{:S(2)}) async-start(), calls=%async_computation.17 | async-start | bytes 32768000 | tf_op jit(solution)/shard_map/all_gather | solution.py:69
  875.3 184.7 %copy-start.2 = (f32[2560]{0:T(1024)S(1)}, f32[2560]{0:T(1024)}, u32[]{:S(2)}) copy-start(f32[2560]{0:T(1024)} %get-tuple-element.12) | copy-start | bytes 30724
  875.9 551.6 %all-reduce.11.cloned.1.call-start = ((), (), s32[]{:S(2)}) async-start(), calls=%async_computation.3 | async-start | bytes 1310720 | tf_op jit(solution)/shard_map/psum | solution.py:87
  1071.0 357.7 %copy-start.4 = (f32[2560]{0:T(1024)S(1)}, f32[2560]{0:T(1024)}, u32[]{:S(2)}) copy-start(f32[2560]{0:T(1024)} %get-tuple-element.5) | copy-start | bytes 30724
Sparse Core Ops, SparseCore 0:
  11.4 25.2 all-gather.30
  38.8 22.4 all-gather.32
  63.4 37.5 all-gather.28
  103.0 37.5 all-gather.34
  145.0 25.6 all-reduce.4
  172.7 158.6 all-gather.36
  332.9 158.6 all-gather.38
  493.7 158.3 all-gather.40
  674.1 25.6 all-reduce.6
  701.2 22.4 all-gather.46
  725.8 22.4 all-gather.44
  749.6 37.5 all-gather.42
  788.7 37.5 all-gather.48
  874.2 25.6 all-reduce.8
  901.4 158.6 all-gather.50
  1061.4 158.6 all-gather.52
  1221.5 158.3 all-gather.54
  1401.7 25.6 all-reduce.10
where the time goes:
time: 1440 us
  waiting for transfers between devices  1130 us (78%)
  matrix products  130 us (9%)
  other arithmetic  106 us (7%)
  local copies, waits for them, and re-layouts  51.5 us (4%)
  between operations  14.7 us (1%)
    all_gather x2, waiting for transfers between devices, layer_block(): wd_full = lax.all_gather(w_down[layer], 'data', axis=1, tiled=True)  320 us
    all_gather x2, waiting for transfers between devices, layer_block(): wg_full = lax.all_gather(w_gate[layer], 'data', axis=0, tiled=True)  309 us
    all_gather x2, waiting for transfers between devices, layer_block(): wu_full = lax.all_gather(w_up[layer], 'data', axis=0, tiled=True)  298 us
    select_n x2, other arithmetic, attend(): k_cache = jnp.where(slot_hit, k_new[:, None], k_cache)  93.6 us
    psum x2, waiting for transfers between devices, layer_block(): lax.psum(jnp.dot(gated_act, wd_full, preferred_element_type=jnp.float32),...  45.3 us
    dot_general x2, matrix products, layer_block(): jnp.dot(gated_act, wd_full, preferred_element_type=jnp.float32)  43.4 us
    all_gather x2, waiting for transfers between devices, layer_block(): wv_full = lax.all_gather(w_v[layer], 'data', axis=0, tiled=True)  43.2 us
    all_gather x2, waiting for transfers between devices, layer_block(): wk_full = lax.all_gather(w_k[layer], 'data', axis=0, tiled=True)  35.8 us
  transfers between devices with their start and end apart: 18, of which 15 were waited for; matrix products, arithmetic and copies ran while one was open for 16% of the time, Pallas kernels for 0%

commit v1 on v0

v1 whole, which is shorter than its diff:
```python
import jax
import jax.numpy as jnp
from jax import lax
from jax.sharding import PartitionSpec as P

SOFT_CAP = 50.0
NORM_EPS = 1e-6
ROPE_BASE = 10000.0

ROW_SPEC = P(("part", "data"), None, None)
POS_SPEC = P(("part", "data"))
CACHE_SPEC = P(("part", "data"), None, "model", None)
PROJ_IN_SPEC = P(None, "data", "model", None)
PROJ_OUT_SPEC = P(None, "model", None, "data")
FF_IN_SPEC = P(None, "data", "model")
FF_OUT_SPEC = P(None, "model", "data")
GAIN_SPEC = P(None, None, None)


def rotary(hidden, cos_t, sin_t):
    half_dim = hidden.shape[-1] // 2
    first_half = hidden[..., :half_dim]
    second_half = hidden[..., half_dim:]
    return jnp.concatenate([first_half * cos_t - second_half * sin_t, second_half * cos_t + first_half * sin_t], axis=-1)


def rope_tables(positions, head_dim):
    inv_freq = ROPE_BASE ** (-jnp.arange(0, head_dim, 2).astype(jnp.float32) / head_dim)
    angles = positions.astype(jnp.float32)[:, None] * inv_freq[None, :]
    return jnp.cos(angles)[:, None, :], jnp.sin(angles)[:, None, :]


def attend(q_new, k_new, v_new, positions, k_cache, v_cache, is_local):
    n_rows, cache_len, kv_loc, head_dim = k_cache.shape
    group_size = q_new.shape[1] // kv_loc
    slot_ids = jnp.arange(cache_len)
    if is_local:
        slot_now = positions % cache_len
        valid_mask = ((positions[:, None] - slot_ids[None, :]) % cache_len) <= positions[:, None]
    else:
        slot_now = positions
        valid_mask = slot_ids[None, :] <= positions[:, None]
    slot_hit = (slot_ids[None, :] == slot_now[:, None])[:, :, None, None]
    k_cache = jnp.where(slot_hit, k_new[:, None], k_cache)
    v_cache = jnp.where(slot_hit, v_new[:, None], v_cache)
    q_grp = q_new.reshape(n_rows, kv_loc, group_size, head_dim)
    scores = jnp.einsum("bkgd,btkd->bkgt", q_grp, k_cache, preferred_element_type=jnp.float32)
    scores = SOFT_CAP * jnp.tanh(scores / SOFT_CAP)
    scores = jnp.where(valid_mask[:, None, None, :], scores, -1e30)
    attn_prob = jax.nn.softmax(scores, axis=-1).astype(jnp.bfloat16)
    head_out = jnp.einsum("bkgt,btkd->bkgd", attn_prob, v_cache, preferred_element_type=jnp.float32)
    return head_out.astype(jnp.bfloat16).reshape(n_rows, kv_loc * group_size, head_dim), k_cache, v_cache


def width_norm(hidden, gain, width):
    sum_sq = lax.psum(jnp.sum(jnp.square(hidden), axis=-1, keepdims=True), "data")
    return hidden * lax.rsqrt(sum_sq / width + NORM_EPS) * (1.0 + gain.astype(jnp.float32))


def layer_block(hidden, positions, k_cache, v_cache, weights, layer, is_local):
    w_q, w_k, w_v, w_o, w_gate, w_up, w_down, norm_gains = weights
    share = hidden.shape[1]
    n_data = lax.axis_size("data")
    width = share * n_data
    gains = lax.dynamic_slice_in_dim(norm_gains[layer], lax.axis_index("data") * share, share, axis=1)
    n_q, head_dim = w_q.shape[2:]
    n_kv = w_k.shape[2]
    residual = hidden.astype(jnp.float32)
    normed = width_norm(residual, gains[0], width).astype(jnp.bfloat16)
    w_in = jnp.concatenate([w_q[layer].reshape(share, -1), w_k[layer].reshape(share, -1), w_v[layer].reshape(share, -1)], axis=1)
    qkv = jnp.dot(normed, w_in, preferred_element_type=jnp.float32)
    qkv = lax.psum_scatter(qkv, "data", scatter_dimension=0, tiled=True)
    n_rows = qkv.shape[0]
    q_proj = qkv[:, :n_q * head_dim].reshape(n_rows, n_q, head_dim)
    k_proj = qkv[:, n_q * head_dim:(n_q + n_kv) * head_dim].reshape(n_rows, n_kv, head_dim)
    v_proj = qkv[:, (n_q + n_kv) * head_dim:].reshape(n_rows, n_kv, head_dim)
    cos_t, sin_t = rope_tables(positions, head_dim)
    q_new = (rotary(q_proj, cos_t, sin_t) * head_dim ** -0.5).astype(jnp.bfloat16)
    k_new = rotary(k_proj, cos_t, sin_t).astype(jnp.bfloat16)
    head_out, k_cache, v_cache = attend(q_new, k_new, v_proj.astype(jnp.bfloat16), positions, k_cache, v_cache, is_local)
    heads_all = lax.all_gather(head_out.reshape(n_rows, -1), "data", axis=0, tiled=True)
    attn_sum = lax.psum(jnp.dot(heads_all, w_o[layer].reshape(-1, share), preferred_element_type=jnp.float32), "model")
    mid_hidden = (residual + width_norm(attn_sum, gains[1], width)).astype(jnp.bfloat16)
    mid_f = mid_hidden.astype(jnp.float32)
    normed_ff = width_norm(mid_f, gains[2], width).astype(jnp.bfloat16)
    gate_proj = jnp.dot(normed_ff, w_gate[layer], preferred_element_type=jnp.float32)
    gate_proj = lax.psum_scatter(gate_proj, "data", scatter_dimension=0, tiled=True)
    up_proj = jnp.dot(normed_ff, w_up[layer], preferred_element_type=jnp.float32)
    up_proj = lax.psum_scatter(up_proj, "data", scatter_dimension=0, tiled=True)
    gated_act = (jax.nn.gelu(gate_proj, approximate=True) * up_proj).astype(jnp.bfloat16)
    acts_all = lax.all_gather(gated_act, "data", axis=0, tiled=True)
    down_sum = lax.psum(jnp.dot(acts_all, w_down[layer], preferred_element_type=jnp.float32), "model")
    return (mid_f + width_norm(down_sum, gains[3], width)).astype(jnp.bfloat16), k_cache, v_cache


def solution(mesh):
    def device_step(hidden, positions, k_local, v_local, k_global, v_global, w_q, w_k, w_v, w_o, w_gate, w_up, w_down, norm_gains):
        weights = (w_q, w_k, w_v, w_o, w_gate, w_up, w_down, norm_gains)
        hidden_cols = lax.all_to_all(hidden[:, 0, :], "data", 1, 0, tiled=True)
        hidden_cols, k_local, v_local = layer_block(hidden_cols, positions, k_local, v_local, weights, 0, True)
        hidden_cols, k_global, v_global = layer_block(hidden_cols, positions, k_global, v_global, weights, 1, False)
        final = lax.all_to_all(hidden_cols, "data", 0, 1, tiled=True)[:, None, :]
        return final, k_local, v_local, k_global, v_global

    in_specs = (ROW_SPEC, POS_SPEC, CACHE_SPEC, CACHE_SPEC, CACHE_SPEC, CACHE_SPEC, PROJ_IN_SPEC, PROJ_IN_SPEC, PROJ_IN_SPEC, PROJ_OUT_SPEC, FF_IN_SPEC, FF_IN_SPEC, FF_OUT_SPEC, GAIN_SPEC)
    out_specs = (ROW_SPEC, CACHE_SPEC, CACHE_SPEC, CACHE_SPEC, CACHE_SPEC)
    return jax.shard_map(device_step, mesh=mesh, in_specs=in_specs, out_specs=out_specs, check_vma=False)
```

time: 1440 us -> 702 us (0.49)
  waiting for transfers between devices: 1130 us -> 348 us
  blocking collectives: 0 us -> 78.5 us
  matrix products: 130 us -> 95.8 us
  local copies, waits for them, and re-layouts: 51.5 us -> 25.3 us
  starting transfers between devices: 1.18 us -> 17.6 us
    all_gather x14 -> x2, waiting for transfers between devices: 1060 us -> 45.1 us  [layer_block(): acts_all = lax.all_gather(gated_act, 'data', axis=0, tiled=True)]
    reduce_scatter x0 -> x6, waiting for transfers between devices: none -> 203 us  [the longest x2 95 us: layer_block(): lax.psum_scatter(gate_proj, 'data', scatter_dimension=0, tiled=True)]
    psum x0 -> x8, blocking collectives: none -> 50.8 us  [width_norm(): lax.psum(jnp.sum(jnp.square(hidden), axis=-1, keepdims=True), 'data')]
    dot_general x12 -> x10, matrix products: 90.6 us -> 55.3 us  [the longest x2 15 us: layer_block(): jnp.dot(normed_ff, w_gate[layer], preferred_element_type=jnp.float32)]
    psum x4, waiting for transfers between devices: 69.1 us -> 100 us  [the longest x2 53 us: layer_block(): lax.psum(jnp.dot(heads_all, w_o[layer].reshape(-1, share), preferred_elem...]
    slice x7 -> x11, local copies, waits for them, and re-layouts: 42.3 us -> 14.4 us  [the longest x1 3.02 us: layer_block(): w_o[layer].reshape(-1, share)]
    all_gather x0 -> x2, blocking collectives: none -> 18.6 us  [layer_block(): lax.all_gather(head_out.reshape(n_rows, -1), 'data', axis=0, tiled=True)]
  transfers between devices with their start and end apart: 18 -> 13, of which waited for: 15 -> 12; matrix products, arithmetic and copies ran while one was open for 16% -> 5% of each run, Pallas kernels for 0% -> 0%
where the time goes in v1:
time: 702 us; the launch traced here: 693 us
  waiting for transfers between devices  348 us (50%)
  other arithmetic  113 us (16%)
  matrix products  95.8 us (14%)
  blocking collectives  78.5 us (11%)
  local copies, waits for them, and re-layouts  25.3 us (4%)
  starting transfers between devices  17.6 us (3%)
  between operations  14.9 us (2%)
    reduce_scatter x2, waiting for transfers between devices, layer_block(): lax.psum_scatter(gate_proj, 'data', scatter_dimension=0, tiled=True)  95 us
    select_n x2, other arithmetic, attend(): k_cache = jnp.where(slot_hit, k_new[:, None], k_cache)  93.6 us
    reduce_scatter x2, waiting for transfers between devices, layer_block(): up_proj = lax.psum_scatter(up_proj, 'data', scatter_dimension=0, tiled=True)  60.8 us
    psum x2, waiting for transfers between devices, layer_block(): lax.psum(jnp.dot(heads_all, w_o[layer].reshape(-1, share), preferred_elem...  53 us
    psum x8, blocking collectives, width_norm(): lax.psum(jnp.sum(jnp.square(hidden), axis=-1, keepdims=True), 'data')  50.8 us
    psum x2, waiting for transfers between devices, layer_block(): lax.psum(jnp.dot(acts_all, w_down[layer], preferred_element_type=jnp.floa...  47.1 us
    reduce_scatter x2, waiting for transfers between devices, layer_block(): qkv = lax.psum_scatter(qkv, 'data', scatter_dimension=0, tiled=True)  46.9 us
    all_gather x2, waiting for transfers between devices, layer_block(): acts_all = lax.all_gather(gated_act, 'data', axis=0, tiled=True)  45.1 us
  transfers between devices with their start and end apart: 13, of which 12 were waited for; matrix products, arithmetic and copies ran while one was open for 5% of the time, Pallas kernels for 0%

profile of v1, /device:TPU:0, one launch (start us, length us, event | category | flops | bytes accessed | tf_op | source)
XLA Modules:
  0.0 692.7 jit_solution(8996500122435319662)
XLA Ops:
  9.1 4.6 all-to-all-start
  15.1 1.7 fusion.156
  17.8 1.7 fusion.157
  22.6 7.6 %psum.84 = f32[256,1]{0,1:T(1,128)S(1)} all-reduce(f32[256,1]{0,1:T(1,128)S(1)} %broadcast_in_dim.137), channel_id=1, replica_groups=mesh['part'=1,'model'=2,'data'=4] {'data'}, use_global_device_ids=true, to_apply=%region_1.0 | all-reduce | flops 256 | bytes 2048 | tf_op jit(solution)/shard_map/psum | solution.py:56
  30.3 3.6 fusion.28
  35.0 3.0 fusion.154
  38.0 22.1 %reduce-scatter.7.cloned.1.call-done = f32[64,2048]{1,0:T(8,128)} async-done(((f32[256,2048]{1,0:T(8,128)}), f32[64,2048]{1,0:T(8,128)}) %reduce-scatter.7.cloned.1.call-update) | async-done | bytes 524304 | tf_op jit(solution)/shard_map/reduce_scatter | solution.py:72
  64.0 12.0 %broadcast_select_fusion.3 = (bf16[64,64,2,256]{3,2,1,0:T(2,128)(2,1)}, bf16[64,64,2,256]{3,2,1,0:T(2,128)(2,1)}) fusion(bf16[64,64,2,256]{3,2,1,0:T(2,128)(2,1)} %param.16, pred[64,64]{1,0:T(8,128)(4,1)S(1)} %iota_compare_fusion.2, bf16[64,2,256]{2,1,0:T(2,128)(2,1)S(1)} %pad_maximum_fusion, bf16[64,64,2,256]{3,2,1,0:T(2,128)(2,1)} %param.17, ...), kind=kLoop, calls=%fused_computation.9 | loop fusion | flops 4194304 | bytes 16912384 | tf_op jit(solution)/shard_map/jit(_where)/select_n | solution.py:44
  76.1 4.2 fusion.160
  80.3 3.0 fusion.70
  83.3 9.3 %all_gather.12 = bf16[256,1024]{1,0:T(8,128)(2,1)S(1)} all-gather(bf16[64,1024]{1,0:T(8,128)(2,1)S(1)} %reshape_reshape.6), channel_id=1, replica_groups=mesh['part'=1,'model'=2,'data'=4] {'data'}, dimensions={0}, use_global_device_ids=true | all-gather | bytes 655360 | tf_op jit(solution)/shard_map/all_gather | solution.py:81
  92.6 2.7 fusion.170
  95.5 26.5 %all-reduce.5.cloned.1.call-done = f32[256,640]{1,0:T(8,128)} async-done(((f32[256,640]{1,0:T(8,128)}), f32[256,640]{1,0:T(8,128)}) %all-reduce.5.cloned.1.call-update) | async-done | bytes 655376 | tf_op jit(solution)/shard_map/psum | solution.py:82
  123.2 6.3 psum.86
  130.9 6.0 psum.87
  136.8 7.5 %fusion.14 = f32[256,5120]{1,0:T(8,128)} fusion(bf16[2,640,5120]{2,1,0:T(8,128)(2,1)} %param.25, bf16[256,640]{1,0:T(8,128)(2,1)S(1)} %get-tuple-element.18, f32[640]{0:T(1024)S(1)} %copy-done.8, f32[256]{0:T(256)S(1)} %bitcast.114), kind=kOutput, calls=%fused_computation.18 | convolution fusion | flops 1678376960 | bytes 12127744 | tf_op jit(solution)/shard_map/dot_general | solution.py:88
  144.4 12.6 %reduce-scatter.9.cloned.1.call-start = ((), (), s32[]{:S(2)}) async-start(), calls=%async_computation.10 | async-start | bytes 6553600 | tf_op jit(solution)/shard_map/reduce_scatter | solution.py:87
  157.0 7.5 %fusion.16 = f32[256,5120]{1,0:T(8,128)} fusion(bf16[2,640,5120]{2,1,0:T(8,128)(2,1)} %param.24, bf16[256,640]{1,0:T(8,128)(2,1)S(1)} %get-tuple-element.18, f32[640]{0:T(1024)S(1)} %copy-done.8, f32[256]{0:T(256)S(1)} %bitcast.115), kind=kOutput, calls=%fused_computation.20 | convolution fusion | flops 1678376960 | bytes 12127744 | tf_op jit(solution)/shard_map/dot_general | solution.py:86
  164.6 24.1 %reduce-scatter.11.cloned.1.call-done = f32[64,5120]{1,0:T(8,128)} async-done(((f32[256,5120]{1,0:T(8,128)}), f32[64,5120]{1,0:T(8,128)}) %reduce-scatter.11.cloned.1.call-update) | async-done | bytes 1310736 | tf_op jit(solution)/shard_map/reduce_scatter | solution.py:89
  188.7 47.8 %reduce-scatter.9.cloned.1.call-done = f32[64,5120]{1,0:T(8,128)} async-done(((f32[256,5120]{1,0:T(8,128)}), f32[64,5120]{1,0:T(8,128)}) %reduce-scatter.9.cloned.1.call-update) | async-done | bytes 1310736 | tf_op jit(solution)/shard_map/reduce_scatter | solution.py:87
  236.4 3.0 fusion.48
  239.5 22.5 %all-gather.3.cloned.1.call-done = bf16[256,5120]{1,0:T(8,128)(2,1)} async-done(((bf16[64,5120]{1,0:T(8,128)(2,1)}), bf16[256,5120]{1,0:T(8,128)(2,1)}) %all-gather.3.cloned.1.call-update) | async-done | bytes 2621456 | tf_op jit(solution)/shard_map/all_gather | solution.py:91
  262.1 6.7 fusion.12
  269.8 2.1 copy.36
  273.4 21.3 %all-reduce.7.cloned.1.call-done = f32[256,640]{1,0:T(8,128)} async-done(((f32[256,640]{1,0:T(8,128)}), f32[256,640]{1,0:T(8,128)}) %all-reduce.7.cloned.1.call-update) | async-done | bytes 655376 | tf_op jit(solution)/shard_map/psum | solution.py:92
  295.9 6.3 psum.89
  302.2 1.4 fusion.96
  303.6 6.0 psum.90
  309.5 4.1 fusion.34
  313.8 24.9 %reduce-scatter.13.cloned.1.call-done = f32[64,2048]{1,0:T(8,128)} async-done(((f32[256,2048]{1,0:T(8,128)}), f32[64,2048]{1,0:T(8,128)}) %reduce-scatter.13.cloned.1.call-update) | async-done | bytes 524304 | tf_op jit(solution)/shard_map/reduce_scatter | solution.py:72
  342.0 81.6 %broadcast_select_fusion.1 = (bf16[64,512,2,256]{3,2,1,0:T(2,128)(2,1)}, bf16[64,512,2,256]{3,2,1,0:T(2,128)(2,1)}) fusion(bf16[64,512,2,256]{3,2,1,0:T(2,128)(2,1)} %param.18, pred[64,512]{1,0:T(8,128)(4,1)S(1)} %get-tuple-element.44, bf16[64,2,256]{2,1,0:T(2,128)(2,1)S(1)} %pad_maximum_fusion.1, bf16[64,512,2,256]{3,2,1,0:T(2,128)(2,1)} %param.19, ...), kind=kLoop, calls=%fused_computation.3 | loop fusion | flops 33554432 | bytes 134381568 | tf_op jit(solution)/shard_map/jit(_where)/select_n | solution.py:44
  423.6 18.2 %fusion.161 = (f32[64,2,2]{2,1,0:T(2,128)S(1)}, f32[64,2,2,512]{3,2,1,0:T(2,128)S(1)}) fusion(bf16[64,512,2,256]{3,2,1,0:T(2,128)(2,1)} %get-tuple-element.37, pred[64,512]{1,0:T(8,128)(4,1)S(1)} %get-tuple-element.43, f32[64,2,2,128]{3,2,1,0:T(2,128)S(1)} %bitcast.98, f32[64,2,2,128]{3,2,1,0:T(2,128)S(1)} %bitcast.97), kind=kOutput, calls=%fused_computation.197 | convolution fusion | flops 67961344 | bytes 34374656 | tf_op jit(solution)/shard_map/sub | solution.py:50
  441.8 15.1 %fusion.73 = bf16[64,2,2,256]{3,2,1,0:T(2,128)(2,1)S(1)} fusion(bf16[64,512,2,256]{3,2,1,0:T(2,128)(2,1)} %get-tuple-element.38, f32[64,2,2,512]{3,2,1,0:T(2,128)S(1)} %get-tuple-element.50, f32[64,2,2]{2,1,0:T(2,128)S(1)} %get-tuple-element.49), kind=kOutput, calls=%fused_computation.71 | convolution fusion | flops 67436544 | bytes 34210816 | tf_op jit(solution)/shard_map/bkgt,btkd->bkgd/dot_general | solution.py:51
  457.0 9.3 %all_gather.14 = bf16[256,1024]{1,0:T(8,128)(2,1)S(1)} all-gather(bf16[64,1024]{1,0:T(8,128)(2,1)S(1)} %reshape_reshape.7), channel_id=1, replica_groups=mesh['part'=1,'model'=2,'data'=4] {'data'}, dimensions={0}, use_global_device_ids=true | all-gather | bytes 655360 | tf_op jit(solution)/shard_map/all_gather | solution.py:81
  466.3 1.5 fusion.171
  467.8 26.4 %all-reduce.9.cloned.1.call-done = f32[256,640]{1,0:T(8,128)} async-done(((f32[256,640]{1,0:T(8,128)}), f32[256,640]{1,0:T(8,128)}) %all-reduce.9.cloned.1.call-update) | async-done | bytes 655376 | tf_op jit(solution)/shard_map/psum | solution.py:82
  495.5 6.3 psum.92
  503.2 6.1 psum.93
  509.3 7.5 %fusion.8 = f32[256,5120]{1,0:T(8,128)} fusion(bf16[2,640,5120]{2,1,0:T(8,128)(2,1)} %param.25, bf16[256,640]{1,0:T(8,128)(2,1)S(1)} %get-tuple-element.14, f32[640]{0:T(1024)S(1)} %get-tuple-element.6, f32[256]{0:T(256)S(1)} %bitcast.116), kind=kOutput, calls=%fused_computation.12 | convolution fusion | flops 1678376960 | bytes 12127744 | tf_op jit(solution)/shard_map/dot_general | solution.py:88
  516.9 7.5 %fusion.10 = f32[256,5120]{1,0:T(8,128)} fusion(bf16[2,640,5120]{2,1,0:T(8,128)(2,1)} %param.24, bf16[256,640]{1,0:T(8,128)(2,1)S(1)} %get-tuple-element.14, f32[640]{0:T(1024)S(1)} %get-tuple-element.6, f32[256]{0:T(256)S(1)} %bitcast.117), kind=kOutput, calls=%fused_computation.14 | convolution fusion | flops 1678376960 | bytes 12127744 | tf_op jit(solution)/shard_map/dot_general | solution.py:86
  524.5 36.7 %reduce-scatter.17.cloned.1.call-done = f32[64,5120]{1,0:T(8,128)} async-done(((f32[256,5120]{1,0:T(8,128)}), f32[64,5120]{1,0:T(8,128)}) %reduce-scatter.17.cloned.1.call-update) | async-done | bytes 1310736 | tf_op jit(solution)/shard_map/reduce_scatter | solution.py:89
  561.2 47.2 %reduce-scatter.15.cloned.1.call-done = f32[64,5120]{1,0:T(8,128)} async-done(((f32[256,5120]{1,0:T(8,128)}), f32[64,5120]{1,0:T(8,128)}) %reduce-scatter.15.cloned.1.call-update) | async-done | bytes 1310736 | tf_op jit(solution)/shard_map/reduce_scatter | solution.py:87
  608.3 3.0 fusion.57
  611.4 22.5 %all-gather.5.cloned.1.call-done = bf16[256,5120]{1,0:T(8,128)(2,1)} async-done(((bf16[64,5120]{1,0:T(8,128)(2,1)}), bf16[256,5120]{1,0:T(8,128)(2,1)}) %all-gather.5.cloned.1.call-update) | async-done | bytes 2621456 | tf_op jit(solution)/shard_map/all_gather | solution.py:91
  634.0 6.7 fusion.6
  640.7 25.9 %all-reduce.11.cloned.1.call-done = f32[256,640]{1,0:T(8,128)} async-done(((f32[256,640]{1,0:T(8,128)}), f32[256,640]{1,0:T(8,128)}) %all-reduce.11.cloned.1.call-update) | async-done | bytes 655376 | tf_op jit(solution)/shard_map/psum | solution.py:92
  667.8 6.3 psum.95
  675.3 9.1 %all_to_all.29 = bf16[4,64,640]{2,1,0:T(8,128)(2,1)S(1)} all-to-all(bf16[4,64,640]{2,1,0:T(8,128)(2,1)S(1)} %bitcast.92), channel_id=1, replica_groups=mesh['part'=1,'model'=2,'data'=4] {'data'}, dimensions={0} | all-to-all | bytes 655360 | tf_op jit(solution)/shard_map/all_to_all | solution.py:102
  (103 shorter events, 28.9 us)
Async XLA Ops:
  7.2 7.9 %copy-start.4 = (bf16[2,640,2,256]{3,2,1,0:T(2,128)(2,1)S(1)}, bf16[2,640,2,256]{3,2,1,0:T(2,128)(2,1)}, u32[]{:S(2)}) copy-start(bf16[2,640,2,256]{3,2,1,0:T(2,128)(2,1)} %param.21) | copy-start | bytes 3932164
  8.3 9.4 %copy-start.5 = (bf16[2,640,2,256]{3,2,1,0:T(2,128)(2,1)S(1)}, bf16[2,640,2,256]{3,2,1,0:T(2,128)(2,1)}, u32[]{:S(2)}) copy-start(bf16[2,640,2,256]{3,2,1,0:T(2,128)(2,1)} %param.22) | copy-start | bytes 3932164
  9.1 13.2 %all-to-all-start = ((bf16[64,4,640]{2,0,1:T(8,128)(2,1)}), bf16[64,4,640]{2,0,1:T(8,128)(2,1)S(1)}, u32[]{:S(2)}, u32[]{:S(2)}) async-start(bf16[64,4,640]{2,0,1:T(8,128)(2,1)} %copy.25), calls=%async_computation | async-start | bytes 655360 | tf_op jit(solution)/shard_map/all_to_all | solution.py:99
  13.7 46.4 %reduce-scatter.7.cloned.1.call-start = ((), (), s32[]{:S(2)}) async-start(), calls=%async_computation.8 | async-start | bytes 2621440 | tf_op jit(solution)/shard_map/reduce_scatter | solution.py:72
  16.8 3.7 copy-start.1
  30.3 3.7 copy-start.9
  34.0 88.0 %all-reduce.5.cloned.1.call-start = ((), (), s32[]{:S(2)}) async-start(), calls=%async_computation.9 | async-start | bytes 1310720 | tf_op jit(solution)/shard_map/psum | solution.py:82
  64.0 12.0 %copy-start.7 = (pred[64,64]{1,0:T(8,128)(4,1)S(1)}, pred[64,64]{1,0:T(8,128)(4,1)}, u32[]{:S(2)}) copy-start(pred[64,64]{1,0:T(8,128)(4,1)} %fusion.124) | copy-start | bytes 12292
  92.6 44.2 %copy-start.8 = (f32[640]{0:T(1024)S(1)}, f32[640]{0:T(1024)}, u32[]{:S(2)}) copy-start(f32[640]{0:T(1024)} %get-tuple-element.10) | copy-start | bytes 7684
  95.4 93.3 %reduce-scatter.11.cloned.1.call-start = ((), (), s32[]{:S(2)}) async-start(), calls=%async_computation.11 | async-start | bytes 6553600 | tf_op jit(solution)/shard_map/reduce_scatter | solution.py:89
  130.9 26.1 %copy-start.2 = (bf16[256,640]{1,0:T(8,128)(2,1)}, bf16[256,640]{1,0:T(8,128)(2,1)S(1)}, u32[]{:S(2)}) copy-start(bf16[256,640]{1,0:T(8,128)(2,1)S(1)} %get-tuple-element.18) | copy-start | bytes 983044
  144.4 92.1 %reduce-scatter.9.cloned.1.call-start = ((), (), s32[]{:S(2)}) async-start(), calls=%async_computation.10 | async-start | bytes 6553600 | tf_op jit(solution)/shard_map/reduce_scatter | solution.py:87
  164.5 97.5 %all-gather.3.cloned.1.call-start = ((), (), s32[]{:S(2)}) async-start(), calls=%async_computation.12 | async-start | bytes 3276800 | tf_op jit(solution)/shard_map/all_gather | solution.py:91
  239.5 29.4 %copy-start = (bf16[1,640,2,256]{3,2,1,0:T(2,128)(2,1)S(1)}, bf16[1,640,2,256]{3,2,1,0:T(2,128)(2,1)}, u32[]{:S(2)}) copy-start(bf16[1,640,2,256]{3,2,1,0:T(2,128)(2,1)} %get-tuple-element.24) | copy-start | bytes 1966084
  239.5 55.2 %all-reduce.7.cloned.1.call-start = ((), (), s32[]{:S(2)}) async-start(), calls=%async_computation.13 | async-start | bytes 1310720 | tf_op jit(solution)/shard_map/psum | solution.py:92
  268.8 69.9 %reduce-scatter.13.cloned.1.call-start = ((), (), s32[]{:S(2)}) async-start(), calls=%async_computation.14 | async-start | bytes 2621440 | tf_op jit(solution)/shard_map/reduce_scatter | solution.py:72
  268.9 4.4 copy-start.6
  269.8 32.3 %copy-start.3 = (bf16[256,640]{1,0:T(8,128)(2,1)S(1)}, bf16[256,640]{1,0:T(8,128)(2,1)}, u32[]{:S(2)}) copy-start(bf16[256,640]{1,0:T(8,128)(2,1)} %copy-done.2) | copy-start | bytes 983044
  309.5 4.2 copy-start.10
  313.7 180.6 %all-reduce.9.cloned.1.call-start = ((), (), s32[]{:S(2)}) async-start(), calls=%async_computation.15 | async-start | bytes 1310720 | tf_op jit(solution)/shard_map/psum | solution.py:82
  467.8 93.4 %reduce-scatter.17.cloned.1.call-start = ((), (), s32[]{:S(2)}) async-start(), calls=%async_computation.17 | async-start | bytes 6553600 | tf_op jit(solution)/shard_map/reduce_scatter | solution.py:89
  516.8 91.5 %reduce-scatter.15.cloned.1.call-start = ((), (), s32[]{:S(2)}) async-start(), calls=%async_computation.16 | async-start | bytes 6553600 | tf_op jit(solution)/shard_map/reduce_scatter | solution.py:87
  524.4 109.5 %all-gather.5.cloned.1.call-start = ((), (), s32[]{:S(2)}) async-start(), calls=%async_computation.18 | async-start | bytes 3276800 | tf_op jit(solution)/shard_map/all_gather | solution.py:91
  611.4 55.2 %all-reduce.11.cloned.1.call-start = ((), (), s32[]{:S(2)}) async-start(), calls=%async_computation.19 | async-start | bytes 1310720 | tf_op jit(solution)/shard_map/psum | solution.py:92
Sparse Core Ops, SparseCore 0:
  34.1 25.9 reduce-scatter.6
  95.5 26.3 all-reduce.4
  144.5 44.1 reduce-scatter.10
  191.6 44.8 reduce-scatter.8
  239.6 22.4 all-gather.2
  268.9 25.6 all-reduce.6
  313.8 24.8 reduce-scatter.12
  467.9 26.3 all-reduce.8
  517.0 44.1 reduce-scatter.16
  563.5 44.8 reduce-scatter.14
  611.5 22.4 all-gather.4
  640.8 25.6 all-reduce.10

commit v2 on v1

--- a/solution.py
+++ b/solution.py
@@ -1,6 +1,10 @@
+import functools
+
 import jax
 import jax.numpy as jnp
 from jax import lax
+from jax.experimental import pallas as pl
+from jax.experimental.pallas import tpu as pltpu
 from jax.sharding import PartitionSpec as P
 
 SOFT_CAP = 50.0
@@ -30,26 +34,115 @@
     return jnp.cos(angles)[:, None, :], jnp.sin(angles)[:, None, :]
 
 
-def attend(q_new, k_new, v_new, positions, k_cache, v_cache, is_local):
+LANES = 128
+STEP_ROWS = 4
+
+
+def attend_kernel(cache_len, n_rows, depth, pos_ref, q_ref, kn_ref, vn_ref, k_hbm, v_hbm, head_ref, ko_hbm, vo_hbm, kbuf, vbuf, rd_sem, wr_sem):
+    n_steps = n_rows // STEP_ROWS
+    n_cols = cache_len * 4
+
+    def reads(step):
+        slot = lax.rem(step, depth)
+        rows = pl.ds(step * STEP_ROWS, STEP_ROWS)
+        return (pltpu.make_async_copy(k_hbm.at[rows], kbuf.at[slot], rd_sem.at[0, slot]),
+                pltpu.make_async_copy(v_hbm.at[rows], vbuf.at[slot], rd_sem.at[1, slot]))
+
+    def writes(step):
+        slot = lax.rem(step, depth)
+        rows = pl.ds(step * STEP_ROWS, STEP_ROWS)
+        return (pltpu.make_async_copy(kbuf.at[slot], ko_hbm.at[rows], wr_sem.at[0, slot]),
+                pltpu.make_async_copy(vbuf.at[slot], vo_hbm.at[rows], wr_sem.at[1, slot]))
+
+    ahead = depth - 2
+    for step in range(ahead):
+        for copy in reads(step):
+            copy.start()
+
+    row_id = lax.broadcasted_iota(jnp.int32, (8, n_cols), 0)
+    col_id = lax.broadcasted_iota(jnp.int32, (8, n_cols), 1)
+    half_row, kv_row = row_id // 4, (row_id // 2) % 2
+    half_col, kv_col, slot_col = (col_id // 2) % 2, col_id % 2, col_id // 4
+    same_half, same_kv = half_row == half_col, kv_row == kv_col
+    sub_id = lax.broadcasted_iota(jnp.int32, (16, LANES), 0) // 4
+
+    @pl.loop(0, n_steps)
+    def _(step):
+        slot = lax.rem(step, depth)
+
+        @pl.when(step + ahead < n_steps)
+        def _():
+            @pl.when(step >= 2)
+            def _():
+                for copy in writes(step - 2):
+                    copy.wait()
+            for copy in reads(step + ahead):
+                copy.start()
+
+        for copy in reads(step):
+            copy.wait()
+        for i in range(STEP_ROWS):
+            row = step * STEP_ROWS + i
+            pos = pos_ref[row]
+            now = lax.rem(pos, cache_len)
+            window = pl.ds(pl.multiple_of(now // 4 * 16, 16), 16)
+            hit = sub_id == lax.rem(now, 4)
+            kbuf[slot, i, window, :] = jnp.where(hit, kn_ref[row], kbuf[slot, i, window, :])
+            vbuf[slot, i, window, :] = jnp.where(hit, vn_ref[row], vbuf[slot, i, window, :])
+        for i in range(STEP_ROWS):
+            row = step * STEP_ROWS + i
+            pos = pos_ref[row]
+            part = lax.dot_general(q_ref[row], kbuf[slot, i], (((1,), (1,)), ((), ())), preferred_element_type=jnp.float32)
+            part = jnp.where(same_half & same_kv, part, 0.0)
+            part = part + pltpu.roll(part, 4, 0)
+            other = jnp.where(half_col == 0, pltpu.roll(part, n_cols - 2, 1), pltpu.roll(part, 2, 1))
+            scores = SOFT_CAP * jnp.tanh((part + other) / SOFT_CAP)
+            scores = jnp.where(same_kv & (slot_col <= pos), scores, -1e30)
+            weights = jnp.exp(scores - jnp.max(scores, axis=1, keepdims=True))
+            total = jnp.sum(jnp.where(same_half, weights, 0.0), axis=1, keepdims=True)
+            prob = jnp.where(same_half, weights / total, 0.0).astype(jnp.bfloat16)
+            out = jnp.dot(prob, vbuf[slot, i], preferred_element_type=jnp.float32)
+            head_ref[row] = out.astype(jnp.bfloat16)
+        for copy in writes(step):
+            copy.start()
+
+    for step in range(max(n_steps - depth, 0), n_steps):
+        for copy in writes(step):
+            copy.wait()
+
+
+def attend(q_new, k_new, v_new, positions, k_cache, v_cache):
     n_rows, cache_len, kv_loc, head_dim = k_cache.shape
+    halves = head_dim // LANES
     group_size = q_new.shape[1] // kv_loc
-    slot_ids = jnp.arange(cache_len)
-    if is_local:
-        slot_now = positions % cache_len
-        valid_mask = ((positions[:, None] - slot_ids[None, :]) % cache_len) <= positions[:, None]
-    else:
-        slot_now = positions
-        valid_mask = slot_ids[None, :] <= positions[:, None]
-    slot_hit = (slot_ids[None, :] == slot_now[:, None])[:, :, None, None]
-    k_cache = jnp.where(slot_hit, k_new[:, None], k_cache)
-    v_cache = jnp.where(slot_hit, v_new[:, None], v_cache)
-    q_grp = q_new.reshape(n_rows, kv_loc, group_size, head_dim)
-    scores = jnp.einsum("bkgd,btkd->bkgt", q_grp, k_cache, preferred_element_type=jnp.float32)
-    scores = SOFT_CAP * jnp.tanh(scores / SOFT_CAP)
-    scores = jnp.where(valid_mask[:, None, None, :], scores, -1e30)
-    attn_prob = jax.nn.softmax(scores, axis=-1).astype(jnp.bfloat16)
-    head_out = jnp.einsum("bkgt,btkd->bkgd", attn_prob, v_cache, preferred_element_type=jnp.float32)
-    return head_out.astype(jnp.bfloat16).reshape(n_rows, kv_loc * group_size, head_dim), k_cache, v_cache
+    depth = 6
+
+    def flat(cache):
+        return cache.reshape(n_rows, cache_len, kv_loc, halves, LANES).transpose(0, 1, 3, 2, 4).reshape(n_rows, cache_len * halves * kv_loc, LANES)
+
+    def unflat(cache):
+        return cache.reshape(n_rows, cache_len, halves, kv_loc, LANES).transpose(0, 1, 3, 2, 4).reshape(n_rows, cache_len, kv_loc, head_dim)
+
+    def fresh(new):
+        return jnp.tile(new.reshape(n_rows, kv_loc, halves, LANES).transpose(0, 2, 1, 3).reshape(n_rows, halves * kv_loc, LANES), (1, 4, 1))
+
+    q_rows = q_new.reshape(n_rows, kv_loc, group_size, halves, LANES).transpose(0, 3, 1, 2, 4).reshape(n_rows, -1, LANES)
+    vmem, hbm = pl.BlockSpec(memory_space=pltpu.VMEM), pl.BlockSpec(memory_space=pl.ANY)
+    k_flat, v_flat = flat(k_cache), flat(v_cache)
+    block = (depth, STEP_ROWS) + k_flat.shape[1:]
+    n_bytes = 4 * k_flat.size * 2
+    heads, k_out, v_out = pl.pallas_call(
+        functools.partial(attend_kernel, cache_len, n_rows, depth),
+        out_shape=(jax.ShapeDtypeStruct(q_rows.shape, jnp.bfloat16), jax.ShapeDtypeStruct(k_flat.shape, jnp.bfloat16), jax.ShapeDtypeStruct(v_flat.shape, jnp.bfloat16)),
+        in_specs=[pl.BlockSpec(memory_space=pltpu.SMEM), vmem, vmem, vmem, hbm, hbm],
+        out_specs=(vmem, hbm, hbm),
+        scratch_shapes=[pltpu.VMEM(block, jnp.bfloat16), pltpu.VMEM(block, jnp.bfloat16), pltpu.SemaphoreType.DMA((2, depth)), pltpu.SemaphoreType.DMA((2, depth))],
+        compiler_params=pltpu.CompilerParams(vmem_limit_bytes=60 * 2**20),
+        cost_estimate=pl.CostEstimate(flops=n_rows * 8 * cache_len * 4 * LANES * 4, bytes_accessed=n_bytes, transcendentals=0),
+        name=f"attend_{cache_len}",
+    )(positions, q_rows, fresh(k_new), fresh(v_new), k_flat, v_flat)
+    head_out = heads.reshape(n_rows, halves, kv_loc * group_size, LANES).transpose(0, 2, 1, 3).reshape(n_rows, kv_loc * group_size, head_dim)
+    return head_out, unflat(k_out), unflat(v_out)
 
 
 def width_norm(hidden, gain, width):
@@ -57,7 +150,7 @@
     return hidden * lax.rsqrt(sum_sq / width + NORM_EPS) * (1.0 + gain.astype(jnp.float32))
 
 
-def layer_block(hidden, positions, k_cache, v_cache, weights, layer, is_local):
+def layer_block(hidden, positions, k_cache, v_cache, weights, layer):
     w_q, w_k, w_v, w_o, w_gate, w_up, w_down, norm_gains = weights
     share = hidden.shape[1]
     n_data = lax.axis_size("data")
@@ -77,7 +170,7 @@
     cos_t, sin_t = rope_tables(positions, head_dim)
     q_new = (rotary(q_proj, cos_t, sin_t) * head_dim ** -0.5).astype(jnp.bfloat16)
     k_new = rotary(k_proj, cos_t, sin_t).astype(jnp.bfloat16)
-    head_out, k_cache, v_cache = attend(q_new, k_new, v_proj.astype(jnp.bfloat16), positions, k_cache, v_cache, is_local)
+    head_out, k_cache, v_cache = attend(q_new, k_new, v_proj.astype(jnp.bfloat16), positions, k_cache, v_cache)
     heads_all = lax.all_gather(head_out.reshape(n_rows, -1), "data", axis=0, tiled=True)
     attn_sum = lax.psum(jnp.dot(heads_all, w_o[layer].reshape(-1, share), preferred_element_type=jnp.float32), "model")
     mid_hidden = (residual + width_norm(attn_sum, gains[1], width)).astype(jnp.bfloat16)
@@ -97,8 +190,8 @@
     def device_step(hidden, positions, k_local, v_local, k_global, v_global, w_q, w_k, w_v, w_o, w_gate, w_up, w_down, norm_gains):
         weights = (w_q, w_k, w_v, w_o, w_gate, w_up, w_down, norm_gains)
         hidden_cols = lax.all_to_all(hidden[:, 0, :], "data", 1, 0, tiled=True)
-        hidden_cols, k_local, v_local = layer_block(hidden_cols, positions, k_local, v_local, weights, 0, True)
-        hidden_cols, k_global, v_global = layer_block(hidden_cols, positions, k_global, v_global, weights, 1, False)
+        hidden_cols, k_local, v_local = layer_block(hidden_cols, positions, k_local, v_local, weights, 0)
+        hidden_cols, k_global, v_global = layer_block(hidden_cols, positions, k_global, v_global, weights, 1)
         final = lax.all_to_all(hidden_cols, "data", 0, 1, tiled=True)[:, None, :]
         return final, k_local, v_local, k_global, v_global
 

time: 702 us -> 648 us (0.923); the launches traced: 693 us -> 646 us
  other arithmetic: 113 us -> 18.7 us
  Pallas kernels: 0 us -> 78.4 us
  matrix products: 95.8 us -> 55.7 us
  waiting for transfers between devices: 348 us -> 361 us
  starting transfers between devices: 17.6 us -> 5.47 us
  local copies, waits for them, and re-layouts: 25.3 us -> 34 us
    select_n x2 -> x0, other arithmetic: 93.6 us -> none  [attend(): k_cache = jnp.where(slot_hit, k_new[:, None], k_cache)]
    pallas_call x0 -> x2, Pallas kernels: none -> 78.4 us  [attend(): pl.pallas_call(functools.partial(attend_kernel, cache_len, n_rows, depth)...]
    sub x2 -> x0, matrix products: 22.4 us -> none  [attend(): attn_prob = jax.nn.softmax(scores, axis=-1).astype(jnp.bfloat16)]
    dot_general x2 -> x0, matrix products: 18 us -> none  [attend(): jnp.einsum('bkgt,btkd->bkgd', attn_prob, v_cache, preferred_element_type=...]
    reduce_scatter x2, starting transfers between devices: 12.6 us -> 0.08 us  [layer_block(): lax.psum_scatter(gate_proj, 'data', scatter_dimension=0, tiled=True)]
    reduce_scatter x2, waiting for transfers between devices: 60.8 us -> 73.2 us  [layer_block(): up_proj = lax.psum_scatter(up_proj, 'data', scatter_dimension=0, tiled=True)]
where the time goes in v2:
time: 648 us; the launch traced here: 646 us
  waiting for transfers between devices  361 us (56%)
  blocking collectives  78.4 us (12%)
  Pallas kernels  78.4 us (12%)
  matrix products  55.7 us (9%)
  local copies, waits for them, and re-layouts  34 us (5%)
  other arithmetic  18.7 us (3%)
  between operations  14.6 us (2%)
    reduce_scatter x2, waiting for transfers between devices, layer_block(): lax.psum_scatter(gate_proj, 'data', scatter_dimension=0, tiled=True)  94.9 us
    pallas_call x2, Pallas kernels, attend(): pl.pallas_call(functools.partial(attend_kernel, cache_len, n_rows, depth)...  78.4 us
    reduce_scatter x2, waiting for transfers between devices, layer_block(): up_proj = lax.psum_scatter(up_proj, 'data', scatter_dimension=0, tiled=True)  73.2 us
    psum x2, waiting for transfers between devices, layer_block(): lax.psum(jnp.dot(heads_all, w_o[layer].reshape(-1, share), preferred_elem...  52.9 us
    psum x8, blocking collectives, width_norm(): lax.psum(jnp.sum(jnp.square(hidden), axis=-1, keepdims=True), 'data')  50.7 us
    reduce_scatter x2, waiting for transfers between devices, layer_block(): qkv = lax.psum_scatter(qkv, 'data', scatter_dimension=0, tiled=True)  47.8 us
    psum x2, waiting for transfers between devices, layer_block(): lax.psum(jnp.dot(acts_all, w_down[layer], preferred_element_type=jnp.floa...  47.1 us
    all_gather x2, waiting for transfers between devices, layer_block(): acts_all = lax.all_gather(gated_act, 'data', axis=0, tiled=True)  44.8 us
  transfers between devices with their start and end apart: 13, of which 12 were waited for; matrix products, arithmetic and copies ran while one was open for 5% of the time, Pallas kernels for 0%

profile of v2, /device:TPU:0, one launch (start us, length us, event | category | flops | bytes accessed | tf_op | source)
XLA Modules:
  0.0 646.3 jit_solution(11791781043250991175)
XLA Ops:
  9.1 4.6 all-to-all-start
  13.7 1.4 fusion.104
  15.1 1.7 fusion.100
  17.8 3.1 fusion.101
  22.7 1.3 copy.55
  24.4 7.6 %psum.84 = f32[256,1]{0,1:T(1,128)S(1)} all-reduce(f32[256,1]{0,1:T(1,128)S(1)} %broadcast_in_dim.18), channel_id=1, replica_groups=mesh['part'=1,'model'=2,'data'=4] {'data'}, use_global_device_ids=true, to_apply=%region_1.0 | all-reduce | flops 256 | bytes 2048 | tf_op jit(solution)/shard_map/psum | solution.py:149
  32.2 4.0 fusion.18
  36.5 3.0 fusion.98
  39.6 22.8 %reduce-scatter.7.cloned.1.call-done = f32[64,2048]{1,0:T(8,128)} async-done(((f32[256,2048]{1,0:T(8,128)}), f32[64,2048]{1,0:T(8,128)}) %reduce-scatter.7.cloned.1.call-update) | async-done | bytes 524304 | tf_op jit(solution)/shard_map/reduce_scatter | solution.py:165
  67.9 1.6 tile.44
  69.5 31.2 %attend_64.1 = (bf16[64,8,128]{2,1,0:T(8,128)(2,1)}, bf16[64,256,128]{2,1,0:T(8,128)(2,1)}, bf16[64,256,128]{2,1,0:T(8,128)(2,1)}) custom-call(s32[64]{0:T(128)} %pos_ref.3, bf16[64,8,128]{2,1,0:T(8,128)(2,1)} %bitcast.183, bf16[64,16,128]{2,1,0:T(8,128)(2,1)} %bitcast.177, bf16[64,16,128]{2,1,0:T(8,128)(2,1)} %bitcast.178, bf16[64,256,128]{2,1,0:T(8,128)(2,1)} %bitcast.165, ...), custom_call_target="tpu_custom_call" | custom-call | flops 67108864 | bytes 16777216 | tf_op jit(solution)/shard_map/attend_64/pallas_call | solution.py:134
  101.8 9.3 %all_gather.12 = bf16[256,1024]{1,0:T(8,128)(2,1)S(1)} all-gather(bf16[64,1024]{1,0:T(8,128)(2,1)S(1)} %reshape_reshape.6), channel_id=1, replica_groups=mesh['part'=1,'model'=2,'data'=4] {'data'}, dimensions={0}, use_global_device_ids=true | all-gather | bytes 655360 | tf_op jit(solution)/shard_map/all_gather | solution.py:174
  111.1 2.8 fusion.105
  113.9 26.5 %all-reduce.5.cloned.1.call-done = f32[256,640]{1,0:T(8,128)} async-done(((f32[256,640]{1,0:T(8,128)}), f32[256,640]{1,0:T(8,128)}) %all-reduce.5.cloned.1.call-update) | async-done | bytes 655376 | tf_op jit(solution)/shard_map/psum | solution.py:175
  141.6 6.3 psum.86
  147.9 1.4 fusion.48
  149.3 6.0 psum.87
  155.3 7.5 %fusion.8 = f32[256,5120]{1,0:T(8,128)} fusion(bf16[2,640,5120]{2,1,0:T(8,128)(2,1)} %param.25, bf16[256,640]{1,0:T(8,128)(2,1)S(1)} %get-tuple-element.30, f32[640]{0:T(1024)S(1)} %get-tuple-element.22, f32[256]{0:T(256)S(1)} %bitcast.206), kind=kOutput, calls=%fused_computation.8 | convolution fusion | flops 1678376960 | bytes 12127744 | tf_op jit(solution)/shard_map/dot_general | solution.py:181
  162.9 7.5 %fusion.10 = f32[256,5120]{1,0:T(8,128)} fusion(bf16[2,640,5120]{2,1,0:T(8,128)(2,1)} %param.24, bf16[256,640]{1,0:T(8,128)(2,1)S(1)} %get-tuple-element.30, f32[640]{0:T(1024)S(1)} %get-tuple-element.22, f32[256]{0:T(256)S(1)} %bitcast.207), kind=kOutput, calls=%fused_computation.10 | convolution fusion | flops 1678376960 | bytes 12127744 | tf_op jit(solution)/shard_map/dot_general | solution.py:179
  170.6 36.5 %reduce-scatter.11.cloned.1.call-done = f32[64,5120]{1,0:T(8,128)} async-done(((f32[256,5120]{1,0:T(8,128)}), f32[64,5120]{1,0:T(8,128)}) %reduce-scatter.11.cloned.1.call-update) | async-done | bytes 1310736 | tf_op jit(solution)/shard_map/reduce_scatter | solution.py:182
  207.1 47.8 %reduce-scatter.9.cloned.1.call-done = f32[64,5120]{1,0:T(8,128)} async-done(((f32[256,5120]{1,0:T(8,128)}), f32[64,5120]{1,0:T(8,128)}) %reduce-scatter.9.cloned.1.call-update) | async-done | bytes 1310736 | tf_op jit(solution)/shard_map/reduce_scatter | solution.py:180
  254.9 3.0 fusion.38
  258.0 22.5 %all-gather.3.cloned.1.call-done = bf16[256,5120]{1,0:T(8,128)(2,1)} async-done(((bf16[64,5120]{1,0:T(8,128)(2,1)}), bf16[256,5120]{1,0:T(8,128)(2,1)}) %all-gather.3.cloned.1.call-update) | async-done | bytes 2621456 | tf_op jit(solution)/shard_map/all_gather | solution.py:184
  280.5 6.7 %fusion.6 = f32[256,640]{1,0:T(8,128)} fusion(bf16[256,5120]{1,0:T(8,128)(2,1)} %all-gather.3.cloned.1.call-done, bf16[2,5120,640]{2,1,0:T(8,128)(2,1)} %param.26), kind=kOutput, calls=%fused_computation.6 | convolution fusion | flops 1677721600 | bytes 9830400 | tf_op jit(solution)/shard_map/dot_general | solution.py:185
  288.3 2.1 copy.60
  291.8 21.3 %all-reduce.7.cloned.1.call-done = f32[256,640]{1,0:T(8,128)} async-done(((f32[256,640]{1,0:T(8,128)}), f32[256,640]{1,0:T(8,128)}) %all-reduce.7.cloned.1.call-update) | async-done | bytes 655376 | tf_op jit(solution)/shard_map/psum | solution.py:185
  314.3 6.3 psum.89
  320.6 1.4 fusion.52
  322.0 6.0 psum.90
  328.0 4.1 fusion.24
  332.1 25.0 %reduce-scatter.13.cloned.1.call-done = f32[64,2048]{1,0:T(8,128)} async-done(((f32[256,2048]{1,0:T(8,128)}), f32[64,2048]{1,0:T(8,128)}) %reduce-scatter.13.cloned.1.call-update) | async-done | bytes 524304 | tf_op jit(solution)/shard_map/reduce_scatter | solution.py:165
  362.8 47.2 %attend_512.1 = (bf16[64,8,128]{2,1,0:T(8,128)(2,1)}, bf16[64,2048,128]{2,1,0:T(8,128)(2,1)}, bf16[64,2048,128]{2,1,0:T(8,128)(2,1)}) custom-call(s32[64]{0:T(128)} %pos_ref.3, bf16[64,8,128]{2,1,0:T(8,128)(2,1)} %bitcast.184, bf16[64,16,128]{2,1,0:T(8,128)(2,1)} %bitcast.175, bf16[64,16,128]{2,1,0:T(8,128)(2,1)} %bitcast.176, ...), custom_call_target="tpu_custom_call" | custom-call | flops 536870912 | bytes 134217728 | tf_op jit(solution)/shard_map/attend_512/pallas_call | solution.py:134
  411.1 9.3 %all_gather.14 = bf16[256,1024]{1,0:T(8,128)(2,1)S(1)} all-gather(bf16[64,1024]{1,0:T(8,128)(2,1)S(1)} %reshape_reshape.7), channel_id=1, replica_groups=mesh['part'=1,'model'=2,'data'=4] {'data'}, dimensions={0}, use_global_device_ids=true | all-gather | bytes 655360 | tf_op jit(solution)/shard_map/all_gather | solution.py:174
  420.4 1.4 fusion.106
  421.9 26.5 %all-reduce.9.cloned.1.call-done = f32[256,640]{1,0:T(8,128)} async-done(((f32[256,640]{1,0:T(8,128)}), f32[256,640]{1,0:T(8,128)}) %all-reduce.9.cloned.1.call-update) | async-done | bytes 655376 | tf_op jit(solution)/shard_map/psum | solution.py:175
  449.6 6.3 psum.92
  455.9 1.4 fusion.56
  457.3 6.0 psum.93
  463.3 7.5 %fusion.2 = f32[256,5120]{1,0:T(8,128)} fusion(bf16[2,640,5120]{2,1,0:T(8,128)(2,1)} %param.25, bf16[256,640]{1,0:T(8,128)(2,1)S(1)} %get-tuple-element.26, f32[640]{0:T(1024)S(1)} %get-tuple-element.18, f32[256]{0:T(256)S(1)} %bitcast.208), kind=kOutput, calls=%fused_computation.2 | convolution fusion | flops 1678376960 | bytes 12127744 | tf_op jit(solution)/shard_map/dot_general | solution.py:181
  470.8 7.5 %fusion.4 = f32[256,5120]{1,0:T(8,128)} fusion(bf16[2,640,5120]{2,1,0:T(8,128)(2,1)} %param.24, bf16[256,640]{1,0:T(8,128)(2,1)S(1)} %get-tuple-element.26, f32[640]{0:T(1024)S(1)} %get-tuple-element.18, f32[256]{0:T(256)S(1)} %bitcast.209), kind=kOutput, calls=%fused_computation.4 | convolution fusion | flops 1678376960 | bytes 12127744 | tf_op jit(solution)/shard_map/dot_general | solution.py:179
  478.4 36.7 %reduce-scatter.17.cloned.1.call-done = f32[64,5120]{1,0:T(8,128)} async-done(((f32[256,5120]{1,0:T(8,128)}), f32[64,5120]{1,0:T(8,128)}) %reduce-scatter.17.cloned.1.call-update) | async-done | bytes 1310736 | tf_op jit(solution)/shard_map/reduce_scatter | solution.py:182
  515.1 47.2 %reduce-scatter.15.cloned.1.call-done = f32[64,5120]{1,0:T(8,128)} async-done(((f32[256,5120]{1,0:T(8,128)}), f32[64,5120]{1,0:T(8,128)}) %reduce-scatter.15.cloned.1.call-update) | async-done | bytes 1310736 | tf_op jit(solution)/shard_map/reduce_scatter | solution.py:180
  562.2 3.0 fusion.47
  565.5 22.3 %all-gather.5.cloned.1.call-done = bf16[256,5120]{1,0:T(8,128)(2,1)} async-done(((bf16[64,5120]{1,0:T(8,128)(2,1)}), bf16[256,5120]{1,0:T(8,128)(2,1)}) %all-gather.5.cloned.1.call-update) | async-done | bytes 2621456 | tf_op jit(solution)/shard_map/all_gather | solution.py:184
  587.8 6.7 %fusion = f32[256,640]{1,0:T(8,128)} fusion(bf16[256,5120]{1,0:T(8,128)(2,1)} %all-gather.5.cloned.1.call-done, bf16[2,5120,640]{2,1,0:T(8,128)(2,1)} %param.26), kind=kOutput, calls=%fused_computation | convolution fusion | flops 1677721600 | bytes 9830400 | tf_op jit(solution)/shard_map/dot_general | solution.py:185
  594.6 25.9 %all-reduce.11.cloned.1.call-done = f32[256,640]{1,0:T(8,128)} async-done(((f32[256,640]{1,0:T(8,128)}), f32[256,640]{1,0:T(8,128)}) %all-reduce.11.cloned.1.call-update) | async-done | bytes 655376 | tf_op jit(solution)/shard_map/psum | solution.py:185
  621.6 6.3 psum.95
  629.2 9.1 %all_to_all.29 = bf16[4,64,640]{2,1,0:T(8,128)(2,1)S(1)} all-to-all(bf16[4,64,640]{2,1,0:T(8,128)(2,1)S(1)} %bitcast.174), channel_id=1, replica_groups=mesh['part'=1,'model'=2,'data'=4] {'data'}, dimensions={0} | all-to-all | bytes 655360 | tf_op jit(solution)/shard_map/all_to_all | solution.py:195
  (104 shorter events, 29.3 us)
Async XLA Ops:
  7.2 7.9 %copy-start.4 = (bf16[2,640,2,256]{3,2,1,0:T(2,128)(2,1)S(1)}, bf16[2,640,2,256]{3,2,1,0:T(2,128)(2,1)}, u32[]{:S(2)}) copy-start(bf16[2,640,2,256]{3,2,1,0:T(2,128)(2,1)} %param.21) | copy-start | bytes 3932164
  9.1 15.1 %all-to-all-start = ((bf16[64,4,640]{2,0,1:T(8,128)(2,1)}), bf16[64,4,640]{2,0,1:T(8,128)(2,1)S(1)}, u32[]{:S(2)}, u32[]{:S(2)}) async-start(bf16[64,4,640]{2,0,1:T(8,128)(2,1)} %copy.29), calls=%async_computation | async-start | bytes 655360 | tf_op jit(solution)/shard_map/all_to_all | solution.py:192
  13.7 48.7 %reduce-scatter.7.cloned.1.call-start = ((), (), s32[]{:S(2)}) async-start(), calls=%async_computation.8 | async-start | bytes 2621440 | tf_op jit(solution)/shard_map/reduce_scatter | solution.py:165
  16.8 5.0 copy-start.1
  32.2 4.1 copy-start.6
  36.2 104.2 %all-reduce.5.cloned.1.call-start = ((), (), s32[]{:S(2)}) async-start(), calls=%async_computation.9 | async-start | bytes 1310720 | tf_op jit(solution)/shard_map/psum | solution.py:175
  113.9 93.3 %reduce-scatter.11.cloned.1.call-start = ((), (), s32[]{:S(2)}) async-start(), calls=%async_computation.11 | async-start | bytes 6553600 | tf_op jit(solution)/shard_map/reduce_scatter | solution.py:182
  149.3 13.6 %copy-start.2 = (bf16[256,640]{1,0:T(8,128)(2,1)}, bf16[256,640]{1,0:T(8,128)(2,1)S(1)}, u32[]{:S(2)}) copy-start(bf16[256,640]{1,0:T(8,128)(2,1)S(1)} %get-tuple-element.30) | copy-start | bytes 983044
  162.8 92.1 %reduce-scatter.9.cloned.1.call-start = ((), (), s32[]{:S(2)}) async-start(), calls=%async_computation.10 | async-start | bytes 6553600 | tf_op jit(solution)/shard_map/reduce_scatter | solution.py:180
  170.4 110.1 %all-gather.3.cloned.1.call-start = ((), (), s32[]{:S(2)}) async-start(), calls=%async_computation.12 | async-start | bytes 3276800 | tf_op jit(solution)/shard_map/all_gather | solution.py:184
  257.9 29.3 %copy-start = (bf16[1,640,2,256]{3,2,1,0:T(2,128)(2,1)S(1)}, bf16[1,640,2,256]{3,2,1,0:T(2,128)(2,1)}, u32[]{:S(2)}) copy-start(bf16[1,640,2,256]{3,2,1,0:T(2,128)(2,1)} %get-tuple-element.36) | copy-start | bytes 1966084
  257.9 55.1 %all-reduce.7.cloned.1.call-start = ((), (), s32[]{:S(2)}) async-start(), calls=%async_computation.13 | async-start | bytes 1310720 | tf_op jit(solution)/shard_map/psum | solution.py:185
  287.2 69.9 %reduce-scatter.13.cloned.1.call-start = ((), (), s32[]{:S(2)}) async-start(), calls=%async_computation.14 | async-start | bytes 2621440 | tf_op jit(solution)/shard_map/reduce_scatter | solution.py:165
  287.3 4.4 copy-start.5
  288.3 32.3 %copy-start.3 = (bf16[256,640]{1,0:T(8,128)(2,1)S(1)}, bf16[256,640]{1,0:T(8,128)(2,1)}, u32[]{:S(2)}) copy-start(bf16[256,640]{1,0:T(8,128)(2,1)} %copy-done.2) | copy-start | bytes 983044
  332.1 116.3 %all-reduce.9.cloned.1.call-start = ((), (), s32[]{:S(2)}) async-start(), calls=%async_computation.15 | async-start | bytes 1310720 | tf_op jit(solution)/shard_map/psum | solution.py:175
  421.9 93.2 %reduce-scatter.17.cloned.1.call-start = ((), (), s32[]{:S(2)}) async-start(), calls=%async_computation.17 | async-start | bytes 6553600 | tf_op jit(solution)/shard_map/reduce_scatter | solution.py:182
  470.8 91.5 %reduce-scatter.15.cloned.1.call-start = ((), (), s32[]{:S(2)}) async-start(), calls=%async_computation.16 | async-start | bytes 6553600 | tf_op jit(solution)/shard_map/reduce_scatter | solution.py:180
  478.3 109.5 %all-gather.5.cloned.1.call-start = ((), (), s32[]{:S(2)}) async-start(), calls=%async_computation.18 | async-start | bytes 3276800 | tf_op jit(solution)/shard_map/all_gather | solution.py:184
  565.3 55.2 %all-reduce.11.cloned.1.call-start = ((), (), s32[]{:S(2)}) async-start(), calls=%async_computation.19 | async-start | bytes 1310720 | tf_op jit(solution)/shard_map/psum | solution.py:185
Sparse Core Ops, SparseCore 0:
  36.3 25.9 reduce-scatter.6
  114.0 26.3 all-reduce.4
  162.9 44.1 reduce-scatter.10
  210.1 44.8 reduce-scatter.8
  258.1 22.4 all-gather.2
  287.4 25.6 all-reduce.6
  332.2 24.8 reduce-scatter.12
  422.0 26.3 all-reduce.8
  470.9 44.1 reduce-scatter.16
  517.4 44.7 reduce-scatter.14
  565.4 22.4 all-gather.4
  594.7 25.6 all-reduce.10

commit v3 on v2

--- a/solution.py
+++ b/solution.py
@@ -145,25 +145,303 @@
     return head_out, unflat(k_out), unflat(v_out)
 
 
-def width_norm(hidden, gain, width):
-    sum_sq = lax.psum(jnp.sum(jnp.square(hidden), axis=-1, keepdims=True), "data")
-    return hidden * lax.rsqrt(sum_sq / width + NORM_EPS) * (1.0 + gain.astype(jnp.float32))
-
-
-def layer_block(hidden, positions, k_cache, v_cache, weights, layer):
-    w_q, w_k, w_v, w_o, w_gate, w_up, w_down, norm_gains = weights
-    share = hidden.shape[1]
-    n_data = lax.axis_size("data")
-    width = share * n_data
-    gains = lax.dynamic_slice_in_dim(norm_gains[layer], lax.axis_index("data") * share, share, axis=1)
-    n_q, head_dim = w_q.shape[2:]
-    n_kv = w_k.shape[2]
-    residual = hidden.astype(jnp.float32)
-    normed = width_norm(residual, gains[0], width).astype(jnp.bfloat16)
-    w_in = jnp.concatenate([w_q[layer].reshape(share, -1), w_k[layer].reshape(share, -1), w_v[layer].reshape(share, -1)], axis=1)
-    qkv = jnp.dot(normed, w_in, preferred_element_type=jnp.float32)
-    qkv = lax.psum_scatter(qkv, "data", scatter_dimension=0, tiled=True)
+FF_CHUNK = 512
+QKV_CHUNK = 512
+MESH = pl.DeviceIdType.MESH
+
+
+def comm_kernel(cfg, *refs):
+    it = iter(refs)
+    post, layer, rows, share, width = cfg["post"], cfg["layer"], cfg["rows"], cfg["share"], cfg["width"]
+    qkv, first, n_ff = cfg["qkv"], cfg["first"], cfg["n_ff"]
+    x_ref = next(it)
+    g_ref = next(it)
+    if post:
+        res_ref, wo_hbm, wg_hbm, wu_hbm, wd_hbm = (next(it) for _ in range(5))
+    if qkv:
+        wi_hbm = next(it)
+        hid_ref, qkv_ref = next(it), next(it)
+    else:
+        out_ref = next(it)
+    tcol, st_src, st_rcv, hp, st_ss, st_rs, misc_ss, misc_rs, ld_sem = (next(it) for _ in range(9))
+    if post:
+        hall, apart, arecv, mpart, mrecv, wo, wg, wu, wd, sib_out, sib_in, mine, x_in, u_all = (next(it) for _ in range(14))
+        y_ss, y_rs, ff_ss, ff_rs = (next(it) for _ in range(4))
+    if qkv:
+        wi, q_out, q_in, q_mine, q_x, q_ss, q_rs = (next(it) for _ in range(7))
+
+    model, me = lax.axis_index("model"), lax.axis_index("data")
+    x_pos, core = me // 2, lax.rem(me, 2)
+    sib, part, diag = x_pos * 2 + 1 - core, (1 - x_pos) * 2 + core, (1 - x_pos) * 2 + 1 - core
+    DIAG, SIB, PART, OWN = (pl.ds(i * rows, rows) for i in range(4))
+    sends = []
+
+    def remote(src, dst, send_sem, recv_sem, data=None):
+        where = {"data": data} if data is not None else {"model": 1 - model}
+        return pltpu.make_async_remote_copy(src_ref=src, dst_ref=dst, send_sem=send_sem, recv_sem=recv_sem, device_id=where, device_id_type=MESH)
+
+    def send(*args):
+        copy = remote(*args)
+        copy.start()
+        sends.append(copy)
+        return copy
+
+    loads = []
+
+    def load(src, dst, sem):
+        copy = pltpu.make_async_copy(src, dst, sem)
+        copy.start()
+        return copy
+
+    if post:
+        wo_load = load(wo_hbm.at[layer], wo, ld_sem.at[0])
+        wg_load = load(wg_hbm.at[layer], wg, ld_sem.at[1])
+        wu_load = load(wu_hbm.at[layer], wu, ld_sem.at[2])
+        wd_load = load(wd_hbm.at[layer], wd, ld_sem.at[3])
+    if qkv:
+        wi_load = load(wi_hbm, wi, ld_sem.at[4])
+
+    barrier = pltpu.get_barrier_semaphore()
+    for dev in (sib, part, diag):
+        pl.semaphore_signal(barrier, inc=1, device_id={"data": dev}, device_id_type=MESH)
+    pl.semaphore_signal(barrier, inc=1, device_id={"model": 1 - model}, device_id_type=MESH)
+    pl.semaphore_wait(barrier, 4)
+
+    def square_sums(block, value):
+        total = None
+        for k in range(share // LANES):
+            piece = value[:, k * LANES:(k + 1) * LANES]
+            total = piece * piece if total is None else total + piece * piece
+        tcol[block, :] = total
+
+    def scales(idx):
+        own = jnp.sum(jnp.transpose(tcol[...]).reshape(LANES // 8, 8, 4 * rows), axis=0)
+        st_src[idx] = own
+        copies = [send(st_src.at[idx], st_rcv.at[idx, k], st_ss.at[idx, k], st_rs.at[idx, k], dev) for k, dev in enumerate((sib, part, diag))]
+        for copy in copies:
+            copy.wait_recv()
+
+        def swap(value):
+            return jnp.concatenate([value[:, LANES:], value[:, :LANES]], axis=1)
+
+        def flip(value):
+            return jnp.concatenate([pltpu.roll(value[:, :LANES], LANES // 2, 1), pltpu.roll(value[:, LANES:], LANES // 2, 1)], axis=1)
+
+        total = own + swap(st_rcv[idx, 0]) + flip(st_rcv[idx, 1]) + swap(flip(st_rcv[idx, 2]))
+        total = jnp.sum(total, axis=0, keepdims=True)
+        inverse = lax.rsqrt(total / width + NORM_EPS)
+        tcol[...] = jnp.transpose(jnp.broadcast_to(inverse, (LANES, 4 * rows)))
+
+    def scaled(block, value, gain):
+        return value * jnp.concatenate([tcol[block, :]] * (share // LANES), axis=1) * g_ref[gain:gain + 1, :]
+
+    blocks = (OWN, SIB, PART, DIAG)
+    if first:
+        for k, (dev, there) in enumerate(((sib, SIB), (part, PART), (diag, DIAG))):
+            cols = pl.ds(pl.multiple_of(dev * share, LANES), share)
+            send(x_ref.at[:, cols], hid_ref.at[there, :], misc_ss.at[k], misc_rs.at[k], dev)
+        hid_ref[OWN, :] = x_ref[:, pl.ds(pl.multiple_of(me * share, LANES), share)]
+        square_sums(OWN, hid_ref[OWN, :].astype(jnp.float32))
+        for copy, block in zip(list(sends), (SIB, PART, DIAG)):
+            copy.wait_recv()
+            square_sums(block, hid_ref[block, :].astype(jnp.float32))
+    if post:
+        to_part = send(x_ref, hall.at[PART, :], misc_ss.at[0], misc_rs.at[0], part)
+        to_sib = send(x_ref, hall.at[SIB, :], misc_ss.at[1], misc_rs.at[1], sib)
+        wo_load.wait()
+        y_copies = []
+        for k, block in enumerate(blocks):
+            if k == 1:
+                to_sib.wait_recv()
+            if k == 2:
+                to_part.wait_recv()
+                forward = send(hall.at[PART, :], hall.at[DIAG, :], misc_ss.at[2], misc_rs.at[2], sib)
+            if k == 3:
+                forward.wait_recv()
+            heads = x_ref[...] if k == 0 else hall[block, :]
+            apart[block, :] = jnp.dot(heads, wo[...], preferred_element_type=jnp.float32)
+            y_copies.append(send(apart.at[block, :], arecv.at[block, :], y_ss.at[k], y_rs.at[k]))
+        for copy, block in zip(y_copies, blocks):
+            copy.wait_recv()
+            total = apart[block, :] + arecv[block, :]
+            arecv[block, :] = total
+            square_sums(block, total)
+        scales(0)
+        for block in blocks:
+            mid = (res_ref[block, :].astype(jnp.float32) + scaled(block, arecv[block, :], 0)).astype(jnp.bfloat16).astype(jnp.float32)
+            arecv[block, :] = mid
+            mpart[block, :] = jnp.zeros((rows, share), jnp.float32)
+        for block in blocks:
+            square_sums(block, arecv[block, :])
+        scales(1)
+        for block in blocks:
+            hp[block, :] = scaled(block, arecv[block, :], 1).astype(jnp.bfloat16)
+        wg_load.wait()
+        wu_load.wait()
+
+        def to_sibling(c):
+            return remote(sib_out.at[c], sib_in.at[c], ff_ss.at[0, c], ff_rs.at[0, c], sib)
+
+        def to_partner(c):
+            return remote(mine.at[c, pl.ds(0, rows)], x_in.at[c], ff_ss.at[1, c], ff_rs.at[1, c], part)
+
+        def act_partner(c):
+            return remote(u_all.at[c, OWN], u_all.at[c, PART], ff_ss.at[2, c], ff_rs.at[2, c], part)
+
+        def act_sibling(c):
+            return remote(u_all.at[c, OWN], u_all.at[c, SIB], ff_ss.at[3, c], ff_rs.at[3, c], sib)
+
+        def act_forward(c):
+            return remote(u_all.at[c, PART], u_all.at[c, DIAG], ff_ss.at[4, c], ff_rs.at[4, c], sib)
+
+        def add_sibling(c):
+            to_sibling(c).wait_recv()
+            mine[c] = mine[c] + sib_in[c]
+            to_partner(c).start()
+
+        @pl.loop(0, n_ff)
+        def _(c):
+            cols = pl.ds(pl.multiple_of(c * FF_CHUNK, FF_CHUNK), FF_CHUNK)
+            for k, weight in enumerate((wg, wu)):
+                sums = jnp.dot(hp[...], weight[:, cols], preferred_element_type=jnp.float32)
+                sib_out[c, :, pl.ds(k * FF_CHUNK, FF_CHUNK)] = sums[:2 * rows]
+                mine[c, :, pl.ds(k * FF_CHUNK, FF_CHUNK)] = sums[2 * rows:]
+            to_sibling(c).start()
+
+            @pl.when(c >= 1)
+            def _():
+                add_sibling(c - 1)
+
+        add_sibling(n_ff - 1)
+
+        @pl.loop(0, n_ff)
+        def _(c):
+            to_partner(c).wait_recv()
+            both = mine[c, pl.ds(rows, rows), :] + x_in[c]
+            u_all[c, OWN, :] = (jax.nn.gelu(both[:, :FF_CHUNK], approximate=True) * both[:, FF_CHUNK:]).astype(jnp.bfloat16)
+            act_partner(c).start()
+            act_sibling(c).start()
+
+        wd_load.wait()
+
+        def down(c):
+            act_sibling(c).wait_recv()
+            act_forward(c).wait_recv()
+            deep = pl.ds(pl.multiple_of(c * FF_CHUNK, FF_CHUNK), FF_CHUNK)
+            mpart[...] += jnp.dot(u_all[c], wd[deep, :], preferred_element_type=jnp.float32)
+
+        @pl.loop(0, n_ff)
+        def _(c):
+            act_partner(c).wait_recv()
+            act_forward(c).start()
+
+            @pl.when(c >= 1)
+            def _():
+                down(c - 1)
+
+        down(n_ff - 1)
+        y_copies = [send(mpart.at[block, :], mrecv.at[block, :], y_ss.at[4 + k], y_rs.at[4 + k]) for k, block in enumerate(blocks)]
+        for copy, block in zip(y_copies, blocks):
+            copy.wait_recv()
+            total = mpart[block, :] + mrecv[block, :]
+            mrecv[block, :] = total
+            square_sums(block, total)
+        scales(2)
+        for block in blocks:
+            value = (arecv[block, :] + scaled(block, mrecv[block, :], 2)).astype(jnp.bfloat16)
+            if qkv:
+                hid_ref[block, :] = value
+            else:
+                hp[block, :] = value
+        if qkv:
+            for block in blocks:
+                square_sums(block, hid_ref[block, :].astype(jnp.float32))
+
+        @pl.loop(0, n_ff)
+        def _(c):
+            for copy in (to_sibling(c), to_partner(c), act_partner(c), act_sibling(c), act_forward(c)):
+                copy.wait_send()
+    if qkv:
+        scales(3)
+        for block in blocks:
+            hp[block, :] = scaled(block, hid_ref[block, :].astype(jnp.float32), 3).astype(jnp.bfloat16)
+        wi_load.wait()
+        n_q = wi.shape[1] // QKV_CHUNK
+
+        def q_partner(c):
+            return remote(q_mine.at[c, pl.ds(0, rows)], q_x.at[c], q_ss.at[1, c], q_rs.at[1, c], part)
+
+        for c in range(n_q):
+            sums = jnp.dot(hp[...], wi[:, c * QKV_CHUNK:(c + 1) * QKV_CHUNK], preferred_element_type=jnp.float32)
+            q_out[c] = sums[:2 * rows]
+            q_mine[c] = sums[2 * rows:]
+            copy = send(q_out.at[c], q_in.at[c], q_ss.at[0, c], q_rs.at[0, c], sib)
+            if c >= 1:
+                before.wait_recv()
+                q_mine[c - 1] = q_mine[c - 1] + q_in[c - 1]
+                q_partner(c - 1).start()
+            before = copy
+        before.wait_recv()
+        q_mine[n_q - 1] = q_mine[n_q - 1] + q_in[n_q - 1]
+        q_partner(n_q - 1).start()
+        for c in range(n_q):
+            q_partner(c).wait_recv()
+            qkv_ref[:, c * QKV_CHUNK:(c + 1) * QKV_CHUNK] = q_mine[c, pl.ds(rows, rows), :] + q_x[c]
+        for c in range(n_q):
+            q_partner(c).wait_send()
+    else:
+        here = pl.ds(pl.multiple_of(me * share, LANES), share)
+        out_copies = [send(hp.at[block, :], out_ref.at[:, here], misc_ss.at[3 + k], misc_rs.at[3 + k], dev)
+                      for k, (dev, block) in enumerate(((sib, SIB), (part, PART), (diag, DIAG)))]
+        out_ref[:, here] = hp[OWN, :]
+        for dev, copy in zip((sib, part, diag), out_copies):
+            copy.wait_recv()
+    for copy in sends:
+        copy.wait_send()
+
+
+def comm(x, gains, qkv_weight=None, post=None, layer=0, collective_id=0):
+    rows = x.shape[0]
+    share = gains.shape[1]
+    n_rows = rows * 4
+    f32, bf16, vmem, hbm = jnp.float32, jnp.bfloat16, pl.BlockSpec(memory_space=pltpu.VMEM), pl.BlockSpec(memory_space=pl.ANY)
+    dma = pltpu.SemaphoreType.DMA
+    args, specs = [x, gains], [vmem, vmem]
+    scratch = [pltpu.VMEM((n_rows, LANES), f32), pltpu.VMEM((4, 8, n_rows), f32), pltpu.VMEM((4, 3, 8, n_rows), f32), pltpu.VMEM((n_rows, share), bf16),
+               dma((4, 3)), dma((4, 3)), dma((6,)), dma((6,)), dma((5,))]
+    n_ff = 0
+    if post is not None:
+        residual, w_o, w_gate, w_up, w_down = post
+        args += list(post)
+        specs += [vmem, hbm, hbm, hbm, hbm]
+        ff = w_gate.shape[2]
+        n_ff = ff // FF_CHUNK
+        scratch += [pltpu.VMEM((n_rows, w_o.shape[1]), bf16)] + [pltpu.VMEM((n_rows, share), f32)] * 4
+        scratch += [pltpu.VMEM(w_o.shape[1:], bf16), pltpu.VMEM((share, ff), bf16), pltpu.VMEM((share, ff), bf16), pltpu.VMEM((ff, share), bf16)]
+        scratch += [pltpu.VMEM((n_ff, 2 * rows, 2 * FF_CHUNK), f32)] * 3 + [pltpu.VMEM((n_ff, rows, 2 * FF_CHUNK), f32), pltpu.VMEM((n_ff, n_rows, FF_CHUNK), bf16)]
+        scratch += [dma((8,)), dma((8,)), dma((5, n_ff)), dma((5, n_ff))]
+    if qkv_weight is not None:
+        args.append(qkv_weight)
+        specs.append(hbm)
+        n_q = qkv_weight.shape[1] // QKV_CHUNK
+        scratch += [pltpu.VMEM(qkv_weight.shape, bf16)] + [pltpu.VMEM((n_q, 2 * rows, QKV_CHUNK), f32)] * 3 + [pltpu.VMEM((n_q, rows, QKV_CHUNK), f32), dma((2, n_q)), dma((2, n_q))]
+        out_shape = (jax.ShapeDtypeStruct((n_rows, share), bf16), jax.ShapeDtypeStruct((rows, qkv_weight.shape[1]), f32))
+        out_specs = (vmem, vmem)
+    else:
+        out_shape = jax.ShapeDtypeStruct((rows, 4 * share), bf16)
+        out_specs = vmem
+    cfg = {"post": post is not None, "qkv": qkv_weight is not None, "first": post is None, "layer": layer, "rows": rows, "share": share, "width": 4 * share, "n_ff": n_ff}
+    return pl.pallas_call(
+        functools.partial(comm_kernel, cfg),
+        out_shape=out_shape, in_specs=specs, out_specs=out_specs, scratch_shapes=scratch,
+        compiler_params=pltpu.CompilerParams(collective_id=collective_id, has_side_effects=True, vmem_limit_bytes=(62 if post is not None else 20) * 2**20),
+        name=f"comm_{collective_id}",
+    )(*args)
+
+
+def attention(qkv, positions, k_cache, v_cache, n_q):
     n_rows = qkv.shape[0]
+    n_kv, head_dim = k_cache.shape[2:]
     q_proj = qkv[:, :n_q * head_dim].reshape(n_rows, n_q, head_dim)
     k_proj = qkv[:, n_q * head_dim:(n_q + n_kv) * head_dim].reshape(n_rows, n_kv, head_dim)
     v_proj = qkv[:, (n_q + n_kv) * head_dim:].reshape(n_rows, n_kv, head_dim)
@@ -171,28 +449,24 @@
     q_new = (rotary(q_proj, cos_t, sin_t) * head_dim ** -0.5).astype(jnp.bfloat16)
     k_new = rotary(k_proj, cos_t, sin_t).astype(jnp.bfloat16)
     head_out, k_cache, v_cache = attend(q_new, k_new, v_proj.astype(jnp.bfloat16), positions, k_cache, v_cache)
-    heads_all = lax.all_gather(head_out.reshape(n_rows, -1), "data", axis=0, tiled=True)
-    attn_sum = lax.psum(jnp.dot(heads_all, w_o[layer].reshape(-1, share), preferred_element_type=jnp.float32), "model")
-    mid_hidden = (residual + width_norm(attn_sum, gains[1], width)).astype(jnp.bfloat16)
-    mid_f = mid_hidden.astype(jnp.float32)
-    normed_ff = width_norm(mid_f, gains[2], width).astype(jnp.bfloat16)
-    gate_proj = jnp.dot(normed_ff, w_gate[layer], preferred_element_type=jnp.float32)
-    gate_proj = lax.psum_scatter(gate_proj, "data", scatter_dimension=0, tiled=True)
-    up_proj = jnp.dot(normed_ff, w_up[layer], preferred_element_type=jnp.float32)
-    up_proj = lax.psum_scatter(up_proj, "data", scatter_dimension=0, tiled=True)
-    gated_act = (jax.nn.gelu(gate_proj, approximate=True) * up_proj).astype(jnp.bfloat16)
-    acts_all = lax.all_gather(gated_act, "data", axis=0, tiled=True)
-    down_sum = lax.psum(jnp.dot(acts_all, w_down[layer], preferred_element_type=jnp.float32), "model")
-    return (mid_f + width_norm(down_sum, gains[3], width)).astype(jnp.bfloat16), k_cache, v_cache
+    return head_out.reshape(n_rows, -1), k_cache, v_cache
 
 
 def solution(mesh):
     def device_step(hidden, positions, k_local, v_local, k_global, v_global, w_q, w_k, w_v, w_o, w_gate, w_up, w_down, norm_gains):
-        weights = (w_q, w_k, w_v, w_o, w_gate, w_up, w_down, norm_gains)
-        hidden_cols = lax.all_to_all(hidden[:, 0, :], "data", 1, 0, tiled=True)
-        hidden_cols, k_local, v_local = layer_block(hidden_cols, positions, k_local, v_local, weights, 0)
-        hidden_cols, k_global, v_global = layer_block(hidden_cols, positions, k_global, v_global, weights, 1)
-        final = lax.all_to_all(hidden_cols, "data", 0, 1, tiled=True)[:, None, :]
+        share = w_q.shape[1]
+        n_q = w_q.shape[2]
+        gains = 1.0 + lax.dynamic_slice_in_dim(norm_gains, lax.axis_index("data") * share, share, axis=2).astype(jnp.float32)
+        in_weights = [jnp.concatenate([w[layer].reshape(share, -1) for w in (w_q, w_k, w_v)], axis=1) for layer in range(2)]
+        out_weights = w_o.reshape(2, -1, share)
+        first_gains = jnp.concatenate([gains[0, 1:], gains[0, :1]], axis=0)
+        mid_gains = jnp.concatenate([gains[0, 1:], gains[1, :1]], axis=0)
+        last_gains = jnp.concatenate([gains[1, 1:], gains[1, :1]], axis=0)
+        residual, qkv = comm(hidden[:, 0, :], first_gains, in_weights[0], collective_id=0)
+        heads, k_local, v_local = attention(qkv, positions, k_local, v_local, n_q)
+        residual, qkv = comm(heads, mid_gains, in_weights[1], (residual, out_weights, w_gate, w_up, w_down), layer=0, collective_id=1)
+        heads, k_global, v_global = attention(qkv, positions, k_global, v_global, n_q)
+        final = comm(heads, last_gains, None, (residual, out_weights, w_gate, w_up, w_down), layer=1, collective_id=2)[:, None, :]
         return final, k_local, v_local, k_global, v_global
 
     in_specs = (ROW_SPEC, POS_SPEC, CACHE_SPEC, CACHE_SPEC, CACHE_SPEC, CACHE_SPEC, PROJ_IN_SPEC, PROJ_IN_SPEC, PROJ_IN_SPEC, PROJ_OUT_SPEC, FF_IN_SPEC, FF_IN_SPEC, FF_OUT_SPEC, GAIN_SPEC)

time: 648 us -> 399 us (0.62)
  waiting for transfers between devices: 361 us -> 0 us
  Pallas kernels: 78.4 us -> 372 us
  blocking collectives: 78.4 us -> 0 us
  matrix products: 55.7 us -> 0 us
  local copies, waits for them, and re-layouts: 34 us -> 19 us
  between operations: 14.6 us -> 0.97 us
  other arithmetic: 18.7 us -> 5.85 us
    pallas_call x0 -> x3, Pallas kernels: none -> 294 us  [comm(): pl.pallas_call(functools.partial(comm_kernel, cfg), out_shape=out_shape,...]
    reduce_scatter x6 -> x0, waiting for transfers between devices: 216 us -> none  [the longest x2 94.9 us: layer_block(): lax.psum_scatter(gate_proj, 'data', scatter_dimension=0, tiled=True)]
    psum x4 -> x0, waiting for transfers between devices: 100 us -> none  [the longest x2 52.9 us: layer_block(): lax.psum(jnp.dot(heads_all, w_o[layer].reshape(-1, share), preferred_elem...]
    dot_general x10 -> x0, matrix products: 55.7 us -> none  [the longest x2 15 us: layer_block(): jnp.dot(normed_ff, w_gate[layer], preferred_element_type=jnp.float32)]
    psum x8 -> x0, blocking collectives: 50.7 us -> none  [width_norm(): lax.psum(jnp.sum(jnp.square(hidden), axis=-1, keepdims=True), 'data')]
    all_gather x2 -> x0, waiting for transfers between devices: 44.8 us -> none  [layer_block(): acts_all = lax.all_gather(gated_act, 'data', axis=0, tiled=True)]
    all_gather x2 -> x0, blocking collectives: 18.6 us -> none  [layer_block(): lax.all_gather(head_out.reshape(n_rows, -1), 'data', axis=0, tiled=True)]
    reduce_sum x8 -> x0, other arithmetic: 9.13 us -> none  [width_norm(): jnp.sum(jnp.square(hidden), axis=-1, keepdims=True)]
  transfers between devices with their start and end apart: 13 -> 0, of which waited for: 12 -> 0; matrix products, arithmetic and copies ran while one was open for 5% -> 0% of each run, Pallas kernels for 0% -> 0%
where the time goes in v3:
time: 399 us; the launch traced here: 398 us
  Pallas kernels  372 us (93%)
  local copies, waits for them, and re-layouts  19 us (5%)
  other arithmetic  5.85 us (1%)
    pallas_call x3, Pallas kernels, comm(): pl.pallas_call(functools.partial(comm_kernel, cfg), out_shape=out_shape,...  294 us
    pallas_call x2, Pallas kernels, attend(): pl.pallas_call(functools.partial(attend_kernel, cache_len, n_rows, depth)...  78.4 us

profile of v3, /device:TPU:0, one launch (start us, length us, event | category | flops | bytes accessed | tf_op | source)
XLA Modules:
  0.0 398.3 jit_solution(4218502867152352022)
XLA Ops:
  0.6 0.7 convert_element_type.44
  1.3 0.7 convert_add_fusion
  2.0 0.6 pad_maximum_fusion.5
  2.7 0.2 multiply_cosine_fusion
  2.9 2.3 fusion.7
  5.2 0.1 copy.59
  5.3 0.1 copy.56
  5.4 0.9 fusion.8
  6.3 0.1 copy.60
  6.4 0.1 copy.57
  6.6 0.6 copy-done.2
  7.1 0.9 fusion.6
  8.0 0.3 copy.58
  8.3 1.7 pad_maximum_fusion.1.refs_7_
  10.1 0.3 copy.55
  10.4 0.3 pad_maximum_fusion.refs_2_
  10.7 0.7 copy-done.1
  11.3 26.9 %comm_0.1 = (bf16[256,640]{1,0:T(8,128)(2,1)S(1)}, f32[64,2048]{1,0:T(8,128)S(1)}) custom-call(bf16[64,2560]{1,0:T(8,128)(2,1)S(1)} %bitcast.111, f32[4,640]{1,0:T(4,128)S(1)} %get-tuple-element.48.refs_1_, bf16[640,2048]{1,0:T(8,128)(2,1)S(1)} %pad_maximum_fusion.refs_2_), custom_call_target="tpu_custom_call" | custom-call | tf_op jit(solution)/shard_map/comm_0/pallas_call | solution.py:434
  38.2 0.0 copy-start
  38.3 0.7 copy-done
  39.0 0.1 copy.35
  39.1 0.1 reshape.182
  39.3 0.1 reshape.184
  39.5 0.1 copy.33
  39.5 0.1 multiply_subtract_fusion.1
  39.6 0.7 fusion
  40.3 0.8 tile.41
  41.1 0.8 tile.44
  41.9 31.2 %attend_64.1 = (bf16[64,8,128]{2,1,0:T(8,128)(2,1)}, bf16[64,256,128]{2,1,0:T(8,128)(2,1)}, bf16[64,256,128]{2,1,0:T(8,128)(2,1)}) custom-call(s32[64]{0:T(128)} %pos_ref.3, bf16[64,8,128]{2,1,0:T(8,128)(2,1)} %bitcast.136, bf16[64,16,128]{2,1,0:T(8,128)(2,1)} %bitcast.133, bf16[64,16,128]{2,1,0:T(8,128)(2,1)} %bitcast.134, bf16[64,256,128]{2,1,0:T(8,128)(2,1)} %bitcast.120, ...), custom_call_target="tpu_custom_call" | custom-call | flops 67108864 | bytes 16777216 | tf_op jit(solution)/shard_map/attend_64/pallas_call | solution.py:134
  73.1 1.0 copy.88
  74.1 0.7 reshape_reshape.6.refs_0_
  74.8 140.3 %comm_1.1 = (bf16[256,640]{1,0:T(8,128)(2,1)}, f32[64,2048]{1,0:T(8,128)}) custom-call(bf16[64,1024]{1,0:T(8,128)(2,1)} %reshape_reshape.6.refs_0_, f32[4,640]{1,0:T(4,128)} %get-tuple-element.47.refs_1_, bf16[256,640]{1,0:T(8,128)(2,1)} %copy-done, bf16[2,1024,640]{2,1,0:T(8,128)(2,1)} %bitcast.114, bf16[2,640,5120]{2,1,0:T(8,128)(2,1)} %refs_4_.3, ...), custom_call_target="tpu_custom_call" | custom-call | tf_op jit(solution)/shard_map/comm_1/pallas_call | solution.py:434
  215.2 0.9 slice.128
  216.2 0.1 copy.43
  216.2 0.9 slice.95
  217.1 1.0 slice.92
  218.1 0.1 reshape.191
  218.2 0.1 reshape.193
  218.4 0.1 multiply_subtract_fusion
  218.5 0.7 fusion.1
  219.2 0.1 copy.41
  219.3 0.8 tile.47
  220.1 0.8 tile.50
  220.8 47.2 %attend_512.1 = (bf16[64,8,128]{2,1,0:T(8,128)(2,1)}, bf16[64,2048,128]{2,1,0:T(8,128)(2,1)}, bf16[64,2048,128]{2,1,0:T(8,128)(2,1)}) custom-call(s32[64]{0:T(128)} %pos_ref.3, bf16[64,8,128]{2,1,0:T(8,128)(2,1)} %bitcast.135, bf16[64,16,128]{2,1,0:T(8,128)(2,1)} %bitcast.131, bf16[64,16,128]{2,1,0:T(8,128)(2,1)} %bitcast.132, ...), custom_call_target="tpu_custom_call" | custom-call | flops 536870912 | bytes 134217728 | tf_op jit(solution)/shard_map/attend_512/pallas_call | solution.py:134
  268.1 1.0 copy.87
  269.1 0.7 reshape_reshape.7.refs_0_
  269.8 126.8 %comm_2.1 = bf16[64,2560]{1,0:T(8,128)(2,1)} custom-call(bf16[64,1024]{1,0:T(8,128)(2,1)} %reshape_reshape.7.refs_0_, f32[4,640]{1,0:T(4,128)} %get-tuple-element.49.refs_1_, bf16[256,640]{1,0:T(8,128)(2,1)} %get-tuple-element.20.refs_2_, bf16[2,1024,640]{2,1,0:T(8,128)(2,1)} %bitcast.115, bf16[2,640,5120]{2,1,0:T(8,128)(2,1)} %refs_4_.3, ...), custom_call_target="tpu_custom_call" | custom-call | tf_op jit(solution)/shard_map/comm_2/pallas_call | solution.py:434
  396.6 1.7 copy.90
  (20 shorter events, 0.3 us)
Async XLA Ops:
  2.9 2.5 copy-start.3
  5.4 1.7 copy-start.2
  10.4 1.0 copy-start.1
  38.2 0.7 copy-start

commit v4 on v3

--- a/solution.py
+++ b/solution.py
@@ -21,101 +21,113 @@
 GAIN_SPEC = P(None, None, None)
 
 
-def rotary(hidden, cos_t, sin_t):
-    half_dim = hidden.shape[-1] // 2
-    first_half = hidden[..., :half_dim]
-    second_half = hidden[..., half_dim:]
-    return jnp.concatenate([first_half * cos_t - second_half * sin_t, second_half * cos_t + first_half * sin_t], axis=-1)
-
-
 def rope_tables(positions, head_dim):
     inv_freq = ROPE_BASE ** (-jnp.arange(0, head_dim, 2).astype(jnp.float32) / head_dim)
     angles = positions.astype(jnp.float32)[:, None] * inv_freq[None, :]
-    return jnp.cos(angles)[:, None, :], jnp.sin(angles)[:, None, :]
+    return jnp.cos(angles), jnp.sin(angles)
 
 
 LANES = 128
-STEP_ROWS = 4
-
-
-def attend_kernel(cache_len, n_rows, depth, pos_ref, q_ref, kn_ref, vn_ref, k_hbm, v_hbm, head_ref, ko_hbm, vo_hbm, kbuf, vbuf, rd_sem, wr_sem):
-    n_steps = n_rows // STEP_ROWS
+
+
+def attend_kernel(cache_len, n_rows, group, depth, pos_ref, qkv_ref, cos_ref, sin_ref, k_hbm, v_hbm, head_ref, ko_hbm, vo_hbm, kbuf, vbuf, q8, kn, vn, outs, sbuf, pbuf, rd_sem, wr_sem):
+    n_steps = n_rows // group
     n_cols = cache_len * 4
 
     def reads(step):
         slot = lax.rem(step, depth)
-        rows = pl.ds(step * STEP_ROWS, STEP_ROWS)
+        rows = pl.ds(step * group, group)
         return (pltpu.make_async_copy(k_hbm.at[rows], kbuf.at[slot], rd_sem.at[0, slot]),
                 pltpu.make_async_copy(v_hbm.at[rows], vbuf.at[slot], rd_sem.at[1, slot]))
 
     def writes(step):
         slot = lax.rem(step, depth)
-        rows = pl.ds(step * STEP_ROWS, STEP_ROWS)
+        rows = pl.ds(step * group, group)
         return (pltpu.make_async_copy(kbuf.at[slot], ko_hbm.at[rows], wr_sem.at[0, slot]),
                 pltpu.make_async_copy(vbuf.at[slot], vo_hbm.at[rows], wr_sem.at[1, slot]))
 
-    ahead = depth - 2
+    ahead = max(depth - 2, 1) if depth < n_steps else n_steps
     for step in range(ahead):
         for copy in reads(step):
             copy.start()
 
+    cos_t, sin_t = cos_ref[...], sin_ref[...]
+    scale = (2 * LANES) ** -0.5
+    for h in range(4):
+        first, second = qkv_ref[:, h * 256:h * 256 + LANES], qkv_ref[:, h * 256 + LANES:h * 256 + 256]
+        q8[:, h, :] = (first * cos_t - second * sin_t) * scale
+        q8[:, 4 + h, :] = (second * cos_t + first * sin_t) * scale
+    for h in range(2):
+        base = 1024 + h * 256
+        first, second = qkv_ref[:, base:base + LANES], qkv_ref[:, base + LANES:base + 256]
+        halves = (first * cos_t - second * sin_t, second * cos_t + first * sin_t)
+        for half in range(2):
+            value = qkv_ref[:, base + 512 + half * LANES:base + 512 + (half + 1) * LANES]
+            for i in range(4):
+                kn[:, i * 4 + half * 2 + h, :] = halves[half]
+                vn[:, i * 4 + half * 2 + h, :] = value
+
     row_id = lax.broadcasted_iota(jnp.int32, (8, n_cols), 0)
     col_id = lax.broadcasted_iota(jnp.int32, (8, n_cols), 1)
-    half_row, kv_row = row_id // 4, (row_id // 2) % 2
-    half_col, kv_col, slot_col = (col_id // 2) % 2, col_id % 2, col_id // 4
-    same_half, same_kv = half_row == half_col, kv_row == kv_col
+    half_col = (col_id // 2) % 2
+    same_half = row_id // 4 == half_col
+    same_kv = (row_id // 2) % 2 == col_id % 2
+    slot_col = col_id // 4
     sub_id = lax.broadcasted_iota(jnp.int32, (16, LANES), 0) // 4
 
     @pl.loop(0, n_steps)
     def _(step):
         slot = lax.rem(step, depth)
-
-        @pl.when(step + ahead < n_steps)
-        def _():
-            @pl.when(step >= 2)
+        if ahead < n_steps:
+            @pl.when(step + ahead < n_steps)
             def _():
-                for copy in writes(step - 2):
-                    copy.wait()
-            for copy in reads(step + ahead):
-                copy.start()
+                @pl.when(step >= depth - ahead)
+                def _():
+                    for copy in writes(step - (depth - ahead)):
+                        copy.wait()
+                for copy in reads(step + ahead):
+                    copy.start()
 
         for copy in reads(step):
             copy.wait()
-        for i in range(STEP_ROWS):
-            row = step * STEP_ROWS + i
-            pos = pos_ref[row]
-            now = lax.rem(pos, cache_len)
+        for i in range(group):
+            row = step * group + i
+            now = lax.rem(pos_ref[row], cache_len)
             window = pl.ds(pl.multiple_of(now // 4 * 16, 16), 16)
             hit = sub_id == lax.rem(now, 4)
-            kbuf[slot, i, window, :] = jnp.where(hit, kn_ref[row], kbuf[slot, i, window, :])
-            vbuf[slot, i, window, :] = jnp.where(hit, vn_ref[row], vbuf[slot, i, window, :])
-        for i in range(STEP_ROWS):
-            row = step * STEP_ROWS + i
-            pos = pos_ref[row]
-            part = lax.dot_general(q_ref[row], kbuf[slot, i], (((1,), (1,)), ((), ())), preferred_element_type=jnp.float32)
-            part = jnp.where(same_half & same_kv, part, 0.0)
+            kbuf[slot, i, window, :] = jnp.where(hit, kn[row].astype(jnp.bfloat16), kbuf[slot, i, window, :])
+            vbuf[slot, i, window, :] = jnp.where(hit, vn[row].astype(jnp.bfloat16), vbuf[slot, i, window, :])
+        for i in range(group):
+            part = lax.dot_general(q8[step * group + i].astype(jnp.bfloat16), kbuf[slot, i], (((1,), (1,)), ((), ())), preferred_element_type=jnp.float32)
+            sbuf[i] = jnp.where(same_half & same_kv, part, 0.0)
+        for i in range(group):
+            part = sbuf[i]
             part = part + pltpu.roll(part, 4, 0)
             other = jnp.where(half_col == 0, pltpu.roll(part, n_cols - 2, 1), pltpu.roll(part, 2, 1))
             scores = SOFT_CAP * jnp.tanh((part + other) / SOFT_CAP)
-            scores = jnp.where(same_kv & (slot_col <= pos), scores, -1e30)
+            scores = jnp.where(same_kv & (slot_col <= pos_ref[step * group + i]), scores, -1e30)
             weights = jnp.exp(scores - jnp.max(scores, axis=1, keepdims=True))
             total = jnp.sum(jnp.where(same_half, weights, 0.0), axis=1, keepdims=True)
-            prob = jnp.where(same_half, weights / total, 0.0).astype(jnp.bfloat16)
-            out = jnp.dot(prob, vbuf[slot, i], preferred_element_type=jnp.float32)
-            head_ref[row] = out.astype(jnp.bfloat16)
+            pbuf[i] = jnp.where(same_half, weights / total, 0.0).astype(jnp.bfloat16)
+        for i in range(group):
+            outs[step * group + i] = jnp.dot(pbuf[i], vbuf[slot, i], preferred_element_type=jnp.float32)
         for copy in writes(step):
             copy.start()
 
-    for step in range(max(n_steps - depth, 0), n_steps):
+    for h in range(4):
+        for half in range(2):
+            head_ref[:, h * 256 + half * LANES:h * 256 + (half + 1) * LANES] = outs[:, half * 4 + h, :].astype(jnp.bfloat16)
+    for step in range(max(n_steps - depth, 0) if ahead < n_steps else 0, n_steps):
         for copy in writes(step):
             copy.wait()
 
 
-def attend(q_new, k_new, v_new, positions, k_cache, v_cache):
+def attend(qkv, tables, positions, k_cache, v_cache):
     n_rows, cache_len, kv_loc, head_dim = k_cache.shape
     halves = head_dim // LANES
-    group_size = q_new.shape[1] // kv_loc
-    depth = 6
+    group = 16 if cache_len <= 64 else 4
+    depth = 4 if cache_len <= 64 else 6
+    f32, bf16 = jnp.float32, jnp.bfloat16
 
     def flat(cache):
         return cache.reshape(n_rows, cache_len, kv_loc, halves, LANES).transpose(0, 1, 3, 2, 4).reshape(n_rows, cache_len * halves * kv_loc, LANES)
@@ -123,26 +135,24 @@
     def unflat(cache):
         return cache.reshape(n_rows, cache_len, halves, kv_loc, LANES).transpose(0, 1, 3, 2, 4).reshape(n_rows, cache_len, kv_loc, head_dim)
 
-    def fresh(new):
-        return jnp.tile(new.reshape(n_rows, kv_loc, halves, LANES).transpose(0, 2, 1, 3).reshape(n_rows, halves * kv_loc, LANES), (1, 4, 1))
-
-    q_rows = q_new.reshape(n_rows, kv_loc, group_size, halves, LANES).transpose(0, 3, 1, 2, 4).reshape(n_rows, -1, LANES)
     vmem, hbm = pl.BlockSpec(memory_space=pltpu.VMEM), pl.BlockSpec(memory_space=pl.ANY)
     k_flat, v_flat = flat(k_cache), flat(v_cache)
-    block = (depth, STEP_ROWS) + k_flat.shape[1:]
-    n_bytes = 4 * k_flat.size * 2
+    n_cols = k_flat.shape[1]
+    block = (depth, group, n_cols, LANES)
+    dma = pltpu.SemaphoreType.DMA
     heads, k_out, v_out = pl.pallas_call(
-        functools.partial(attend_kernel, cache_len, n_rows, depth),
-        out_shape=(jax.ShapeDtypeStruct(q_rows.shape, jnp.bfloat16), jax.ShapeDtypeStruct(k_flat.shape, jnp.bfloat16), jax.ShapeDtypeStruct(v_flat.shape, jnp.bfloat16)),
+        functools.partial(attend_kernel, cache_len, n_rows, group, depth),
+        out_shape=(jax.ShapeDtypeStruct((n_rows, 4 * head_dim), bf16), jax.ShapeDtypeStruct(k_flat.shape, bf16), jax.ShapeDtypeStruct(v_flat.shape, bf16)),
         in_specs=[pl.BlockSpec(memory_space=pltpu.SMEM), vmem, vmem, vmem, hbm, hbm],
         out_specs=(vmem, hbm, hbm),
-        scratch_shapes=[pltpu.VMEM(block, jnp.bfloat16), pltpu.VMEM(block, jnp.bfloat16), pltpu.SemaphoreType.DMA((2, depth)), pltpu.SemaphoreType.DMA((2, depth))],
-        compiler_params=pltpu.CompilerParams(vmem_limit_bytes=60 * 2**20),
-        cost_estimate=pl.CostEstimate(flops=n_rows * 8 * cache_len * 4 * LANES * 4, bytes_accessed=n_bytes, transcendentals=0),
+        scratch_shapes=[pltpu.VMEM(block, bf16), pltpu.VMEM(block, bf16), pltpu.VMEM((n_rows, 8, LANES), f32), pltpu.VMEM((n_rows, 16, LANES), f32),
+                        pltpu.VMEM((n_rows, 16, LANES), f32), pltpu.VMEM((n_rows, 8, LANES), f32), pltpu.VMEM((group, 8, n_cols), f32), pltpu.VMEM((group, 8, n_cols), bf16),
+                        dma((2, depth)), dma((2, depth))],
+        compiler_params=pltpu.CompilerParams(vmem_limit_bytes=(32 if cache_len <= 64 else 48) * 2**20),
+        cost_estimate=pl.CostEstimate(flops=n_rows * 8 * n_cols * LANES * 4, bytes_accessed=4 * k_flat.size * 2, transcendentals=0),
         name=f"attend_{cache_len}",
-    )(positions, q_rows, fresh(k_new), fresh(v_new), k_flat, v_flat)
-    head_out = heads.reshape(n_rows, halves, kv_loc * group_size, LANES).transpose(0, 2, 1, 3).reshape(n_rows, kv_loc * group_size, head_dim)
-    return head_out, unflat(k_out), unflat(v_out)
+    )(positions, qkv, *tables, k_flat, v_flat)
+    return heads, unflat(k_out), unflat(v_out)
 
 
 FF_CHUNK = 512
@@ -159,7 +169,7 @@
     if post:
         res_ref, wo_hbm, wg_hbm, wu_hbm, wd_hbm = (next(it) for _ in range(5))
     if qkv:
-        wi_hbm = next(it)
+        wq_hbm, wk_hbm, wv_hbm = (next(it) for _ in range(3))
         hid_ref, qkv_ref = next(it), next(it)
     else:
         out_ref = next(it)
@@ -168,7 +178,7 @@
         hall, apart, arecv, mpart, mrecv, wo, wg, wu, wd, sib_out, sib_in, mine, x_in, u_all = (next(it) for _ in range(14))
         y_ss, y_rs, ff_ss, ff_rs = (next(it) for _ in range(4))
     if qkv:
-        wi, q_out, q_in, q_mine, q_x, q_ss, q_rs = (next(it) for _ in range(7))
+        wi, wq, wk, wv, q_out, q_in, q_mine, q_x, q_ss, q_rs = (next(it) for _ in range(10))
 
     model, me = lax.axis_index("model"), lax.axis_index("data")
     x_pos, core = me // 2, lax.rem(me, 2)
@@ -199,7 +209,16 @@
         wu_load = load(wu_hbm.at[layer], wu, ld_sem.at[2])
         wd_load = load(wd_hbm.at[layer], wd, ld_sem.at[3])
     if qkv:
-        wi_load = load(wi_hbm, wi, ld_sem.at[4])
+        in_loads = [load(src.at[layer + 1], dst, ld_sem.at[4 + k]) for k, (src, dst) in enumerate(((wq_hbm, wq), (wk_hbm, wk), (wv_hbm, wv)))]
+
+    def relay_weights():
+        col = 0
+        for copy, weight in zip(in_loads, (wq, wk, wv)):
+            copy.wait()
+            n_heads, head_dim = weight.shape[1:]
+            for h in range(n_heads):
+                wi[:, col:col + head_dim] = weight[:, h, :]
+                col += head_dim
 
     barrier = pltpu.get_barrier_semaphore()
     for dev in (sib, part, diag):
@@ -232,14 +251,19 @@
         inverse = lax.rsqrt(total / width + NORM_EPS)
         tcol[...] = jnp.transpose(jnp.broadcast_to(inverse, (LANES, 4 * rows)))
 
+    def gain_row(k):
+        at, which = (layer + 1, 0) if k == 3 else (layer, k + 1)
+        return 1.0 + g_ref[at, which:which + 1, pl.ds(pl.multiple_of(me * share, LANES), share)].astype(jnp.float32)
+
     def scaled(block, value, gain):
-        return value * jnp.concatenate([tcol[block, :]] * (share // LANES), axis=1) * g_ref[gain:gain + 1, :]
+        return value * jnp.concatenate([tcol[block, :]] * (share // LANES), axis=1) * gain_row(gain)
 
     blocks = (OWN, SIB, PART, DIAG)
     if first:
         for k, (dev, there) in enumerate(((sib, SIB), (part, PART), (diag, DIAG))):
             cols = pl.ds(pl.multiple_of(dev * share, LANES), share)
             send(x_ref.at[:, cols], hid_ref.at[there, :], misc_ss.at[k], misc_rs.at[k], dev)
+        relay_weights()
         hid_ref[OWN, :] = x_ref[:, pl.ds(pl.multiple_of(me * share, LANES), share)]
         square_sums(OWN, hid_ref[OWN, :].astype(jnp.float32))
         for copy, block in zip(list(sends), (SIB, PART, DIAG)):
@@ -323,6 +347,8 @@
             act_sibling(c).start()
 
         wd_load.wait()
+        if qkv:
+            relay_weights()
 
         def down(c):
             act_sibling(c).wait_recv()
@@ -365,7 +391,6 @@
         scales(3)
         for block in blocks:
             hp[block, :] = scaled(block, hid_ref[block, :].astype(jnp.float32), 3).astype(jnp.bfloat16)
-        wi_load.wait()
         n_q = wi.shape[1] // QKV_CHUNK
 
         def q_partner(c):
@@ -400,15 +425,15 @@
         copy.wait_send()
 
 
-def comm(x, gains, qkv_weight=None, post=None, layer=0, collective_id=0):
+def comm(x, gains, in_weights=None, post=None, layer=0, collective_id=0):
     rows = x.shape[0]
-    share = gains.shape[1]
+    share = gains.shape[2] // 4
     n_rows = rows * 4
     f32, bf16, vmem, hbm = jnp.float32, jnp.bfloat16, pl.BlockSpec(memory_space=pltpu.VMEM), pl.BlockSpec(memory_space=pl.ANY)
     dma = pltpu.SemaphoreType.DMA
     args, specs = [x, gains], [vmem, vmem]
     scratch = [pltpu.VMEM((n_rows, LANES), f32), pltpu.VMEM((4, 8, n_rows), f32), pltpu.VMEM((4, 3, 8, n_rows), f32), pltpu.VMEM((n_rows, share), bf16),
-               dma((4, 3)), dma((4, 3)), dma((6,)), dma((6,)), dma((5,))]
+               dma((4, 3)), dma((4, 3)), dma((6,)), dma((6,)), dma((7,))]
     n_ff = 0
     if post is not None:
         residual, w_o, w_gate, w_up, w_down = post
@@ -420,17 +445,19 @@
         scratch += [pltpu.VMEM(w_o.shape[1:], bf16), pltpu.VMEM((share, ff), bf16), pltpu.VMEM((share, ff), bf16), pltpu.VMEM((ff, share), bf16)]
         scratch += [pltpu.VMEM((n_ff, 2 * rows, 2 * FF_CHUNK), f32)] * 3 + [pltpu.VMEM((n_ff, rows, 2 * FF_CHUNK), f32), pltpu.VMEM((n_ff, n_rows, FF_CHUNK), bf16)]
         scratch += [dma((8,)), dma((8,)), dma((5, n_ff)), dma((5, n_ff))]
-    if qkv_weight is not None:
-        args.append(qkv_weight)
-        specs.append(hbm)
-        n_q = qkv_weight.shape[1] // QKV_CHUNK
-        scratch += [pltpu.VMEM(qkv_weight.shape, bf16)] + [pltpu.VMEM((n_q, 2 * rows, QKV_CHUNK), f32)] * 3 + [pltpu.VMEM((n_q, rows, QKV_CHUNK), f32), dma((2, n_q)), dma((2, n_q))]
-        out_shape = (jax.ShapeDtypeStruct((n_rows, share), bf16), jax.ShapeDtypeStruct((rows, qkv_weight.shape[1]), f32))
+    if in_weights is not None:
+        args += list(in_weights)
+        specs += [hbm] * 3
+        n_in = sum(w.shape[2] * w.shape[3] for w in in_weights)
+        n_q = n_in // QKV_CHUNK
+        scratch += [pltpu.VMEM((share, n_in), bf16)] + [pltpu.VMEM(w.shape[1:], bf16) for w in in_weights]
+        scratch += [pltpu.VMEM((n_q, 2 * rows, QKV_CHUNK), f32)] * 3 + [pltpu.VMEM((n_q, rows, QKV_CHUNK), f32), dma((2, n_q)), dma((2, n_q))]
+        out_shape = (jax.ShapeDtypeStruct((n_rows, share), bf16), jax.ShapeDtypeStruct((rows, n_in), f32))
         out_specs = (vmem, vmem)
     else:
         out_shape = jax.ShapeDtypeStruct((rows, 4 * share), bf16)
         out_specs = vmem
-    cfg = {"post": post is not None, "qkv": qkv_weight is not None, "first": post is None, "layer": layer, "rows": rows, "share": share, "width": 4 * share, "n_ff": n_ff}
+    cfg = {"post": post is not None, "qkv": in_weights is not None, "first": post is None, "layer": layer, "rows": rows, "share": share, "width": 4 * share, "n_ff": n_ff}
     return pl.pallas_call(
         functools.partial(comm_kernel, cfg),
         out_shape=out_shape, in_specs=specs, out_specs=out_specs, scratch_shapes=scratch,
@@ -439,34 +466,17 @@
     )(*args)
 
 
-def attention(qkv, positions, k_cache, v_cache, n_q):
-    n_rows = qkv.shape[0]
-    n_kv, head_dim = k_cache.shape[2:]
-    q_proj = qkv[:, :n_q * head_dim].reshape(n_rows, n_q, head_dim)
-    k_proj = qkv[:, n_q * head_dim:(n_q + n_kv) * head_dim].reshape(n_rows, n_kv, head_dim)
-    v_proj = qkv[:, (n_q + n_kv) * head_dim:].reshape(n_rows, n_kv, head_dim)
-    cos_t, sin_t = rope_tables(positions, head_dim)
-    q_new = (rotary(q_proj, cos_t, sin_t) * head_dim ** -0.5).astype(jnp.bfloat16)
-    k_new = rotary(k_proj, cos_t, sin_t).astype(jnp.bfloat16)
-    head_out, k_cache, v_cache = attend(q_new, k_new, v_proj.astype(jnp.bfloat16), positions, k_cache, v_cache)
-    return head_out.reshape(n_rows, -1), k_cache, v_cache
-
-
 def solution(mesh):
     def device_step(hidden, positions, k_local, v_local, k_global, v_global, w_q, w_k, w_v, w_o, w_gate, w_up, w_down, norm_gains):
         share = w_q.shape[1]
-        n_q = w_q.shape[2]
-        gains = 1.0 + lax.dynamic_slice_in_dim(norm_gains, lax.axis_index("data") * share, share, axis=2).astype(jnp.float32)
-        in_weights = [jnp.concatenate([w[layer].reshape(share, -1) for w in (w_q, w_k, w_v)], axis=1) for layer in range(2)]
-        out_weights = w_o.reshape(2, -1, share)
-        first_gains = jnp.concatenate([gains[0, 1:], gains[0, :1]], axis=0)
-        mid_gains = jnp.concatenate([gains[0, 1:], gains[1, :1]], axis=0)
-        last_gains = jnp.concatenate([gains[1, 1:], gains[1, :1]], axis=0)
-        residual, qkv = comm(hidden[:, 0, :], first_gains, in_weights[0], collective_id=0)
-        heads, k_local, v_local = attention(qkv, positions, k_local, v_local, n_q)
-        residual, qkv = comm(heads, mid_gains, in_weights[1], (residual, out_weights, w_gate, w_up, w_down), layer=0, collective_id=1)
-        heads, k_global, v_global = attention(qkv, positions, k_global, v_global, n_q)
-        final = comm(heads, last_gains, None, (residual, out_weights, w_gate, w_up, w_down), layer=1, collective_id=2)[:, None, :]
+        tables = rope_tables(positions, w_q.shape[3])
+        in_weights = (w_q, w_k, w_v)
+        post_weights = (w_o.reshape(2, -1, share), w_gate, w_up, w_down)
+        residual, qkv = comm(hidden[:, 0, :], norm_gains, in_weights, layer=-1, collective_id=0)
+        heads, k_local, v_local = attend(qkv, tables, positions, k_local, v_local)
+        residual, qkv = comm(heads, norm_gains, in_weights, (residual,) + post_weights, layer=0, collective_id=1)
+        heads, k_global, v_global = attend(qkv, tables, positions, k_global, v_global)
+        final = comm(heads, norm_gains, None, (residual,) + post_weights, layer=1, collective_id=2)[:, None, :]
         return final, k_local, v_local, k_global, v_global
 
     in_specs = (ROW_SPEC, POS_SPEC, CACHE_SPEC, CACHE_SPEC, CACHE_SPEC, CACHE_SPEC, PROJ_IN_SPEC, PROJ_IN_SPEC, PROJ_IN_SPEC, PROJ_OUT_SPEC, FF_IN_SPEC, FF_IN_SPEC, FF_OUT_SPEC, GAIN_SPEC)

time: 399 us -> 360 us (0.902)
  Pallas kernels: 372 us -> 345 us
  local copies, waits for them, and re-layouts: 19 us -> 13.1 us
  other arithmetic: 5.85 us -> 0.93 us
    pallas_call x2, Pallas kernels: 78.4 us -> 50 us  [attend(): pl.pallas_call(functools.partial(attend_kernel, cache_len, n_rows, group,...]
    unnamed x15 -> x25, local copies, waits for them, and re-layouts: 4.72 us -> 13.1 us
    slice x11 -> x0, local copies, waits for them, and re-layouts: 7.03 us -> none  [the longest x3 4.09 us: device_step(): w[layer].reshape(share, -1)]
    another operation x10 -> x0, local copies, waits for them, and re-layouts: 4.76 us -> none  [the longest x8 3.3 us: fresh(): jnp.tile(new.reshape(n_rows, kv_loc, halves, LANES).transpose(0, 2, 1, 3)...]
where the time goes in v4:
time: 360 us
  Pallas kernels  345 us (96%)
  local copies, waits for them, and re-layouts  13.1 us (4%)
    pallas_call x3, Pallas kernels, comm(): pl.pallas_call(functools.partial(comm_kernel, cfg), out_shape=out_shape,...  295 us
    pallas_call x2, Pallas kernels, attend(): pl.pallas_call(functools.partial(attend_kernel, cache_len, n_rows, group,...  50 us
    unnamed x25, local copies, waits for them, and re-layouts  13.1 us

profile of v4, /device:TPU:0, one launch (start us, length us, event | category | flops | bytes accessed | tf_op | source)
XLA Modules:
  0.0 360.0 jit_solution(8007275605167650049)
XLA Ops:
  0.6 0.0 copy-start.11
  0.6 0.7 convert_element_type.10
  1.4 0.2 multiply_sine_fusion
  1.6 0.0 copy-start
  1.6 1.7 copy-done
  3.3 0.0 copy-start.1
  3.3 1.3 copy-done.1
  4.6 0.0 copy-start.2
  4.6 1.3 copy-done.2
  6.0 0.0 copy-start.6
  6.0 0.8 copy-done.6
  6.7 0.0 copy-start.8
  6.7 1.0 copy-done.8
  7.7 0.0 copy-start.3
  7.7 27.7 %comm_0.1 = (bf16[256,640]{1,0:T(8,128)(2,1)S(1)}, f32[64,2048]{1,0:T(8,128)S(1)}) custom-call(bf16[64,2560]{1,0:T(8,128)(2,1)S(1)} %bitcast.45, bf16[2,4,2560]{2,1,0:T(4,128)(2,1)S(1)} %copy-done.6, bf16[2,640,4,256]{3,2,1,0:T(4,128)(2,1)S(1)} %copy-done, bf16[2,640,2,256]{3,2,1,0:T(2,128)(2,1)S(1)} %copy-done.1, bf16[2,640,2,256]{3,2,1,0:T(2,128)(2,1)S(1)} %copy-done.2), custom_call_target="tpu_custom_call" | custom-call | tf_op jit(solution)/shard_map/comm_0/pallas_call | solution.py:461
  35.4 0.0 copy-start.7
  35.5 0.7 copy-done.7
  36.2 0.0 copy-done.11
  36.2 0.0 copy-done.3
  36.2 0.0 copy-start.4
  36.2 2.2 copy-done.4
  38.4 6.4 %attend_64.1 = (bf16[64,1024]{1,0:T(8,128)(2,1)S(1)}, bf16[64,256,128]{2,1,0:T(8,128)(2,1)}, bf16[64,256,128]{2,1,0:T(8,128)(2,1)}) custom-call(s32[64]{0:T(128)S(1)} %copy-done.11, f32[64,2048]{1,0:T(8,128)S(1)} %get-tuple-element.15.qkv_ref, f32[64,128]{1,0:T(8,128)S(1)} %get-tuple-element.26.cos_ref, f32[64,128]{1,0:T(8,128)S(1)} %get-tuple-element.25.sin_ref, ...), custom_call_target="tpu_custom_call" | custom-call | flops 67108864 | bytes 16777216 | tf_op jit(solution)/shard_map/attend_64/pallas_call | solution.py:143
  44.8 0.0 copy-start.9
  44.8 0.6 copy-done.9
  45.5 140.7 %comm_1.1 = (bf16[256,640]{1,0:T(8,128)(2,1)}, f32[64,2048]{1,0:T(8,128)}) custom-call(bf16[64,1024]{1,0:T(8,128)(2,1)} %copy-done.9, bf16[2,4,2560]{2,1,0:T(4,128)(2,1)} %refs_1_.5, bf16[256,640]{1,0:T(8,128)(2,1)} %copy-done.7, bf16[2,1024,640]{2,1,0:T(8,128)(2,1)} %bitcast.48, bf16[2,640,5120]{2,1,0:T(8,128)(2,1)} %refs_4_.5, ...), custom_call_target="tpu_custom_call" | custom-call | tf_op jit(solution)/shard_map/comm_1/pallas_call | solution.py:461
  186.2 0.0 copy-start.5
  186.2 1.0 copy-done.5
  187.2 43.5 %attend_512.1 = (bf16[64,1024]{1,0:T(8,128)(2,1)S(1)}, bf16[64,2048,128]{2,1,0:T(8,128)(2,1)}, bf16[64,2048,128]{2,1,0:T(8,128)(2,1)}) custom-call(s32[64]{0:T(128)S(1)} %copy-done.11, f32[64,2048]{1,0:T(8,128)S(1)} %copy-done.5, f32[64,128]{1,0:T(8,128)S(1)} %get-tuple-element.26.cos_ref, f32[64,128]{1,0:T(8,128)S(1)} %get-tuple-element.25.sin_ref, ...), custom_call_target="tpu_custom_call" | custom-call | flops 536870912 | bytes 134217728 | tf_op jit(solution)/shard_map/attend_512/pallas_call | solution.py:143
  230.8 0.0 copy-start.10
  230.8 0.6 copy-done.10
  231.4 126.8 %comm_2.1 = bf16[64,2560]{1,0:T(8,128)(2,1)} custom-call(bf16[64,1024]{1,0:T(8,128)(2,1)} %copy-done.10, bf16[2,4,2560]{2,1,0:T(4,128)(2,1)} %refs_1_.5, bf16[256,640]{1,0:T(8,128)(2,1)} %get-tuple-element.20.refs_2_, bf16[2,1024,640]{2,1,0:T(8,128)(2,1)} %bitcast.49, bf16[2,640,5120]{2,1,0:T(8,128)(2,1)} %refs_4_.5, bf16[2,640,5120]{2,1,0:T(8,128)(2,1)} %refs_5_.3, ...), custom_call_target="tpu_custom_call" | custom-call | tf_op jit(solution)/shard_map/comm_2/pallas_call | solution.py:461
  358.2 1.7 copy.28
  (1 shorter events, 0.0 us)
Async XLA Ops:
  0.6 35.5 %copy-start.11 = (s32[64]{0:T(128)S(1)}, s32[64]{0:T(128)}, u32[]{:S(2)}) copy-start(s32[64]{0:T(128)} %pos_ref.3) | copy-start | bytes 772
  1.6 1.7 copy-start
  3.3 1.3 copy-start.1
  4.6 1.3 copy-start.2
  6.0 0.8 copy-start.6
  6.7 1.0 copy-start.8
  7.7 28.5 %copy-start.3 = (bf16[64,64,2,256]{3,2,1,0:T(2,128)(2,1)S(1)}, bf16[64,64,2,256]{3,2,1,0:T(2,128)(2,1)}, u32[]{:S(2)}) copy-start(bf16[64,64,2,256]{3,2,1,0:T(2,128)(2,1)} %param.16) | copy-start | bytes 12582916
  35.4 0.7 copy-start.7
  36.2 2.2 copy-start.4
  44.8 0.7 copy-start.9
  186.2 1.0 copy-start.5
  230.8 0.7 copy-start.10

commit v5 on v4

--- a/solution.py
+++ b/solution.py
@@ -148,7 +148,7 @@
         scratch_shapes=[pltpu.VMEM(block, bf16), pltpu.VMEM(block, bf16), pltpu.VMEM((n_rows, 8, LANES), f32), pltpu.VMEM((n_rows, 16, LANES), f32),
                         pltpu.VMEM((n_rows, 16, LANES), f32), pltpu.VMEM((n_rows, 8, LANES), f32), pltpu.VMEM((group, 8, n_cols), f32), pltpu.VMEM((group, 8, n_cols), bf16),
                         dma((2, depth)), dma((2, depth))],
-        compiler_params=pltpu.CompilerParams(vmem_limit_bytes=(32 if cache_len <= 64 else 48) * 2**20),
+        compiler_params=pltpu.CompilerParams(vmem_limit_bytes=62 * 2**20),
         cost_estimate=pl.CostEstimate(flops=n_rows * 8 * n_cols * LANES * 4, bytes_accessed=4 * k_flat.size * 2, transcendentals=0),
         name=f"attend_{cache_len}",
     )(positions, qkv, *tables, k_flat, v_flat)
@@ -160,10 +160,13 @@
 MESH = pl.DeviceIdType.MESH
 
 
+GROUPS = 2
+
+
 def comm_kernel(cfg, *refs):
     it = iter(refs)
     post, layer, rows, share, width = cfg["post"], cfg["layer"], cfg["rows"], cfg["share"], cfg["width"]
-    qkv, first, n_ff = cfg["qkv"], cfg["first"], cfg["n_ff"]
+    qkv, n_ff, n_q = cfg["qkv"], cfg["n_ff"], cfg["n_q"]
     x_ref = next(it)
     g_ref = next(it)
     if post:
@@ -183,7 +186,10 @@
     model, me = lax.axis_index("model"), lax.axis_index("data")
     x_pos, core = me // 2, lax.rem(me, 2)
     sib, part, diag = x_pos * 2 + 1 - core, (1 - x_pos) * 2 + core, (1 - x_pos) * 2 + 1 - core
+    n_group = 4 * rows
     DIAG, SIB, PART, OWN = (pl.ds(i * rows, rows) for i in range(4))
+    blocks = (OWN, SIB, PART, DIAG)
+    mine_rows = [pl.ds(h * rows, rows) for h in range(GROUPS)]
     sends = []
 
     def remote(src, dst, send_sem, recv_sem, data=None):
@@ -195,8 +201,6 @@
         copy.start()
         sends.append(copy)
         return copy
-
-    loads = []
 
     def load(src, dst, sem):
         copy = pltpu.make_async_copy(src, dst, sem)
@@ -226,242 +230,295 @@
     pl.semaphore_signal(barrier, inc=1, device_id={"model": 1 - model}, device_id_type=MESH)
     pl.semaphore_wait(barrier, 4)
 
-    def square_sums(block, value):
+    def square_sums(h, block, value):
         total = None
         for k in range(share // LANES):
             piece = value[:, k * LANES:(k + 1) * LANES]
             total = piece * piece if total is None else total + piece * piece
-        tcol[block, :] = total
-
-    def scales(idx):
-        own = jnp.sum(jnp.transpose(tcol[...]).reshape(LANES // 8, 8, 4 * rows), axis=0)
-        st_src[idx] = own
-        copies = [send(st_src.at[idx], st_rcv.at[idx, k], st_ss.at[idx, k], st_rs.at[idx, k], dev) for k, dev in enumerate((sib, part, diag))]
+        tcol[h, block, :] = total
+
+    flip_low = lax.rem(lax.broadcasted_iota(jnp.int32, (8, n_group), 1) // rows, 2) == 0
+
+    def start_scales(h, which):
+        idx = which * GROUPS + h
+        st_src[idx] = jnp.sum(jnp.transpose(tcol[h]).reshape(LANES // 8, 8, n_group), axis=0)
+        return [send(st_src.at[idx], st_rcv.at[idx, k], st_ss.at[idx, k], st_rs.at[idx, k], dev) for k, dev in enumerate((sib, part, diag))]
+
+    def end_scales(h, which, copies):
+        idx = which * GROUPS + h
         for copy in copies:
             copy.wait_recv()
 
         def swap(value):
-            return jnp.concatenate([value[:, LANES:], value[:, :LANES]], axis=1)
+            return pltpu.roll(value, 2 * rows, 1)
 
         def flip(value):
-            return jnp.concatenate([pltpu.roll(value[:, :LANES], LANES // 2, 1), pltpu.roll(value[:, LANES:], LANES // 2, 1)], axis=1)
-
-        total = own + swap(st_rcv[idx, 0]) + flip(st_rcv[idx, 1]) + swap(flip(st_rcv[idx, 2]))
+            return jnp.where(flip_low, pltpu.roll(value, n_group - rows, 1), pltpu.roll(value, rows, 1))
+
+        total = st_src[idx] + swap(st_rcv[idx, 0]) + flip(st_rcv[idx, 1]) + swap(flip(st_rcv[idx, 2]))
         total = jnp.sum(total, axis=0, keepdims=True)
         inverse = lax.rsqrt(total / width + NORM_EPS)
-        tcol[...] = jnp.transpose(jnp.broadcast_to(inverse, (LANES, 4 * rows)))
+        tcol[h] = jnp.transpose(jnp.broadcast_to(inverse, (LANES, n_group)))
+
+    def scales(h, which):
+        end_scales(h, which, start_scales(h, which))
 
     def gain_row(k):
         at, which = (layer + 1, 0) if k == 3 else (layer, k + 1)
         return 1.0 + g_ref[at, which:which + 1, pl.ds(pl.multiple_of(me * share, LANES), share)].astype(jnp.float32)
 
-    def scaled(block, value, gain):
-        return value * jnp.concatenate([tcol[block, :]] * (share // LANES), axis=1) * gain_row(gain)
-
-    blocks = (OWN, SIB, PART, DIAG)
-    if first:
-        for k, (dev, there) in enumerate(((sib, SIB), (part, PART), (diag, DIAG))):
-            cols = pl.ds(pl.multiple_of(dev * share, LANES), share)
-            send(x_ref.at[:, cols], hid_ref.at[there, :], misc_ss.at[k], misc_rs.at[k], dev)
+    def scaled(h, block, value, gain):
+        return value * jnp.concatenate([tcol[h, block, :]] * (share // LANES), axis=1) * gain_row(gain)
+
+    def q_partner(s):
+        return remote(q_mine.at[s, pl.ds(0, rows)], q_x.at[s], q_ss.at[1, s], q_rs.at[1, s], part)
+
+    def start_qkv(h):
+        for block in blocks:
+            square_sums(h, block, hid_ref[h, block, :].astype(jnp.float32))
+        scales(h, 3)
+        for block in blocks:
+            hp[h, block, :] = scaled(h, block, hid_ref[h, block, :].astype(jnp.float32), 3).astype(jnp.bfloat16)
+        before = None
+        for c in range(n_q):
+            s = h * n_q + c
+            sums = jnp.dot(hp[h], wi[:, c * QKV_CHUNK:(c + 1) * QKV_CHUNK], preferred_element_type=jnp.float32)
+            q_out[s] = sums[:2 * rows]
+            q_mine[s] = sums[2 * rows:]
+            copy = send(q_out.at[s], q_in.at[s], q_ss.at[0, s], q_rs.at[0, s], sib)
+            if c >= 1:
+                before.wait_recv()
+                q_mine[s - 1] = q_mine[s - 1] + q_in[s - 1]
+                q_partner(s - 1).start()
+            before = copy
+        before.wait_recv()
+        s = h * n_q + n_q - 1
+        q_mine[s] = q_mine[s] + q_in[s]
+        q_partner(s).start()
+
+    def end_qkv():
+        for h in range(GROUPS):
+            for c in range(n_q):
+                s = h * n_q + c
+                q_partner(s).wait_recv()
+                qkv_ref[mine_rows[h], c * QKV_CHUNK:(c + 1) * QKV_CHUNK] = q_mine[s, pl.ds(rows, rows), :] + q_x[s]
+        for s in range(GROUPS * n_q):
+            q_partner(s).wait_send()
+
+    if not post:
+        copies = []
+        for h in range(GROUPS):
+            for k, (dev, there) in enumerate(((sib, SIB), (part, PART), (diag, DIAG))):
+                cols = pl.ds(pl.multiple_of(dev * share, LANES), share)
+                copies.append(send(x_ref.at[mine_rows[h], cols], hid_ref.at[h, there, :], misc_ss.at[h * 3 + k], misc_rs.at[h * 3 + k], dev))
         relay_weights()
-        hid_ref[OWN, :] = x_ref[:, pl.ds(pl.multiple_of(me * share, LANES), share)]
-        square_sums(OWN, hid_ref[OWN, :].astype(jnp.float32))
-        for copy, block in zip(list(sends), (SIB, PART, DIAG)):
-            copy.wait_recv()
-            square_sums(block, hid_ref[block, :].astype(jnp.float32))
-    if post:
-        to_part = send(x_ref, hall.at[PART, :], misc_ss.at[0], misc_rs.at[0], part)
-        to_sib = send(x_ref, hall.at[SIB, :], misc_ss.at[1], misc_rs.at[1], sib)
+        for h in range(GROUPS):
+            hid_ref[h, OWN, :] = x_ref[mine_rows[h], pl.ds(pl.multiple_of(me * share, LANES), share)]
+            for copy in copies[h * 3:h * 3 + 3]:
+                copy.wait_recv()
+            start_qkv(h)
+        end_qkv()
+    else:
+        to_part = send(x_ref, hall.at[2], misc_ss.at[0], misc_rs.at[0], part)
+        to_sib = send(x_ref, hall.at[1], misc_ss.at[1], misc_rs.at[1], sib)
         wo_load.wait()
-        y_copies = []
-        for k, block in enumerate(blocks):
-            if k == 1:
-                to_sib.wait_recv()
-            if k == 2:
-                to_part.wait_recv()
-                forward = send(hall.at[PART, :], hall.at[DIAG, :], misc_ss.at[2], misc_rs.at[2], sib)
-            if k == 3:
-                forward.wait_recv()
-            heads = x_ref[...] if k == 0 else hall[block, :]
-            apart[block, :] = jnp.dot(heads, wo[...], preferred_element_type=jnp.float32)
-            y_copies.append(send(apart.at[block, :], arecv.at[block, :], y_ss.at[k], y_rs.at[k]))
-        for copy, block in zip(y_copies, blocks):
-            copy.wait_recv()
-            total = apart[block, :] + arecv[block, :]
-            arecv[block, :] = total
-            square_sums(block, total)
-        scales(0)
-        for block in blocks:
-            mid = (res_ref[block, :].astype(jnp.float32) + scaled(block, arecv[block, :], 0)).astype(jnp.bfloat16).astype(jnp.float32)
-            arecv[block, :] = mid
-            mpart[block, :] = jnp.zeros((rows, share), jnp.float32)
-        for block in blocks:
-            square_sums(block, arecv[block, :])
-        scales(1)
-        for block in blocks:
-            hp[block, :] = scaled(block, arecv[block, :], 1).astype(jnp.bfloat16)
+        y_copies = [[None] * 4 for _ in range(GROUPS)]
+
+        def project(k, heads):
+            sums = jnp.dot(heads, wo[...], preferred_element_type=jnp.float32)
+            for h in range(GROUPS):
+                apart[h, blocks[k], :] = sums[h * rows:(h + 1) * rows]
+
+        def to_model(h, k):
+            y_copies[h][k] = send(apart.at[h, blocks[k], :], arecv.at[h, blocks[k], :], y_ss.at[h * 4 + k], y_rs.at[h * 4 + k])
+
+        project(0, x_ref[...])
+        to_model(0, 0)
+        to_sib.wait_recv()
+        project(1, hall[1])
+        to_model(0, 1)
+        to_model(1, 0)
+        to_part.wait_recv()
+        forward = send(hall.at[2], hall.at[0], misc_ss.at[2], misc_rs.at[2], sib)
+        project(2, hall[2])
+        to_model(0, 2)
+        forward.wait_recv()
+        project(3, hall[0])
+        to_model(0, 3)
+        for h in range(1, GROUPS):
+            for k in range(1, 4):
+                to_model(h, k)
+
+        def enter_ff(h):
+            for k, block in enumerate(blocks):
+                y_copies[h][k].wait_recv()
+                total = apart[h, block, :] + arecv[h, block, :]
+                arecv[h, block, :] = total
+                square_sums(h, block, total)
+            scales(h, 0)
+            for block in blocks:
+                residual = res_ref[h, block, :].astype(jnp.float32)
+                mid = (residual + scaled(h, block, arecv[h, block, :], 0)).astype(jnp.bfloat16).astype(jnp.float32)
+                arecv[h, block, :] = mid
+            for block in blocks:
+                square_sums(h, block, arecv[h, block, :])
+            copies = start_scales(h, 1)
+            mpart[h] = jnp.zeros((n_group, share), jnp.float32)
+            end_scales(h, 1, copies)
+            for block in blocks:
+                hp[h, block, :] = scaled(h, block, arecv[h, block, :], 1).astype(jnp.bfloat16)
+
+        def to_sibling(s):
+            return remote(sib_out.at[s], sib_in.at[s], ff_ss.at[0, s], ff_rs.at[0, s], sib)
+
+        def to_partner(s):
+            return remote(mine.at[s, pl.ds(0, rows)], x_in.at[s], ff_ss.at[1, s], ff_rs.at[1, s], part)
+
+        def act_partner(s):
+            return remote(u_all.at[s, OWN], u_all.at[s, PART], ff_ss.at[2, s], ff_rs.at[2, s], part)
+
+        def act_sibling(s):
+            return remote(u_all.at[s, OWN], u_all.at[s, SIB], ff_ss.at[3, s], ff_rs.at[3, s], sib)
+
+        def act_forward(s):
+            return remote(u_all.at[s, PART], u_all.at[s, DIAG], ff_ss.at[4, s], ff_rs.at[4, s], sib)
+
+        def add_sibling(s):
+            to_sibling(s).wait_recv()
+            mine[s] = mine[s] + sib_in[s]
+            to_partner(s).start()
+
+        def gate_up(h):
+            @pl.loop(0, n_ff)
+            def _(c):
+                s = h * n_ff + c
+                cols = pl.ds(pl.multiple_of(c * FF_CHUNK, FF_CHUNK), FF_CHUNK)
+                for k, weight in enumerate((wg, wu)):
+                    sums = jnp.dot(hp[h], weight[:, cols], preferred_element_type=jnp.float32)
+                    sib_out[s, :, pl.ds(k * FF_CHUNK, FF_CHUNK)] = sums[:2 * rows]
+                    mine[s, :, pl.ds(k * FF_CHUNK, FF_CHUNK)] = sums[2 * rows:]
+                to_sibling(s).start()
+
+                @pl.when(c >= 1)
+                def _():
+                    add_sibling(s - 1)
+
+            add_sibling(h * n_ff + n_ff - 1)
+
+        enter_ff(0)
         wg_load.wait()
         wu_load.wait()
-
-        def to_sibling(c):
-            return remote(sib_out.at[c], sib_in.at[c], ff_ss.at[0, c], ff_rs.at[0, c], sib)
-
-        def to_partner(c):
-            return remote(mine.at[c, pl.ds(0, rows)], x_in.at[c], ff_ss.at[1, c], ff_rs.at[1, c], part)
-
-        def act_partner(c):
-            return remote(u_all.at[c, OWN], u_all.at[c, PART], ff_ss.at[2, c], ff_rs.at[2, c], part)
-
-        def act_sibling(c):
-            return remote(u_all.at[c, OWN], u_all.at[c, SIB], ff_ss.at[3, c], ff_rs.at[3, c], sib)
-
-        def act_forward(c):
-            return remote(u_all.at[c, PART], u_all.at[c, DIAG], ff_ss.at[4, c], ff_rs.at[4, c], sib)
-
-        def add_sibling(c):
-            to_sibling(c).wait_recv()
-            mine[c] = mine[c] + sib_in[c]
-            to_partner(c).start()
-
-        @pl.loop(0, n_ff)
-        def _(c):
-            cols = pl.ds(pl.multiple_of(c * FF_CHUNK, FF_CHUNK), FF_CHUNK)
-            for k, weight in enumerate((wg, wu)):
-                sums = jnp.dot(hp[...], weight[:, cols], preferred_element_type=jnp.float32)
-                sib_out[c, :, pl.ds(k * FF_CHUNK, FF_CHUNK)] = sums[:2 * rows]
-                mine[c, :, pl.ds(k * FF_CHUNK, FF_CHUNK)] = sums[2 * rows:]
-            to_sibling(c).start()
-
-            @pl.when(c >= 1)
-            def _():
-                add_sibling(c - 1)
-
-        add_sibling(n_ff - 1)
-
-        @pl.loop(0, n_ff)
-        def _(c):
-            to_partner(c).wait_recv()
-            both = mine[c, pl.ds(rows, rows), :] + x_in[c]
-            u_all[c, OWN, :] = (jax.nn.gelu(both[:, :FF_CHUNK], approximate=True) * both[:, FF_CHUNK:]).astype(jnp.bfloat16)
-            act_partner(c).start()
-            act_sibling(c).start()
-
-        wd_load.wait()
+        for h in range(GROUPS):
+            gate_up(h)
+            if h + 1 < GROUPS:
+                enter_ff(h + 1)
         if qkv:
             relay_weights()
 
-        def down(c):
-            act_sibling(c).wait_recv()
-            act_forward(c).wait_recv()
+        @pl.loop(0, GROUPS * n_ff)
+        def _(s):
+            to_partner(s).wait_recv()
+            both = mine[s, pl.ds(rows, rows), :] + x_in[s]
+            u_all[s, OWN, :] = (jax.nn.gelu(both[:, :FF_CHUNK], approximate=True) * both[:, FF_CHUNK:]).astype(jnp.bfloat16)
+            act_partner(s).start()
+            act_sibling(s).start()
+
+        wd_load.wait()
+
+        def down(h, c):
+            s = h * n_ff + c
+            act_sibling(s).wait_recv()
+            act_forward(s).wait_recv()
             deep = pl.ds(pl.multiple_of(c * FF_CHUNK, FF_CHUNK), FF_CHUNK)
-            mpart[...] += jnp.dot(u_all[c], wd[deep, :], preferred_element_type=jnp.float32)
-
-        @pl.loop(0, n_ff)
-        def _(c):
-            act_partner(c).wait_recv()
-            act_forward(c).start()
-
-            @pl.when(c >= 1)
-            def _():
-                down(c - 1)
-
-        down(n_ff - 1)
-        y_copies = [send(mpart.at[block, :], mrecv.at[block, :], y_ss.at[4 + k], y_rs.at[4 + k]) for k, block in enumerate(blocks)]
-        for copy, block in zip(y_copies, blocks):
+            mpart[h] += jnp.dot(u_all[s], wd[deep, :], preferred_element_type=jnp.float32)
+
+        m_copies = []
+        for h in range(GROUPS):
+            @pl.loop(0, n_ff)
+            def _(c):
+                act_partner(h * n_ff + c).wait_recv()
+                act_forward(h * n_ff + c).start()
+
+                @pl.when(c >= 1)
+                def _():
+                    down(h, c - 1)
+
+            down(h, n_ff - 1)
+            m_copies.append(send(mpart.at[h], mrecv.at[h], y_ss.at[4 * GROUPS + h], y_rs.at[4 * GROUPS + h]))
+
+        out_copies = []
+        for h in range(GROUPS):
+            m_copies[h].wait_recv()
+            for block in blocks:
+                total = mpart[h, block, :] + mrecv[h, block, :]
+                mrecv[h, block, :] = total
+                square_sums(h, block, total)
+            scales(h, 2)
+            for block in blocks:
+                value = (arecv[h, block, :] + scaled(h, block, mrecv[h, block, :], 2)).astype(jnp.bfloat16)
+                if qkv:
+                    hid_ref[h, block, :] = value
+                else:
+                    hp[h, block, :] = value
+            if qkv:
+                start_qkv(h)
+            else:
+                here = pl.ds(pl.multiple_of(me * share, LANES), share)
+                for k, (dev, block) in enumerate(((sib, SIB), (part, PART), (diag, DIAG))):
+                    out_copies.append(send(hp.at[h, block, :], out_ref.at[mine_rows[h], here], misc_ss.at[3 + h * 3 + k], misc_rs.at[3 + h * 3 + k], dev))
+                out_ref[mine_rows[h], here] = hp[h, OWN, :]
+        if qkv:
+            end_qkv()
+        for copy in out_copies:
             copy.wait_recv()
-            total = mpart[block, :] + mrecv[block, :]
-            mrecv[block, :] = total
-            square_sums(block, total)
-        scales(2)
-        for block in blocks:
-            value = (arecv[block, :] + scaled(block, mrecv[block, :], 2)).astype(jnp.bfloat16)
-            if qkv:
-                hid_ref[block, :] = value
-            else:
-                hp[block, :] = value
-        if qkv:
-            for block in blocks:
-                square_sums(block, hid_ref[block, :].astype(jnp.float32))
-
-        @pl.loop(0, n_ff)
-        def _(c):
-            for copy in (to_sibling(c), to_partner(c), act_partner(c), act_sibling(c), act_forward(c)):
+
+        @pl.loop(0, GROUPS * n_ff)
+        def _(s):
+            for copy in (to_sibling(s), to_partner(s), act_partner(s), act_sibling(s), act_forward(s)):
                 copy.wait_send()
-    if qkv:
-        scales(3)
-        for block in blocks:
-            hp[block, :] = scaled(block, hid_ref[block, :].astype(jnp.float32), 3).astype(jnp.bfloat16)
-        n_q = wi.shape[1] // QKV_CHUNK
-
-        def q_partner(c):
-            return remote(q_mine.at[c, pl.ds(0, rows)], q_x.at[c], q_ss.at[1, c], q_rs.at[1, c], part)
-
-        for c in range(n_q):
-            sums = jnp.dot(hp[...], wi[:, c * QKV_CHUNK:(c + 1) * QKV_CHUNK], preferred_element_type=jnp.float32)
-            q_out[c] = sums[:2 * rows]
-            q_mine[c] = sums[2 * rows:]
-            copy = send(q_out.at[c], q_in.at[c], q_ss.at[0, c], q_rs.at[0, c], sib)
-            if c >= 1:
-                before.wait_recv()
-                q_mine[c - 1] = q_mine[c - 1] + q_in[c - 1]
-                q_partner(c - 1).start()
-            before = copy
-        before.wait_recv()
-        q_mine[n_q - 1] = q_mine[n_q - 1] + q_in[n_q - 1]
-        q_partner(n_q - 1).start()
-        for c in range(n_q):
-            q_partner(c).wait_recv()
-            qkv_ref[:, c * QKV_CHUNK:(c + 1) * QKV_CHUNK] = q_mine[c, pl.ds(rows, rows), :] + q_x[c]
-        for c in range(n_q):
-            q_partner(c).wait_send()
-    else:
-        here = pl.ds(pl.multiple_of(me * share, LANES), share)
-        out_copies = [send(hp.at[block, :], out_ref.at[:, here], misc_ss.at[3 + k], misc_rs.at[3 + k], dev)
-                      for k, (dev, block) in enumerate(((sib, SIB), (part, PART), (diag, DIAG)))]
-        out_ref[:, here] = hp[OWN, :]
-        for dev, copy in zip((sib, part, diag), out_copies):
-            copy.wait_recv()
     for copy in sends:
         copy.wait_send()
 
 
 def comm(x, gains, in_weights=None, post=None, layer=0, collective_id=0):
-    rows = x.shape[0]
+    rows = x.shape[0] // GROUPS
     share = gains.shape[2] // 4
-    n_rows = rows * 4
+    n_group = rows * 4
     f32, bf16, vmem, hbm = jnp.float32, jnp.bfloat16, pl.BlockSpec(memory_space=pltpu.VMEM), pl.BlockSpec(memory_space=pl.ANY)
     dma = pltpu.SemaphoreType.DMA
     args, specs = [x, gains], [vmem, vmem]
-    scratch = [pltpu.VMEM((n_rows, LANES), f32), pltpu.VMEM((4, 8, n_rows), f32), pltpu.VMEM((4, 3, 8, n_rows), f32), pltpu.VMEM((n_rows, share), bf16),
-               dma((4, 3)), dma((4, 3)), dma((6,)), dma((6,)), dma((7,))]
-    n_ff = 0
+    n_stat = 4 * GROUPS
+    scratch = [pltpu.VMEM((GROUPS, n_group, LANES), f32), pltpu.VMEM((n_stat, 8, n_group), f32), pltpu.VMEM((n_stat, 3, 8, n_group), f32), pltpu.VMEM((GROUPS, n_group, share), bf16),
+               dma((n_stat, 3)), dma((n_stat, 3)), dma((3 + 3 * GROUPS,)), dma((3 + 3 * GROUPS,)), dma((7,))]
+    n_ff = n_q = 0
     if post is not None:
         residual, w_o, w_gate, w_up, w_down = post
         args += list(post)
         specs += [vmem, hbm, hbm, hbm, hbm]
         ff = w_gate.shape[2]
         n_ff = ff // FF_CHUNK
-        scratch += [pltpu.VMEM((n_rows, w_o.shape[1]), bf16)] + [pltpu.VMEM((n_rows, share), f32)] * 4
+        steps = GROUPS * n_ff
+        scratch += [pltpu.VMEM((3, GROUPS * rows, w_o.shape[1]), bf16)] + [pltpu.VMEM((GROUPS, n_group, share), f32)] * 4
         scratch += [pltpu.VMEM(w_o.shape[1:], bf16), pltpu.VMEM((share, ff), bf16), pltpu.VMEM((share, ff), bf16), pltpu.VMEM((ff, share), bf16)]
-        scratch += [pltpu.VMEM((n_ff, 2 * rows, 2 * FF_CHUNK), f32)] * 3 + [pltpu.VMEM((n_ff, rows, 2 * FF_CHUNK), f32), pltpu.VMEM((n_ff, n_rows, FF_CHUNK), bf16)]
-        scratch += [dma((8,)), dma((8,)), dma((5, n_ff)), dma((5, n_ff))]
+        scratch += [pltpu.VMEM((steps, 2 * rows, 2 * FF_CHUNK), f32)] * 3 + [pltpu.VMEM((steps, rows, 2 * FF_CHUNK), f32), pltpu.VMEM((steps, n_group, FF_CHUNK), bf16)]
+        scratch += [dma((5 * GROUPS,)), dma((5 * GROUPS,)), dma((5, steps)), dma((5, steps))]
     if in_weights is not None:
         args += list(in_weights)
         specs += [hbm] * 3
         n_in = sum(w.shape[2] * w.shape[3] for w in in_weights)
         n_q = n_in // QKV_CHUNK
         scratch += [pltpu.VMEM((share, n_in), bf16)] + [pltpu.VMEM(w.shape[1:], bf16) for w in in_weights]
-        scratch += [pltpu.VMEM((n_q, 2 * rows, QKV_CHUNK), f32)] * 3 + [pltpu.VMEM((n_q, rows, QKV_CHUNK), f32), dma((2, n_q)), dma((2, n_q))]
-        out_shape = (jax.ShapeDtypeStruct((n_rows, share), bf16), jax.ShapeDtypeStruct((rows, n_in), f32))
+        scratch += [pltpu.VMEM((GROUPS * n_q, 2 * rows, QKV_CHUNK), f32)] * 3 + [pltpu.VMEM((GROUPS * n_q, rows, QKV_CHUNK), f32), dma((2, GROUPS * n_q)), dma((2, GROUPS * n_q))]
+        out_shape = (jax.ShapeDtypeStruct((GROUPS, n_group, share), bf16), jax.ShapeDtypeStruct((GROUPS * rows, n_in), f32))
         out_specs = (vmem, vmem)
     else:
-        out_shape = jax.ShapeDtypeStruct((rows, 4 * share), bf16)
+        out_shape = jax.ShapeDtypeStruct((GROUPS * rows, 4 * share), bf16)
         out_specs = vmem
-    cfg = {"post": post is not None, "qkv": in_weights is not None, "first": post is None, "layer": layer, "rows": rows, "share": share, "width": 4 * share, "n_ff": n_ff}
+    cfg = {"post": post is not None, "qkv": in_weights is not None, "layer": layer, "rows": rows, "share": share, "width": 4 * share, "n_ff": n_ff, "n_q": n_q}
     return pl.pallas_call(
         functools.partial(comm_kernel, cfg),
         out_shape=out_shape, in_specs=specs, out_specs=out_specs, scratch_shapes=scratch,
-        compiler_params=pltpu.CompilerParams(collective_id=collective_id, has_side_effects=True, vmem_limit_bytes=(62 if post is not None else 20) * 2**20),
+        compiler_params=pltpu.CompilerParams(collective_id=collective_id, has_side_effects=True, vmem_limit_bytes=62 * 2**20),
         name=f"comm_{collective_id}",
     )(*args)
 

time: 360 us -> 347 us (0.964)
  local copies, waits for them, and re-layouts: 13.1 us -> 1.72 us
    unnamed x25 -> x1, local copies, waits for them, and re-layouts: 13.1 us -> 1.72 us
    pallas_call x3, Pallas kernels: 295 us -> 290 us  [comm(): pl.pallas_call(functools.partial(comm_kernel, cfg), out_shape=out_shape,...]
where the time goes in v5:
time: 347 us
  Pallas kernels  343 us (99%)
    pallas_call x3, Pallas kernels, comm(): pl.pallas_call(functools.partial(comm_kernel, cfg), out_shape=out_shape,...  290 us
    pallas_call x2, Pallas kernels, attend(): pl.pallas_call(functools.partial(attend_kernel, cache_len, n_rows, group,...  52.9 us

profile of v5, /device:TPU:0, one launch (start us, length us, event | category | flops | bytes accessed | tf_op | source)
XLA Modules:
  0.0 347.2 jit_solution(9626693999999332337)
XLA Ops:
  0.6 0.7 convert_element_type.10
  1.3 0.8 multiply_sine_fusion
  2.1 33.0 %comm_0.1 = (bf16[2,128,640]{2,1,0:T(8,128)(2,1)}, f32[64,2048]{1,0:T(8,128)}) custom-call(bf16[64,2560]{1,0:T(8,128)(2,1)} %bitcast.50, bf16[2,4,2560]{2,1,0:T(4,128)(2,1)} %refs_1_.5, bf16[2,640,4,256]{3,2,1,0:T(4,128)(2,1)} %refs_7_.1, bf16[2,640,2,256]{3,2,1,0:T(2,128)(2,1)} %refs_8_.1, bf16[2,640,2,256]{3,2,1,0:T(2,128)(2,1)} %refs_9_.1), custom_call_target="tpu_custom_call" | custom-call | tf_op jit(solution)/shard_map/comm_0/pallas_call | solution.py:518
  35.1 8.2 %attend_64.1 = (bf16[64,1024]{1,0:T(8,128)(2,1)}, bf16[64,256,128]{2,1,0:T(8,128)(2,1)}, bf16[64,256,128]{2,1,0:T(8,128)(2,1)}) custom-call(s32[64]{0:T(128)} %pos_ref.3, f32[64,2048]{1,0:T(8,128)} %get-tuple-element.15.qkv_ref, f32[64,128]{1,0:T(8,128)} %get-tuple-element.26.cos_ref, f32[64,128]{1,0:T(8,128)} %get-tuple-element.25.sin_ref, ...), custom_call_target="tpu_custom_call" | custom-call | flops 67108864 | bytes 16777216 | tf_op jit(solution)/shard_map/attend_64/pallas_call | solution.py:143
  43.3 136.0 %comm_1.1 = (bf16[2,128,640]{2,1,0:T(8,128)(2,1)}, f32[64,2048]{1,0:T(8,128)}) custom-call(bf16[64,1024]{1,0:T(8,128)(2,1)} %get-tuple-element.16.refs_0_, bf16[2,4,2560]{2,1,0:T(4,128)(2,1)} %refs_1_.5, bf16[2,128,640]{2,1,0:T(8,128)(2,1)} %get-tuple-element.17.refs_2_, bf16[2,1024,640]{2,1,0:T(8,128)(2,1)} %bitcast.45, bf16[2,640,5120]{2,1,0:T(8,128)(2,1)} %refs_4_.5, ...), custom_call_target="tpu_custom_call" | custom-call | tf_op jit(solution)/shard_map/comm_1/pallas_call | solution.py:518
  179.3 44.7 %attend_512.1 = (bf16[64,1024]{1,0:T(8,128)(2,1)}, bf16[64,2048,128]{2,1,0:T(8,128)(2,1)}, bf16[64,2048,128]{2,1,0:T(8,128)(2,1)}) custom-call(s32[64]{0:T(128)} %pos_ref.3, f32[64,2048]{1,0:T(8,128)} %get-tuple-element.18.qkv_ref, f32[64,128]{1,0:T(8,128)} %get-tuple-element.26.cos_ref, f32[64,128]{1,0:T(8,128)} %get-tuple-element.25.sin_ref, ...), custom_call_target="tpu_custom_call" | custom-call | flops 536870912 | bytes 134217728 | tf_op jit(solution)/shard_map/attend_512/pallas_call | solution.py:143
  224.1 121.4 %comm_2.1 = bf16[64,2560]{1,0:T(8,128)(2,1)} custom-call(bf16[64,1024]{1,0:T(8,128)(2,1)} %get-tuple-element.19.refs_0_, bf16[2,4,2560]{2,1,0:T(4,128)(2,1)} %refs_1_.5, bf16[2,128,640]{2,1,0:T(8,128)(2,1)} %get-tuple-element.20.refs_2_, bf16[2,1024,640]{2,1,0:T(8,128)(2,1)} %bitcast.46, bf16[2,640,5120]{2,1,0:T(8,128)(2,1)} %refs_4_.5, ...), custom_call_target="tpu_custom_call" | custom-call | tf_op jit(solution)/shard_map/comm_2/pallas_call | solution.py:518
  345.5 1.7 copy.28
  (1 shorter events, 0.0 us)

commit v6 on v5

--- a/solution.py
+++ b/solution.py
@@ -155,30 +155,36 @@
     return heads, unflat(k_out), unflat(v_out)
 
 
-FF_CHUNK = 512
-QKV_CHUNK = 512
+FF_CHUNK = 1024
+QKV_CHUNK = 1024
 MESH = pl.DeviceIdType.MESH
 
 
-GROUPS = 2
+GROUPS = 4
 
 
 def comm_kernel(cfg, *refs):
     it = iter(refs)
     post, layer, rows, share, width = cfg["post"], cfg["layer"], cfg["rows"], cfg["share"], cfg["width"]
     qkv, n_ff, n_q = cfg["qkv"], cfg["n_ff"], cfg["n_q"]
-    x_ref = next(it)
-    g_ref = next(it)
+    raw = cfg["raw"]
+    x_hbm, g_hbm = next(it), next(it)
     if post:
-        res_ref, wo_hbm, wg_hbm, wu_hbm, wd_hbm = (next(it) for _ in range(5))
+        res_hbm, wo_hbm, wg_hbm, wu_hbm, wd_hbm = (next(it) for _ in range(5))
     if qkv:
         wq_hbm, wk_hbm, wv_hbm = (next(it) for _ in range(3))
-        hid_ref, qkv_ref = next(it), next(it)
+        if post:
+            hid_ref = next(it)
+        qkv_ref = next(it)
     else:
         out_ref = next(it)
-    tcol, st_src, st_rcv, hp, st_ss, st_rs, misc_ss, misc_rs, ld_sem = (next(it) for _ in range(9))
+    x_ref, g_ref, tcol, st_src, st_rcv, hp, st_ss, st_rs, misc_ss, misc_rs, ld_sem = (next(it) for _ in range(11))
+    if not post:
+        out_rows = next(it)
     if post:
-        hall, apart, arecv, mpart, mrecv, wo, wg, wu, wd, sib_out, sib_in, mine, x_in, u_all = (next(it) for _ in range(14))
+        if raw:
+            raw_ref = next(it)
+        res_ref, hall, apart, arecv, mpart, mrecv, wo, wg, wu, wd, sib_out, sib_in, mine, x_in, u_all = (next(it) for _ in range(15))
         y_ss, y_rs, ff_ss, ff_rs = (next(it) for _ in range(4))
     if qkv:
         wi, wq, wk, wv, q_out, q_in, q_mine, q_x, q_ss, q_rs = (next(it) for _ in range(10))
@@ -207,7 +213,9 @@
         copy.start()
         return copy
 
+    early = [load(x_hbm, x_ref, ld_sem.at[7]), load(g_hbm, g_ref, ld_sem.at[8])]
     if post:
+        early.append(load(res_hbm, raw_ref if raw else res_ref, ld_sem.at[9]))
         wo_load = load(wo_hbm.at[layer], wo, ld_sem.at[0])
         wg_load = load(wg_hbm.at[layer], wg, ld_sem.at[1])
         wu_load = load(wu_hbm.at[layer], wu, ld_sem.at[2])
@@ -215,10 +223,11 @@
     if qkv:
         in_loads = [load(src.at[layer + 1], dst, ld_sem.at[4 + k]) for k, (src, dst) in enumerate(((wq_hbm, wq), (wk_hbm, wk), (wv_hbm, wv)))]
 
-    def relay_weights():
-        col = 0
-        for copy, weight in zip(in_loads, (wq, wk, wv)):
-            copy.wait()
+    def relay_weights(c):
+        col = c * QKV_CHUNK
+        for k in ((0,), (1, 2))[c]:
+            in_loads[k].wait()
+            weight = (wq, wk, wv)[k]
             n_heads, head_dim = weight.shape[1:]
             for h in range(n_heads):
                 wi[:, col:col + head_dim] = weight[:, h, :]
@@ -228,6 +237,9 @@
     for dev in (sib, part, diag):
         pl.semaphore_signal(barrier, inc=1, device_id={"data": dev}, device_id_type=MESH)
     pl.semaphore_signal(barrier, inc=1, device_id={"model": 1 - model}, device_id_type=MESH)
+    tcol[...] = jnp.zeros_like(tcol)
+    for copy in early:
+        copy.wait()
     pl.semaphore_wait(barrier, 4)
 
     def square_sums(h, block, value):
@@ -237,11 +249,11 @@
             total = piece * piece if total is None else total + piece * piece
         tcol[h, block, :] = total
 
-    flip_low = lax.rem(lax.broadcasted_iota(jnp.int32, (8, n_group), 1) // rows, 2) == 0
+    lane_block = lax.broadcasted_iota(jnp.int32, (8, LANES), 1) // rows
 
     def start_scales(h, which):
         idx = which * GROUPS + h
-        st_src[idx] = jnp.sum(jnp.transpose(tcol[h]).reshape(LANES // 8, 8, n_group), axis=0)
+        st_src[idx] = jnp.sum(jnp.transpose(tcol[h]).reshape(LANES // 8, 8, LANES), axis=0)
         return [send(st_src.at[idx], st_rcv.at[idx, k], st_ss.at[idx, k], st_rs.at[idx, k], dev) for k, dev in enumerate((sib, part, diag))]
 
     def end_scales(h, which, copies):
@@ -249,19 +261,14 @@
         for copy in copies:
             copy.wait_recv()
 
-        def swap(value):
-            return pltpu.roll(value, 2 * rows, 1)
-
-        def flip(value):
-            return jnp.where(flip_low, pltpu.roll(value, n_group - rows, 1), pltpu.roll(value, rows, 1))
-
-        total = st_src[idx] + swap(st_rcv[idx, 0]) + flip(st_rcv[idx, 1]) + swap(flip(st_rcv[idx, 2]))
+        def exchange(value, n):
+            even = lax.rem(lane_block // n, 2) == 0
+            return jnp.where(even, pltpu.roll(value, LANES - n * rows, 1), pltpu.roll(value, n * rows, 1))
+
+        total = st_src[idx] + exchange(st_rcv[idx, 0], 2) + exchange(st_rcv[idx, 1], 1) + exchange(exchange(st_rcv[idx, 2], 1), 2)
         total = jnp.sum(total, axis=0, keepdims=True)
         inverse = lax.rsqrt(total / width + NORM_EPS)
-        tcol[h] = jnp.transpose(jnp.broadcast_to(inverse, (LANES, n_group)))
-
-    def scales(h, which):
-        end_scales(h, which, start_scales(h, which))
+        tcol[h] = jnp.transpose(jnp.broadcast_to(inverse, (LANES, LANES)))
 
     def gain_row(k):
         at, which = (layer + 1, 0) if k == 3 else (layer, k + 1)
@@ -273,15 +280,12 @@
     def q_partner(s):
         return remote(q_mine.at[s, pl.ds(0, rows)], q_x.at[s], q_ss.at[1, s], q_rs.at[1, s], part)
 
-    def start_qkv(h):
-        for block in blocks:
-            square_sums(h, block, hid_ref[h, block, :].astype(jnp.float32))
-        scales(h, 3)
-        for block in blocks:
-            hp[h, block, :] = scaled(h, block, hid_ref[h, block, :].astype(jnp.float32), 3).astype(jnp.bfloat16)
+    def start_qkv(h, relay=False):
         before = None
         for c in range(n_q):
             s = h * n_q + c
+            if relay:
+                relay_weights(c)
             sums = jnp.dot(hp[h], wi[:, c * QKV_CHUNK:(c + 1) * QKV_CHUNK], preferred_element_type=jnp.float32)
             q_out[s] = sums[:2 * rows]
             q_mine[s] = sums[2 * rows:]
@@ -305,22 +309,36 @@
         for s in range(GROUPS * n_q):
             q_partner(s).wait_send()
 
-    if not post:
+    def spread(src, dst, base):
         copies = []
         for h in range(GROUPS):
             for k, (dev, there) in enumerate(((sib, SIB), (part, PART), (diag, DIAG))):
                 cols = pl.ds(pl.multiple_of(dev * share, LANES), share)
-                copies.append(send(x_ref.at[mine_rows[h], cols], hid_ref.at[h, there, :], misc_ss.at[h * 3 + k], misc_rs.at[h * 3 + k], dev))
-        relay_weights()
+                i = base + h * 3 + k
+                copies.append(send(src.at[mine_rows[h], cols], dst.at[h, there, :], misc_ss.at[i], misc_rs.at[i], dev))
+        return copies
+
+    my_cols = pl.ds(pl.multiple_of(me * share, LANES), share)
+    if not post:
+        xn = out_rows
         for h in range(GROUPS):
-            hid_ref[h, OWN, :] = x_ref[mine_rows[h], pl.ds(pl.multiple_of(me * share, LANES), share)]
+            value = x_ref[mine_rows[h], :].astype(jnp.float32)
+            inverse = lax.rsqrt(jnp.mean(value * value, axis=1, keepdims=True) + NORM_EPS)
+            xn[mine_rows[h], :] = (value * inverse * (1.0 + g_ref[0, 0:1, :].astype(jnp.float32))).astype(jnp.bfloat16)
+        copies = spread(xn, hp, 0)
+        for h in range(GROUPS):
+            hp[h, OWN, :] = xn[mine_rows[h], my_cols]
             for copy in copies[h * 3:h * 3 + 3]:
                 copy.wait_recv()
-            start_qkv(h)
+            start_qkv(h, relay=h == 0)
         end_qkv()
     else:
         to_part = send(x_ref, hall.at[2], misc_ss.at[0], misc_rs.at[0], part)
         to_sib = send(x_ref, hall.at[1], misc_ss.at[1], misc_rs.at[1], sib)
+        if raw:
+            raw_copies = spread(raw_ref, res_ref, 3)
+            for h in range(GROUPS):
+                res_ref[h, OWN, :] = raw_ref[mine_rows[h], my_cols]
         wo_load.wait()
         y_copies = [[None] * 4 for _ in range(GROUPS)]
 
@@ -329,42 +347,48 @@
             for h in range(GROUPS):
                 apart[h, blocks[k], :] = sums[h * rows:(h + 1) * rows]
 
-        def to_model(h, k):
-            y_copies[h][k] = send(apart.at[h, blocks[k], :], arecv.at[h, blocks[k], :], y_ss.at[h * 4 + k], y_rs.at[h * 4 + k])
+        def to_model(*pairs):
+            for h, k in pairs:
+                y_copies[h][k] = send(apart.at[h, blocks[k], :], arecv.at[h, blocks[k], :], y_ss.at[h * 4 + k], y_rs.at[h * 4 + k])
 
         project(0, x_ref[...])
-        to_model(0, 0)
+        to_model((0, 0), (1, 0))
         to_sib.wait_recv()
         project(1, hall[1])
-        to_model(0, 1)
-        to_model(1, 0)
+        to_model((0, 1), (1, 1), (2, 0))
         to_part.wait_recv()
         forward = send(hall.at[2], hall.at[0], misc_ss.at[2], misc_rs.at[2], sib)
         project(2, hall[2])
-        to_model(0, 2)
+        to_model((0, 2))
         forward.wait_recv()
         project(3, hall[0])
-        to_model(0, 3)
-        for h in range(1, GROUPS):
-            for k in range(1, 4):
-                to_model(h, k)
-
-        def enter_ff(h):
+        to_model((0, 3), (1, 2), (1, 3), (2, 1), (2, 2), (2, 3), (3, 0), (3, 1), (3, 2), (3, 3))
+        stats = {}
+
+        def attn_sums(h):
             for k, block in enumerate(blocks):
                 y_copies[h][k].wait_recv()
                 total = apart[h, block, :] + arecv[h, block, :]
                 arecv[h, block, :] = total
                 square_sums(h, block, total)
-            scales(h, 0)
+            stats[h] = start_scales(h, 0)
+
+        def attn_residual(h):
+            end_scales(h, 0, stats[h])
+            if raw:
+                for copy in raw_copies[h * 3:h * 3 + 3]:
+                    copy.wait_recv()
             for block in blocks:
                 residual = res_ref[h, block, :].astype(jnp.float32)
                 mid = (residual + scaled(h, block, arecv[h, block, :], 0)).astype(jnp.bfloat16).astype(jnp.float32)
                 arecv[h, block, :] = mid
             for block in blocks:
                 square_sums(h, block, arecv[h, block, :])
-            copies = start_scales(h, 1)
+            stats[h] = start_scales(h, 1)
+
+        def attn_normed(h):
             mpart[h] = jnp.zeros((n_group, share), jnp.float32)
-            end_scales(h, 1, copies)
+            end_scales(h, 1, stats[h])
             for block in blocks:
                 hp[h, block, :] = scaled(h, block, arecv[h, block, :], 1).astype(jnp.bfloat16)
 
@@ -405,15 +429,27 @@
 
             add_sibling(h * n_ff + n_ff - 1)
 
-        enter_ff(0)
+        attn_sums(0)
+        attn_residual(0)
+        attn_sums(1)
+        attn_normed(0)
         wg_load.wait()
         wu_load.wait()
-        for h in range(GROUPS):
-            gate_up(h)
-            if h + 1 < GROUPS:
-                enter_ff(h + 1)
+        gate_up(0)
+        attn_residual(1)
+        attn_sums(2)
+        attn_normed(1)
+        gate_up(1)
+        attn_residual(2)
+        attn_sums(3)
+        attn_normed(2)
+        gate_up(2)
+        attn_residual(3)
+        attn_normed(3)
+        gate_up(3)
         if qkv:
-            relay_weights()
+            relay_weights(0)
+            relay_weights(1)
 
         @pl.loop(0, GROUPS * n_ff)
         def _(s):
@@ -447,13 +483,17 @@
             m_copies.append(send(mpart.at[h], mrecv.at[h], y_ss.at[4 * GROUPS + h], y_rs.at[4 * GROUPS + h]))
 
         out_copies = []
-        for h in range(GROUPS):
+
+        def ff_sums(h):
             m_copies[h].wait_recv()
             for block in blocks:
                 total = mpart[h, block, :] + mrecv[h, block, :]
                 mrecv[h, block, :] = total
                 square_sums(h, block, total)
-            scales(h, 2)
+            stats[h] = start_scales(h, 2)
+
+        def ff_residual(h):
+            end_scales(h, 2, stats[h])
             for block in blocks:
                 value = (arecv[h, block, :] + scaled(h, block, mrecv[h, block, :], 2)).astype(jnp.bfloat16)
                 if qkv:
@@ -461,12 +501,36 @@
                 else:
                     hp[h, block, :] = value
             if qkv:
-                start_qkv(h)
+                for block in blocks:
+                    square_sums(h, block, hid_ref[h, block, :].astype(jnp.float32))
+                stats[h] = start_scales(h, 3)
             else:
-                here = pl.ds(pl.multiple_of(me * share, LANES), share)
                 for k, (dev, block) in enumerate(((sib, SIB), (part, PART), (diag, DIAG))):
-                    out_copies.append(send(hp.at[h, block, :], out_ref.at[mine_rows[h], here], misc_ss.at[3 + h * 3 + k], misc_rs.at[3 + h * 3 + k], dev))
-                out_ref[mine_rows[h], here] = hp[h, OWN, :]
+                    i = 3 + h * 3 + k
+                    out_copies.append(send(hp.at[h, block, :], out_ref.at[mine_rows[h], my_cols], misc_ss.at[i], misc_rs.at[i], dev))
+                out_ref[mine_rows[h], my_cols] = hp[h, OWN, :]
+
+        def ff_normed(h):
+            end_scales(h, 3, stats[h])
+            for block in blocks:
+                hp[h, block, :] = scaled(h, block, hid_ref[h, block, :].astype(jnp.float32), 3).astype(jnp.bfloat16)
+            start_qkv(h)
+
+        ff_sums(0)
+        ff_sums(1)
+        ff_residual(0)
+        ff_sums(2)
+        ff_residual(1)
+        if qkv:
+            ff_normed(0)
+        ff_sums(3)
+        ff_residual(2)
+        if qkv:
+            ff_normed(1)
+        ff_residual(3)
+        if qkv:
+            ff_normed(2)
+            ff_normed(3)
         if qkv:
             end_qkv()
         for copy in out_copies:
@@ -486,19 +550,24 @@
     n_group = rows * 4
     f32, bf16, vmem, hbm = jnp.float32, jnp.bfloat16, pl.BlockSpec(memory_space=pltpu.VMEM), pl.BlockSpec(memory_space=pl.ANY)
     dma = pltpu.SemaphoreType.DMA
-    args, specs = [x, gains], [vmem, vmem]
+    args, specs = [x, gains], [hbm, hbm]
+    raw = post is not None and post[0].ndim == 2
     n_stat = 4 * GROUPS
-    scratch = [pltpu.VMEM((GROUPS, n_group, LANES), f32), pltpu.VMEM((n_stat, 8, n_group), f32), pltpu.VMEM((n_stat, 3, 8, n_group), f32), pltpu.VMEM((GROUPS, n_group, share), bf16),
-               dma((n_stat, 3)), dma((n_stat, 3)), dma((3 + 3 * GROUPS,)), dma((3 + 3 * GROUPS,)), dma((7,))]
+    n_misc = 3 + 3 * GROUPS
+    scratch = [pltpu.VMEM(x.shape, bf16), pltpu.VMEM(gains.shape, bf16), pltpu.VMEM((GROUPS, LANES, LANES), f32), pltpu.VMEM((n_stat, 8, LANES), f32), pltpu.VMEM((n_stat, 3, 8, LANES), f32), pltpu.VMEM((GROUPS, n_group, share), bf16),
+               dma((n_stat, 3)), dma((n_stat, 3)), dma((n_misc,)), dma((n_misc,)), dma((10,))]
+    if post is None:
+        scratch.append(pltpu.VMEM(x.shape, bf16))
     n_ff = n_q = 0
     if post is not None:
         residual, w_o, w_gate, w_up, w_down = post
         args += list(post)
-        specs += [vmem, hbm, hbm, hbm, hbm]
+        specs += [hbm] * 5
         ff = w_gate.shape[2]
         n_ff = ff // FF_CHUNK
         steps = GROUPS * n_ff
-        scratch += [pltpu.VMEM((3, GROUPS * rows, w_o.shape[1]), bf16)] + [pltpu.VMEM((GROUPS, n_group, share), f32)] * 4
+        scratch += [pltpu.VMEM(residual.shape, bf16)] if raw else []
+        scratch += [pltpu.VMEM((GROUPS, n_group, share), bf16), pltpu.VMEM((3, GROUPS * rows, w_o.shape[1]), bf16)] + [pltpu.VMEM((GROUPS, n_group, share), f32)] * 4
         scratch += [pltpu.VMEM(w_o.shape[1:], bf16), pltpu.VMEM((share, ff), bf16), pltpu.VMEM((share, ff), bf16), pltpu.VMEM((ff, share), bf16)]
         scratch += [pltpu.VMEM((steps, 2 * rows, 2 * FF_CHUNK), f32)] * 3 + [pltpu.VMEM((steps, rows, 2 * FF_CHUNK), f32), pltpu.VMEM((steps, n_group, FF_CHUNK), bf16)]
         scratch += [dma((5 * GROUPS,)), dma((5 * GROUPS,)), dma((5, steps)), dma((5, steps))]
@@ -509,12 +578,12 @@
         n_q = n_in // QKV_CHUNK
         scratch += [pltpu.VMEM((share, n_in), bf16)] + [pltpu.VMEM(w.shape[1:], bf16) for w in in_weights]
         scratch += [pltpu.VMEM((GROUPS * n_q, 2 * rows, QKV_CHUNK), f32)] * 3 + [pltpu.VMEM((GROUPS * n_q, rows, QKV_CHUNK), f32), dma((2, GROUPS * n_q)), dma((2, GROUPS * n_q))]
-        out_shape = (jax.ShapeDtypeStruct((GROUPS, n_group, share), bf16), jax.ShapeDtypeStruct((GROUPS * rows, n_in), f32))
-        out_specs = (vmem, vmem)
+        out_shape = [jax.ShapeDtypeStruct((GROUPS, n_group, share), bf16), jax.ShapeDtypeStruct((GROUPS * rows, n_in), f32)][post is None:]
+        out_specs = [vmem, vmem][post is None:]
     else:
         out_shape = jax.ShapeDtypeStruct((GROUPS * rows, 4 * share), bf16)
         out_specs = vmem
-    cfg = {"post": post is not None, "qkv": in_weights is not None, "layer": layer, "rows": rows, "share": share, "width": 4 * share, "n_ff": n_ff, "n_q": n_q}
+    cfg = {"raw": raw, "post": post is not None, "qkv": in_weights is not None, "layer": layer, "rows": rows, "share": share, "width": 4 * share, "n_ff": n_ff, "n_q": n_q}
     return pl.pallas_call(
         functools.partial(comm_kernel, cfg),
         out_shape=out_shape, in_specs=specs, out_specs=out_specs, scratch_shapes=scratch,
@@ -529,9 +598,10 @@
         tables = rope_tables(positions, w_q.shape[3])
         in_weights = (w_q, w_k, w_v)
         post_weights = (w_o.reshape(2, -1, share), w_gate, w_up, w_down)
-        residual, qkv = comm(hidden[:, 0, :], norm_gains, in_weights, layer=-1, collective_id=0)
+        hidden_rows = hidden[:, 0, :]
+        qkv, = comm(hidden_rows, norm_gains, in_weights, layer=-1, collective_id=0)
         heads, k_local, v_local = attend(qkv, tables, positions, k_local, v_local)
-        residual, qkv = comm(heads, norm_gains, in_weights, (residual,) + post_weights, layer=0, collective_id=1)
+        residual, qkv = comm(heads, norm_gains, in_weights, (hidden_rows,) + post_weights, layer=0, collective_id=1)
         heads, k_global, v_global = attend(qkv, tables, positions, k_global, v_global)
         final = comm(heads, norm_gains, None, (residual,) + post_weights, layer=1, collective_id=2)[:, None, :]
         return final, k_local, v_local, k_global, v_global

time: 347 us -> 341 us (0.983)
  Pallas kernels: 343 us -> 337 us
    pallas_call x3, Pallas kernels: 290 us -> 284 us  [comm(): pl.pallas_call(functools.partial(comm_kernel, cfg), out_shape=out_shape,...]
where the time goes in v6:
time: 341 us
  Pallas kernels  337 us (99%)
    pallas_call x3, Pallas kernels, comm(): pl.pallas_call(functools.partial(comm_kernel, cfg), out_shape=out_shape,...  284 us
    pallas_call x2, Pallas kernels, attend(): pl.pallas_call(functools.partial(attend_kernel, cache_len, n_rows, group,...  52.9 us

profile of v6, /device:TPU:0, one launch (start us, length us, event | category | flops | bytes accessed | tf_op | source)
XLA Modules:
  0.0 341.0 jit_solution(15214032241880916874)
XLA Ops:
  0.6 0.7 convert_element_type.10
  1.3 0.8 multiply_sine_fusion
  2.1 27.5 %comm_0.1.qkv_ref = f32[64,2048]{1,0:T(8,128)} custom-call(bf16[64,2560]{1,0:T(8,128)(2,1)} %bitcast.49, bf16[2,4,2560]{2,1,0:T(4,128)(2,1)} %refs_1_.5, bf16[2,640,4,256]{3,2,1,0:T(4,128)(2,1)} %refs_7_.1, bf16[2,640,2,256]{3,2,1,0:T(2,128)(2,1)} %refs_8_.1, bf16[2,640,2,256]{3,2,1,0:T(2,128)(2,1)} %refs_9_.1), custom_call_target="tpu_custom_call" | custom-call | tf_op jit(solution)/shard_map/comm_0/pallas_call | solution.py:587
  29.6 8.2 %attend_64.1 = (bf16[64,1024]{1,0:T(8,128)(2,1)}, bf16[64,256,128]{2,1,0:T(8,128)(2,1)}, bf16[64,256,128]{2,1,0:T(8,128)(2,1)}) custom-call(s32[64]{0:T(128)} %pos_ref.3, f32[64,2048]{1,0:T(8,128)} %comm_0.1.qkv_ref, f32[64,128]{1,0:T(8,128)} %get-tuple-element.22.cos_ref, f32[64,128]{1,0:T(8,128)} %get-tuple-element.21.sin_ref, ...), custom_call_target="tpu_custom_call" | custom-call | flops 67108864 | bytes 16777216 | tf_op jit(solution)/shard_map/attend_64/pallas_call | solution.py:143
  37.8 134.9 %comm_1.1 = (bf16[4,64,640]{2,1,0:T(8,128)(2,1)}, f32[64,2048]{1,0:T(8,128)}) custom-call(bf16[64,1024]{1,0:T(8,128)(2,1)} %get-tuple-element.13.refs_0_, bf16[2,4,2560]{2,1,0:T(4,128)(2,1)} %refs_1_.5, bf16[64,2560]{1,0:T(8,128)(2,1)} %bitcast.50, bf16[2,1024,640]{2,1,0:T(8,128)(2,1)} %bitcast.45, bf16[2,640,5120]{2,1,0:T(8,128)(2,1)} %refs_4_.5, ...), custom_call_target="tpu_custom_call" | custom-call | tf_op jit(solution)/shard_map/comm_1/pallas_call | solution.py:587
  172.7 44.7 %attend_512.1 = (bf16[64,1024]{1,0:T(8,128)(2,1)}, bf16[64,2048,128]{2,1,0:T(8,128)(2,1)}, bf16[64,2048,128]{2,1,0:T(8,128)(2,1)}) custom-call(s32[64]{0:T(128)} %pos_ref.3, f32[64,2048]{1,0:T(8,128)} %get-tuple-element.14.qkv_ref, f32[64,128]{1,0:T(8,128)} %get-tuple-element.22.cos_ref, f32[64,128]{1,0:T(8,128)} %get-tuple-element.21.sin_ref, ...), custom_call_target="tpu_custom_call" | custom-call | flops 536870912 | bytes 134217728 | tf_op jit(solution)/shard_map/attend_512/pallas_call | solution.py:143
  217.4 121.8 %comm_2.1 = bf16[64,2560]{1,0:T(8,128)(2,1)} custom-call(bf16[64,1024]{1,0:T(8,128)(2,1)} %get-tuple-element.15.refs_0_, bf16[2,4,2560]{2,1,0:T(4,128)(2,1)} %refs_1_.5, bf16[4,64,640]{2,1,0:T(8,128)(2,1)} %get-tuple-element.16.refs_2_, bf16[2,1024,640]{2,1,0:T(8,128)(2,1)} %bitcast.46, bf16[2,640,5120]{2,1,0:T(8,128)(2,1)} %refs_4_.5, ...), custom_call_target="tpu_custom_call" | custom-call | tf_op jit(solution)/shard_map/comm_2/pallas_call | solution.py:587
  339.3 1.7 copy.28
  (1 shorter events, 0.0 us)

commit v7 on v6

--- a/solution.py
+++ b/solution.py
@@ -125,8 +125,8 @@
 def attend(qkv, tables, positions, k_cache, v_cache):
     n_rows, cache_len, kv_loc, head_dim = k_cache.shape
     halves = head_dim // LANES
-    group = 16 if cache_len <= 64 else 4
-    depth = 4 if cache_len <= 64 else 6
+    group = 16 if cache_len <= 64 else 2
+    depth = 4 if cache_len <= 64 else 12
     f32, bf16 = jnp.float32, jnp.bfloat16
 
     def flat(cache):
@@ -155,7 +155,7 @@
     return heads, unflat(k_out), unflat(v_out)
 
 
-FF_CHUNK = 1024
+FF_CHUNK = 2560
 QKV_CHUNK = 1024
 MESH = pl.DeviceIdType.MESH
 

time: 341 us -> 355 us (1.041); the launches traced: 341 us -> 349 us
  Pallas kernels: 337 us -> 345 us
    pallas_call x3, Pallas kernels: 284 us -> 290 us  [comm(): pl.pallas_call(functools.partial(comm_kernel, cfg), out_shape=out_shape,...]
where the time goes in v7:
time: 355 us; the launch traced here: 349 us
  Pallas kernels  345 us (97%)
    pallas_call x3, Pallas kernels, comm(): pl.pallas_call(functools.partial(comm_kernel, cfg), out_shape=out_shape,...  290 us
    pallas_call x2, Pallas kernels, attend(): pl.pallas_call(functools.partial(attend_kernel, cache_len, n_rows, group,...  55 us

profile of v7, /device:TPU:0, one launch (start us, length us, event | category | flops | bytes accessed | tf_op | source)
XLA Modules:
  0.0 349.5 jit_solution(17899356363890564259)
XLA Ops:
  0.6 0.7 convert_element_type.10
  1.3 0.8 multiply_sine_fusion
  2.1 27.5 %comm_0.1.qkv_ref = f32[64,2048]{1,0:T(8,128)} custom-call(bf16[64,2560]{1,0:T(8,128)(2,1)} %bitcast.49, bf16[2,4,2560]{2,1,0:T(4,128)(2,1)} %refs_1_.5, bf16[2,640,4,256]{3,2,1,0:T(4,128)(2,1)} %refs_7_.1, bf16[2,640,2,256]{3,2,1,0:T(2,128)(2,1)} %refs_8_.1, bf16[2,640,2,256]{3,2,1,0:T(2,128)(2,1)} %refs_9_.1), custom_call_target="tpu_custom_call" | custom-call | tf_op jit(solution)/shard_map/comm_0/pallas_call | solution.py:587
  29.6 8.2 %attend_64.1 = (bf16[64,1024]{1,0:T(8,128)(2,1)}, bf16[64,256,128]{2,1,0:T(8,128)(2,1)}, bf16[64,256,128]{2,1,0:T(8,128)(2,1)}) custom-call(s32[64]{0:T(128)} %pos_ref.3, f32[64,2048]{1,0:T(8,128)} %comm_0.1.qkv_ref, f32[64,128]{1,0:T(8,128)} %get-tuple-element.22.cos_ref, f32[64,128]{1,0:T(8,128)} %get-tuple-element.21.sin_ref, ...), custom_call_target="tpu_custom_call" | custom-call | flops 67108864 | bytes 16777216 | tf_op jit(solution)/shard_map/attend_64/pallas_call | solution.py:143
  37.8 137.5 %comm_1.1 = (bf16[4,64,640]{2,1,0:T(8,128)(2,1)}, f32[64,2048]{1,0:T(8,128)}) custom-call(bf16[64,1024]{1,0:T(8,128)(2,1)} %get-tuple-element.13.refs_0_, bf16[2,4,2560]{2,1,0:T(4,128)(2,1)} %refs_1_.5, bf16[64,2560]{1,0:T(8,128)(2,1)} %bitcast.50, bf16[2,1024,640]{2,1,0:T(8,128)(2,1)} %bitcast.45, bf16[2,640,5120]{2,1,0:T(8,128)(2,1)} %refs_4_.5, ...), custom_call_target="tpu_custom_call" | custom-call | tf_op jit(solution)/shard_map/comm_1/pallas_call | solution.py:587
  175.4 46.8 %attend_512.1 = (bf16[64,1024]{1,0:T(8,128)(2,1)}, bf16[64,2048,128]{2,1,0:T(8,128)(2,1)}, bf16[64,2048,128]{2,1,0:T(8,128)(2,1)}) custom-call(s32[64]{0:T(128)} %pos_ref.3, f32[64,2048]{1,0:T(8,128)} %get-tuple-element.14.qkv_ref, f32[64,128]{1,0:T(8,128)} %get-tuple-element.22.cos_ref, f32[64,128]{1,0:T(8,128)} %get-tuple-element.21.sin_ref, ...), custom_call_target="tpu_custom_call" | custom-call | flops 536870912 | bytes 134217728 | tf_op jit(solution)/shard_map/attend_512/pallas_call | solution.py:143
  222.2 125.1 %comm_2.1 = bf16[64,2560]{1,0:T(8,128)(2,1)} custom-call(bf16[64,1024]{1,0:T(8,128)(2,1)} %get-tuple-element.15.refs_0_, bf16[2,4,2560]{2,1,0:T(4,128)(2,1)} %refs_1_.5, bf16[4,64,640]{2,1,0:T(8,128)(2,1)} %get-tuple-element.16.refs_2_, bf16[2,1024,640]{2,1,0:T(8,128)(2,1)} %bitcast.46, bf16[2,640,5120]{2,1,0:T(8,128)(2,1)} %refs_4_.5, ...), custom_call_target="tpu_custom_call" | custom-call | tf_op jit(solution)/shard_map/comm_2/pallas_call | solution.py:587
  347.3 1.7 copy.28
  (1 shorter events, 0.0 us)

commit v8 on v6

--- a/solution.py
+++ b/solution.py
@@ -46,7 +46,7 @@
         return (pltpu.make_async_copy(kbuf.at[slot], ko_hbm.at[rows], wr_sem.at[0, slot]),
                 pltpu.make_async_copy(vbuf.at[slot], vo_hbm.at[rows], wr_sem.at[1, slot]))
 
-    ahead = max(depth - 2, 1) if depth < n_steps else n_steps
+    ahead = depth // 2 if depth < n_steps else n_steps
     for step in range(ahead):
         for copy in reads(step):
             copy.start()
@@ -155,7 +155,8 @@
     return heads, unflat(k_out), unflat(v_out)
 
 
-FF_CHUNK = 1024
+FF_CHUNK = 512
+IN_FLIGHT = 2
 QKV_CHUNK = 1024
 MESH = pl.DeviceIdType.MESH
 
@@ -280,12 +281,10 @@
     def q_partner(s):
         return remote(q_mine.at[s, pl.ds(0, rows)], q_x.at[s], q_ss.at[1, s], q_rs.at[1, s], part)
 
-    def start_qkv(h, relay=False):
+    def start_qkv(h):
         before = None
         for c in range(n_q):
             s = h * n_q + c
-            if relay:
-                relay_weights(c)
             sums = jnp.dot(hp[h], wi[:, c * QKV_CHUNK:(c + 1) * QKV_CHUNK], preferred_element_type=jnp.float32)
             q_out[s] = sums[:2 * rows]
             q_mine[s] = sums[2 * rows:]
@@ -326,11 +325,13 @@
             inverse = lax.rsqrt(jnp.mean(value * value, axis=1, keepdims=True) + NORM_EPS)
             xn[mine_rows[h], :] = (value * inverse * (1.0 + g_ref[0, 0:1, :].astype(jnp.float32))).astype(jnp.bfloat16)
         copies = spread(xn, hp, 0)
+        relay_weights(0)
+        relay_weights(1)
         for h in range(GROUPS):
             hp[h, OWN, :] = xn[mine_rows[h], my_cols]
             for copy in copies[h * 3:h * 3 + 3]:
                 copy.wait_recv()
-            start_qkv(h, relay=h == 0)
+            start_qkv(h)
         end_qkv()
     else:
         to_part = send(x_ref, hall.at[2], misc_ss.at[0], misc_rs.at[0], part)
@@ -410,10 +411,14 @@
         def add_sibling(s):
             to_sibling(s).wait_recv()
             mine[s] = mine[s] + sib_in[s]
+
+            @pl.when(s >= IN_FLIGHT)
+            def _():
+                to_partner(s - IN_FLIGHT).wait_send()
             to_partner(s).start()
 
-        def gate_up(h):
-            @pl.loop(0, n_ff)
+        def gate_up(h, start, end):
+            @pl.loop(start, end)
             def _(c):
                 s = h * n_ff + c
                 cols = pl.ds(pl.multiple_of(c * FF_CHUNK, FF_CHUNK), FF_CHUNK)
@@ -423,11 +428,9 @@
                     mine[s, :, pl.ds(k * FF_CHUNK, FF_CHUNK)] = sums[2 * rows:]
                 to_sibling(s).start()
 
-                @pl.when(c >= 1)
+                @pl.when(s >= 1)
                 def _():
                     add_sibling(s - 1)
-
-            add_sibling(h * n_ff + n_ff - 1)
 
         attn_sums(0)
         attn_residual(0)
@@ -435,18 +438,19 @@
         attn_normed(0)
         wg_load.wait()
         wu_load.wait()
-        gate_up(0)
-        attn_residual(1)
-        attn_sums(2)
-        attn_normed(1)
-        gate_up(1)
-        attn_residual(2)
-        attn_sums(3)
-        attn_normed(2)
-        gate_up(2)
-        attn_residual(3)
-        attn_normed(3)
-        gate_up(3)
+        cuts = (n_ff * 3 // 10, n_ff * 7 // 10)
+        for h in range(GROUPS):
+            if h + 1 < GROUPS:
+                gate_up(h, 0, cuts[0])
+                attn_residual(h + 1)
+                gate_up(h, cuts[0], cuts[1])
+                attn_normed(h + 1)
+                if h + 2 < GROUPS:
+                    attn_sums(h + 2)
+                gate_up(h, cuts[1], n_ff)
+            else:
+                gate_up(h, 0, n_ff)
+        add_sibling(GROUPS * n_ff - 1)
         if qkv:
             relay_weights(0)
             relay_weights(1)
@@ -538,8 +542,10 @@
 
         @pl.loop(0, GROUPS * n_ff)
         def _(s):
-            for copy in (to_sibling(s), to_partner(s), act_partner(s), act_sibling(s), act_forward(s)):
+            for copy in (to_sibling(s), act_partner(s), act_sibling(s), act_forward(s)):
                 copy.wait_send()
+        for s in range(GROUPS * n_ff - IN_FLIGHT, GROUPS * n_ff):
+            to_partner(s).wait_send()
     for copy in sends:
         copy.wait_send()
 

time: 341 us -> 337 us (0.988)
  Pallas kernels: 337 us -> 333 us
    pallas_call x3, Pallas kernels: 284 us -> 280 us  [comm(): pl.pallas_call(functools.partial(comm_kernel, cfg), out_shape=out_shape,...]
where the time goes in v8:
time: 337 us; the launch traced here: 336 us
  Pallas kernels  333 us (99%)
    pallas_call x3, Pallas kernels, comm(): pl.pallas_call(functools.partial(comm_kernel, cfg), out_shape=out_shape,...  280 us
    pallas_call x2, Pallas kernels, attend(): pl.pallas_call(functools.partial(attend_kernel, cache_len, n_rows, group,...  52.9 us

profile of v8, /device:TPU:0, one launch (start us, length us, event | category | flops | bytes accessed | tf_op | source)
XLA Modules:
  0.0 336.5 jit_solution(3823977820698574742)
XLA Ops:
  0.6 0.7 convert_element_type.10
  1.3 0.8 multiply_sine_fusion
  2.1 25.4 %comm_0.1.qkv_ref = f32[64,2048]{1,0:T(8,128)} custom-call(bf16[64,2560]{1,0:T(8,128)(2,1)} %bitcast.49, bf16[2,4,2560]{2,1,0:T(4,128)(2,1)} %refs_1_.5, bf16[2,640,4,256]{3,2,1,0:T(4,128)(2,1)} %refs_7_.1, bf16[2,640,2,256]{3,2,1,0:T(2,128)(2,1)} %refs_8_.1, bf16[2,640,2,256]{3,2,1,0:T(2,128)(2,1)} %refs_9_.1), custom_call_target="tpu_custom_call" | custom-call | tf_op jit(solution)/shard_map/comm_0/pallas_call | solution.py:593
  27.6 8.2 %attend_64.1 = (bf16[64,1024]{1,0:T(8,128)(2,1)}, bf16[64,256,128]{2,1,0:T(8,128)(2,1)}, bf16[64,256,128]{2,1,0:T(8,128)(2,1)}) custom-call(s32[64]{0:T(128)} %pos_ref.3, f32[64,2048]{1,0:T(8,128)} %comm_0.1.qkv_ref, f32[64,128]{1,0:T(8,128)} %get-tuple-element.22.cos_ref, f32[64,128]{1,0:T(8,128)} %get-tuple-element.21.sin_ref, ...), custom_call_target="tpu_custom_call" | custom-call | flops 67108864 | bytes 16777216 | tf_op jit(solution)/shard_map/attend_64/pallas_call | solution.py:143
  35.8 135.5 %comm_1.1 = (bf16[4,64,640]{2,1,0:T(8,128)(2,1)}, f32[64,2048]{1,0:T(8,128)}) custom-call(bf16[64,1024]{1,0:T(8,128)(2,1)} %get-tuple-element.13.refs_0_, bf16[2,4,2560]{2,1,0:T(4,128)(2,1)} %refs_1_.5, bf16[64,2560]{1,0:T(8,128)(2,1)} %bitcast.50, bf16[2,1024,640]{2,1,0:T(8,128)(2,1)} %bitcast.45, bf16[2,640,5120]{2,1,0:T(8,128)(2,1)} %refs_4_.5, ...), custom_call_target="tpu_custom_call" | custom-call | tf_op jit(solution)/shard_map/comm_1/pallas_call | solution.py:593
  171.2 44.7 %attend_512.1 = (bf16[64,1024]{1,0:T(8,128)(2,1)}, bf16[64,2048,128]{2,1,0:T(8,128)(2,1)}, bf16[64,2048,128]{2,1,0:T(8,128)(2,1)}) custom-call(s32[64]{0:T(128)} %pos_ref.3, f32[64,2048]{1,0:T(8,128)} %get-tuple-element.14.qkv_ref, f32[64,128]{1,0:T(8,128)} %get-tuple-element.22.cos_ref, f32[64,128]{1,0:T(8,128)} %get-tuple-element.21.sin_ref, ...), custom_call_target="tpu_custom_call" | custom-call | flops 536870912 | bytes 134217728 | tf_op jit(solution)/shard_map/attend_512/pallas_call | solution.py:143
  216.0 118.8 %comm_2.1 = bf16[64,2560]{1,0:T(8,128)(2,1)} custom-call(bf16[64,1024]{1,0:T(8,128)(2,1)} %get-tuple-element.15.refs_0_, bf16[2,4,2560]{2,1,0:T(4,128)(2,1)} %refs_1_.5, bf16[4,64,640]{2,1,0:T(8,128)(2,1)} %get-tuple-element.16.refs_2_, bf16[2,1024,640]{2,1,0:T(8,128)(2,1)} %bitcast.46, bf16[2,640,5120]{2,1,0:T(8,128)(2,1)} %refs_4_.5, ...), custom_call_target="tpu_custom_call" | custom-call | tf_op jit(solution)/shard_map/comm_2/pallas_call | solution.py:593
  334.8 1.7 copy.28
  (1 shorter events, 0.0 us)

commit v9 on v8

--- a/solution.py
+++ b/solution.py
@@ -30,7 +30,7 @@
 LANES = 128
 
 
-def attend_kernel(cache_len, n_rows, group, depth, pos_ref, qkv_ref, cos_ref, sin_ref, k_hbm, v_hbm, head_ref, ko_hbm, vo_hbm, kbuf, vbuf, q8, kn, vn, outs, sbuf, pbuf, rd_sem, wr_sem):
+def attend_kernel(cache_len, n_rows, group, depth, pos_ref, qkv_hbm, cos_hbm, sin_hbm, k_hbm, v_hbm, head_hbm, ko_hbm, vo_hbm, qkv_ref, cos_ref, sin_ref, head_ref, kbuf, vbuf, q8, kn, vn, outs, sbuf, pbuf, io_sem, rd_sem, wr_sem):
     n_steps = n_rows // group
     n_cols = cache_len * 4
 
@@ -46,10 +46,15 @@
         return (pltpu.make_async_copy(kbuf.at[slot], ko_hbm.at[rows], wr_sem.at[0, slot]),
                 pltpu.make_async_copy(vbuf.at[slot], vo_hbm.at[rows], wr_sem.at[1, slot]))
 
+    loads = [pltpu.make_async_copy(src, dst, io_sem.at[k]) for k, (src, dst) in enumerate(((qkv_hbm, qkv_ref), (cos_hbm, cos_ref), (sin_hbm, sin_ref)))]
+    for copy in loads:
+        copy.start()
     ahead = depth // 2 if depth < n_steps else n_steps
     for step in range(ahead):
         for copy in reads(step):
             copy.start()
+    for copy in loads:
+        copy.wait()
 
     cos_t, sin_t = cos_ref[...], sin_ref[...]
     scale = (2 * LANES) ** -0.5
@@ -117,9 +122,12 @@
     for h in range(4):
         for half in range(2):
             head_ref[:, h * 256 + half * LANES:h * 256 + (half + 1) * LANES] = outs[:, half * 4 + h, :].astype(jnp.bfloat16)
+    heads_out = pltpu.make_async_copy(head_ref, head_hbm, io_sem.at[3])
+    heads_out.start()
     for step in range(max(n_steps - depth, 0) if ahead < n_steps else 0, n_steps):
         for copy in writes(step):
             copy.wait()
+    heads_out.wait()
 
 
 def attend(qkv, tables, positions, k_cache, v_cache):
@@ -135,7 +143,7 @@
     def unflat(cache):
         return cache.reshape(n_rows, cache_len, halves, kv_loc, LANES).transpose(0, 1, 3, 2, 4).reshape(n_rows, cache_len, kv_loc, head_dim)
 
-    vmem, hbm = pl.BlockSpec(memory_space=pltpu.VMEM), pl.BlockSpec(memory_space=pl.ANY)
+    hbm = pl.BlockSpec(memory_space=pl.ANY)
     k_flat, v_flat = flat(k_cache), flat(v_cache)
     n_cols = k_flat.shape[1]
     block = (depth, group, n_cols, LANES)
@@ -143,11 +151,12 @@
     heads, k_out, v_out = pl.pallas_call(
         functools.partial(attend_kernel, cache_len, n_rows, group, depth),
         out_shape=(jax.ShapeDtypeStruct((n_rows, 4 * head_dim), bf16), jax.ShapeDtypeStruct(k_flat.shape, bf16), jax.ShapeDtypeStruct(v_flat.shape, bf16)),
-        in_specs=[pl.BlockSpec(memory_space=pltpu.SMEM), vmem, vmem, vmem, hbm, hbm],
-        out_specs=(vmem, hbm, hbm),
-        scratch_shapes=[pltpu.VMEM(block, bf16), pltpu.VMEM(block, bf16), pltpu.VMEM((n_rows, 8, LANES), f32), pltpu.VMEM((n_rows, 16, LANES), f32),
+        in_specs=[pl.BlockSpec(memory_space=pltpu.SMEM), hbm, hbm, hbm, hbm, hbm],
+        out_specs=(hbm, hbm, hbm),
+        scratch_shapes=[pltpu.VMEM(qkv.shape, f32), pltpu.VMEM(tables[0].shape, f32), pltpu.VMEM(tables[0].shape, f32), pltpu.VMEM((n_rows, 4 * head_dim), bf16),
+                        pltpu.VMEM(block, bf16), pltpu.VMEM(block, bf16), pltpu.VMEM((n_rows, 8, LANES), f32), pltpu.VMEM((n_rows, 16, LANES), f32),
                         pltpu.VMEM((n_rows, 16, LANES), f32), pltpu.VMEM((n_rows, 8, LANES), f32), pltpu.VMEM((group, 8, n_cols), f32), pltpu.VMEM((group, 8, n_cols), bf16),
-                        dma((2, depth)), dma((2, depth))],
+                        dma((4,)), dma((2, depth)), dma((2, depth))],
         compiler_params=pltpu.CompilerParams(vmem_limit_bytes=62 * 2**20),
         cost_estimate=pl.CostEstimate(flops=n_rows * 8 * n_cols * LANES * 4, bytes_accessed=4 * k_flat.size * 2, transcendentals=0),
         name=f"attend_{cache_len}",
@@ -334,36 +343,43 @@
             start_qkv(h)
         end_qkv()
     else:
-        to_part = send(x_ref, hall.at[2], misc_ss.at[0], misc_rs.at[0], part)
-        to_sib = send(x_ref, hall.at[1], misc_ss.at[1], misc_rs.at[1], sib)
+        head_cuts = (pl.ds(0, rows), pl.ds(rows, (GROUPS - 1) * rows))
+        to_part = [send(x_ref.at[cut], hall.at[2, cut], misc_ss.at[n], misc_rs.at[n], part) for n, cut in enumerate(head_cuts)]
+        to_sib = send(x_ref, hall.at[1], misc_ss.at[2], misc_rs.at[2], sib)
         if raw:
-            raw_copies = spread(raw_ref, res_ref, 3)
+            raw_copies = spread(raw_ref, res_ref, 5)
             for h in range(GROUPS):
                 res_ref[h, OWN, :] = raw_ref[mine_rows[h], my_cols]
         wo_load.wait()
         y_copies = [[None] * 4 for _ in range(GROUPS)]
 
-        def project(k, heads):
+        def project(heads, places):
             sums = jnp.dot(heads, wo[...], preferred_element_type=jnp.float32)
-            for h in range(GROUPS):
-                apart[h, blocks[k], :] = sums[h * rows:(h + 1) * rows]
+            for n, (h, k) in enumerate(places):
+                apart[h, blocks[k], :] = sums[n * rows:(n + 1) * rows]
 
         def to_model(*pairs):
             for h, k in pairs:
                 y_copies[h][k] = send(apart.at[h, blocks[k], :], arecv.at[h, blocks[k], :], y_ss.at[h * 4 + k], y_rs.at[h * 4 + k])
 
-        project(0, x_ref[...])
+        def forward(n):
+            to_part[n].wait_recv()
+            return send(hall.at[2, head_cuts[n]], hall.at[0, head_cuts[n]], misc_ss.at[3 + n], misc_rs.at[3 + n], sib)
+
+        project(x_ref[...], [(h, 0) for h in range(GROUPS)])
         to_model((0, 0), (1, 0))
         to_sib.wait_recv()
-        project(1, hall[1])
-        to_model((0, 1), (1, 1), (2, 0))
-        to_part.wait_recv()
-        forward = send(hall.at[2], hall.at[0], misc_ss.at[2], misc_rs.at[2], sib)
-        project(2, hall[2])
-        to_model((0, 2))
-        forward.wait_recv()
-        project(3, hall[0])
-        to_model((0, 3), (1, 2), (1, 3), (2, 1), (2, 2), (2, 3), (3, 0), (3, 1), (3, 2), (3, 3))
+        project(hall[1], [(h, 1) for h in range(GROUPS)])
+        to_model((0, 1), (1, 1))
+        forward(0).wait_recv()
+        project(jnp.concatenate([hall[2, head_cuts[0], :], hall[0, head_cuts[0], :]], axis=0), [(0, 2), (0, 3)])
+        to_model((0, 2), (0, 3), (2, 0), (2, 1))
+        rest = forward(1)
+        project(hall[2, head_cuts[1], :], [(h, 2) for h in range(1, GROUPS)])
+        to_model((1, 2))
+        rest.wait_recv()
+        project(hall[0, head_cuts[1], :], [(h, 3) for h in range(1, GROUPS)])
+        to_model((1, 3), (2, 2), (2, 3), (3, 0), (3, 1), (3, 2), (3, 3))
         stats = {}
 
         def attn_sums(h):
@@ -433,7 +449,11 @@
                     add_sibling(s - 1)
 
         attn_sums(0)
+        if qkv:
+            relay_weights(0)
         attn_residual(0)
+        if qkv:
+            relay_weights(1)
         attn_sums(1)
         attn_normed(0)
         wg_load.wait()
@@ -451,10 +471,6 @@
             else:
                 gate_up(h, 0, n_ff)
         add_sibling(GROUPS * n_ff - 1)
-        if qkv:
-            relay_weights(0)
-            relay_weights(1)
-
         @pl.loop(0, GROUPS * n_ff)
         def _(s):
             to_partner(s).wait_recv()
@@ -510,7 +526,7 @@
                 stats[h] = start_scales(h, 3)
             else:
                 for k, (dev, block) in enumerate(((sib, SIB), (part, PART), (diag, DIAG))):
-                    i = 3 + h * 3 + k
+                    i = 5 + h * 3 + k
                     out_copies.append(send(hp.at[h, block, :], out_ref.at[mine_rows[h], my_cols], misc_ss.at[i], misc_rs.at[i], dev))
                 out_ref[mine_rows[h], my_cols] = hp[h, OWN, :]
 
@@ -559,7 +575,7 @@
     args, specs = [x, gains], [hbm, hbm]
     raw = post is not None and post[0].ndim == 2
     n_stat = 4 * GROUPS
-    n_misc = 3 + 3 * GROUPS
+    n_misc = 5 + 3 * GROUPS
     scratch = [pltpu.VMEM(x.shape, bf16), pltpu.VMEM(gains.shape, bf16), pltpu.VMEM((GROUPS, LANES, LANES), f32), pltpu.VMEM((n_stat, 8, LANES), f32), pltpu.VMEM((n_stat, 3, 8, LANES), f32), pltpu.VMEM((GROUPS, n_group, share), bf16),
                dma((n_stat, 3)), dma((n_stat, 3)), dma((n_misc,)), dma((n_misc,)), dma((10,))]
     if post is None:

time: 337 us -> 333 us (0.988)
  Pallas kernels: 333 us -> 329 us
    pallas_call x3, Pallas kernels: 280 us -> 275 us  [comm(): pl.pallas_call(functools.partial(comm_kernel, cfg), out_shape=out_shape,...]
where the time goes in v9:
time: 333 us
  Pallas kernels  329 us (99%)
    pallas_call x3, Pallas kernels, comm(): pl.pallas_call(functools.partial(comm_kernel, cfg), out_shape=out_shape,...  275 us
    pallas_call x2, Pallas kernels, attend(): pl.pallas_call(functools.partial(attend_kernel, cache_len, n_rows, group,...  54.4 us

profile of v9, /device:TPU:0, one launch (start us, length us, event | category | flops | bytes accessed | tf_op | source)
XLA Modules:
  0.0 332.9 jit_solution(4483977824399581412)
XLA Ops:
  0.6 0.7 convert_element_type.10
  1.3 0.8 multiply_sine_fusion
  2.1 25.5 %comm_0.1.qkv_hbm = f32[64,2048]{1,0:T(8,128)} custom-call(bf16[64,2560]{1,0:T(8,128)(2,1)} %bitcast.49, bf16[2,4,2560]{2,1,0:T(4,128)(2,1)} %refs_1_.5, bf16[2,640,4,256]{3,2,1,0:T(4,128)(2,1)} %refs_7_.1, bf16[2,640,2,256]{3,2,1,0:T(2,128)(2,1)} %refs_8_.1, bf16[2,640,2,256]{3,2,1,0:T(2,128)(2,1)} %refs_9_.1), custom_call_target="tpu_custom_call" | custom-call | tf_op jit(solution)/shard_map/comm_0/pallas_call | solution.py:609
  27.6 9.4 %attend_64.1 = (bf16[64,1024]{1,0:T(8,128)(2,1)}, bf16[64,256,128]{2,1,0:T(8,128)(2,1)}, bf16[64,256,128]{2,1,0:T(8,128)(2,1)}) custom-call(s32[64]{0:T(128)} %pos_ref.3, f32[64,2048]{1,0:T(8,128)} %comm_0.1.qkv_hbm, f32[64,128]{1,0:T(8,128)} %get-tuple-element.22.cos_hbm, f32[64,128]{1,0:T(8,128)} %get-tuple-element.21.sin_hbm, ...), custom_call_target="tpu_custom_call" | custom-call | flops 67108864 | bytes 16777216 | tf_op jit(solution)/shard_map/attend_64/pallas_call | solution.py:151
  37.0 131.2 %comm_1.1 = (bf16[4,64,640]{2,1,0:T(8,128)(2,1)}, f32[64,2048]{1,0:T(8,128)}) custom-call(bf16[64,1024]{1,0:T(8,128)(2,1)} %get-tuple-element.13.refs_0_, bf16[2,4,2560]{2,1,0:T(4,128)(2,1)} %refs_1_.5, bf16[64,2560]{1,0:T(8,128)(2,1)} %bitcast.50, bf16[2,1024,640]{2,1,0:T(8,128)(2,1)} %bitcast.45, bf16[2,640,5120]{2,1,0:T(8,128)(2,1)} %refs_4_.5, ...), custom_call_target="tpu_custom_call" | custom-call | tf_op jit(solution)/shard_map/comm_1/pallas_call | solution.py:609
  168.2 45.0 %attend_512.1 = (bf16[64,1024]{1,0:T(8,128)(2,1)}, bf16[64,2048,128]{2,1,0:T(8,128)(2,1)}, bf16[64,2048,128]{2,1,0:T(8,128)(2,1)}) custom-call(s32[64]{0:T(128)} %pos_ref.3, f32[64,2048]{1,0:T(8,128)} %get-tuple-element.14.qkv_hbm, f32[64,128]{1,0:T(8,128)} %get-tuple-element.22.cos_hbm, f32[64,128]{1,0:T(8,128)} %get-tuple-element.21.sin_hbm, ...), custom_call_target="tpu_custom_call" | custom-call | flops 536870912 | bytes 134217728 | tf_op jit(solution)/shard_map/attend_512/pallas_call | solution.py:151
  213.2 118.0 %comm_2.1 = bf16[64,2560]{1,0:T(8,128)(2,1)} custom-call(bf16[64,1024]{1,0:T(8,128)(2,1)} %get-tuple-element.15.refs_0_, bf16[2,4,2560]{2,1,0:T(4,128)(2,1)} %refs_1_.5, bf16[4,64,640]{2,1,0:T(8,128)(2,1)} %get-tuple-element.16.refs_2_, bf16[2,1024,640]{2,1,0:T(8,128)(2,1)} %bitcast.46, bf16[2,640,5120]{2,1,0:T(8,128)(2,1)} %refs_4_.5, ...), custom_call_target="tpu_custom_call" | custom-call | tf_op jit(solution)/shard_map/comm_2/pallas_call | solution.py:609
  331.2 1.7 copy.28
  (1 shorter events, 0.0 us)

commit v10 on v9

--- a/solution.py
+++ b/solution.py
@@ -30,7 +30,7 @@
 LANES = 128
 
 
-def attend_kernel(cache_len, n_rows, group, depth, pos_ref, qkv_hbm, cos_hbm, sin_hbm, k_hbm, v_hbm, head_hbm, ko_hbm, vo_hbm, qkv_ref, cos_ref, sin_ref, head_ref, kbuf, vbuf, q8, kn, vn, outs, sbuf, pbuf, io_sem, rd_sem, wr_sem):
+def attend_kernel(cache_len, n_rows, group, depth, pos_ref, qkv_ref, cos_ref, sin_ref, k_hbm, v_hbm, head_ref, ko_hbm, vo_hbm, kbuf, vbuf, q8, kn, vn, outs, sbuf, pbuf, rd_sem, wr_sem):
     n_steps = n_rows // group
     n_cols = cache_len * 4
 
@@ -46,15 +46,10 @@
         return (pltpu.make_async_copy(kbuf.at[slot], ko_hbm.at[rows], wr_sem.at[0, slot]),
                 pltpu.make_async_copy(vbuf.at[slot], vo_hbm.at[rows], wr_sem.at[1, slot]))
 
-    loads = [pltpu.make_async_copy(src, dst, io_sem.at[k]) for k, (src, dst) in enumerate(((qkv_hbm, qkv_ref), (cos_hbm, cos_ref), (sin_hbm, sin_ref)))]
-    for copy in loads:
-        copy.start()
     ahead = depth // 2 if depth < n_steps else n_steps
     for step in range(ahead):
         for copy in reads(step):
             copy.start()
-    for copy in loads:
-        copy.wait()
 
     cos_t, sin_t = cos_ref[...], sin_ref[...]
     scale = (2 * LANES) ** -0.5
@@ -122,12 +117,9 @@
     for h in range(4):
         for half in range(2):
             head_ref[:, h * 256 + half * LANES:h * 256 + (half + 1) * LANES] = outs[:, half * 4 + h, :].astype(jnp.bfloat16)
-    heads_out = pltpu.make_async_copy(head_ref, head_hbm, io_sem.at[3])
-    heads_out.start()
     for step in range(max(n_steps - depth, 0) if ahead < n_steps else 0, n_steps):
         for copy in writes(step):
             copy.wait()
-    heads_out.wait()
 
 
 def attend(qkv, tables, positions, k_cache, v_cache):
@@ -143,7 +135,7 @@
     def unflat(cache):
         return cache.reshape(n_rows, cache_len, halves, kv_loc, LANES).transpose(0, 1, 3, 2, 4).reshape(n_rows, cache_len, kv_loc, head_dim)
 
-    hbm = pl.BlockSpec(memory_space=pl.ANY)
+    vmem, hbm = pl.BlockSpec(memory_space=pltpu.VMEM), pl.BlockSpec(memory_space=pltpu.HBM)
     k_flat, v_flat = flat(k_cache), flat(v_cache)
     n_cols = k_flat.shape[1]
     block = (depth, group, n_cols, LANES)
@@ -151,13 +143,12 @@
     heads, k_out, v_out = pl.pallas_call(
         functools.partial(attend_kernel, cache_len, n_rows, group, depth),
         out_shape=(jax.ShapeDtypeStruct((n_rows, 4 * head_dim), bf16), jax.ShapeDtypeStruct(k_flat.shape, bf16), jax.ShapeDtypeStruct(v_flat.shape, bf16)),
-        in_specs=[pl.BlockSpec(memory_space=pltpu.SMEM), hbm, hbm, hbm, hbm, hbm],
-        out_specs=(hbm, hbm, hbm),
-        scratch_shapes=[pltpu.VMEM(qkv.shape, f32), pltpu.VMEM(tables[0].shape, f32), pltpu.VMEM(tables[0].shape, f32), pltpu.VMEM((n_rows, 4 * head_dim), bf16),
-                        pltpu.VMEM(block, bf16), pltpu.VMEM(block, bf16), pltpu.VMEM((n_rows, 8, LANES), f32), pltpu.VMEM((n_rows, 16, LANES), f32),
+        in_specs=[pl.BlockSpec(memory_space=pltpu.SMEM), vmem, vmem, vmem, hbm, hbm],
+        out_specs=(vmem, hbm, hbm),
+        scratch_shapes=[pltpu.VMEM(block, bf16), pltpu.VMEM(block, bf16), pltpu.VMEM((n_rows, 8, LANES), f32), pltpu.VMEM((n_rows, 16, LANES), f32),
                         pltpu.VMEM((n_rows, 16, LANES), f32), pltpu.VMEM((n_rows, 8, LANES), f32), pltpu.VMEM((group, 8, n_cols), f32), pltpu.VMEM((group, 8, n_cols), bf16),
-                        dma((4,)), dma((2, depth)), dma((2, depth))],
-        compiler_params=pltpu.CompilerParams(vmem_limit_bytes=62 * 2**20),
+                        dma((2, depth)), dma((2, depth))],
+        compiler_params=pltpu.CompilerParams(vmem_limit_bytes=int((62 if cache_len <= 64 else 34) * 2**20)),
         cost_estimate=pl.CostEstimate(flops=n_rows * 8 * n_cols * LANES * 4, bytes_accessed=4 * k_flat.size * 2, transcendentals=0),
         name=f"attend_{cache_len}",
     )(positions, qkv, *tables, k_flat, v_flat)
@@ -178,9 +169,9 @@
     post, layer, rows, share, width = cfg["post"], cfg["layer"], cfg["rows"], cfg["share"], cfg["width"]
     qkv, n_ff, n_q = cfg["qkv"], cfg["n_ff"], cfg["n_q"]
     raw = cfg["raw"]
-    x_hbm, g_hbm = next(it), next(it)
+    x_any, g_hbm = next(it), next(it)
     if post:
-        res_hbm, wo_hbm, wg_hbm, wu_hbm, wd_hbm = (next(it) for _ in range(5))
+        res_any, wo_any, wg_hbm, wu_hbm, wd_hbm = (next(it) for _ in range(5))
     if qkv:
         wq_hbm, wk_hbm, wv_hbm = (next(it) for _ in range(3))
         if post:
@@ -188,13 +179,15 @@
         qkv_ref = next(it)
     else:
         out_ref = next(it)
-    x_ref, g_ref, tcol, st_src, st_rcv, hp, st_ss, st_rs, misc_ss, misc_rs, ld_sem = (next(it) for _ in range(11))
+    if not post:
+        x_ref = next(it)
+    g_ref, tcol, st_src, st_rcv, hp, st_ss, st_rs, misc_ss, misc_rs, ld_sem = (next(it) for _ in range(10))
     if not post:
         out_rows = next(it)
     if post:
         if raw:
-            raw_ref = next(it)
-        res_ref, hall, apart, arecv, mpart, mrecv, wo, wg, wu, wd, sib_out, sib_in, mine, x_in, u_all = (next(it) for _ in range(15))
+            raw_ref, res_ref, wo = (next(it) for _ in range(3))
+        hall, apart, arecv, mpart, mrecv, wg, wu, wd, sib_out, sib_in, mine, x_in, u_all = (next(it) for _ in range(13))
         y_ss, y_rs, ff_ss, ff_rs = (next(it) for _ in range(4))
     if qkv:
         wi, wq, wk, wv, q_out, q_in, q_mine, q_x, q_ss, q_rs = (next(it) for _ in range(10))
@@ -223,10 +216,20 @@
         copy.start()
         return copy
 
-    early = [load(x_hbm, x_ref, ld_sem.at[7]), load(g_hbm, g_ref, ld_sem.at[8])]
+    early = [load(g_hbm, g_ref, ld_sem.at[8])]
     if post:
-        early.append(load(res_hbm, raw_ref if raw else res_ref, ld_sem.at[9]))
-        wo_load = load(wo_hbm.at[layer], wo, ld_sem.at[0])
+        x_ref = x_any
+    else:
+        early.append(load(x_any, x_ref, ld_sem.at[7]))
+    if post:
+        if raw:
+            early.append(load(res_any, raw_ref, ld_sem.at[9]))
+        else:
+            res_ref = res_any
+        if raw:
+            wo_load = load(wo_any.at[layer], wo, ld_sem.at[0])
+        else:
+            wo = wo_any.at[layer]
         wg_load = load(wg_hbm.at[layer], wg, ld_sem.at[1])
         wu_load = load(wu_hbm.at[layer], wu, ld_sem.at[2])
         wd_load = load(wd_hbm.at[layer], wd, ld_sem.at[3])
@@ -350,7 +353,8 @@
             raw_copies = spread(raw_ref, res_ref, 5)
             for h in range(GROUPS):
                 res_ref[h, OWN, :] = raw_ref[mine_rows[h], my_cols]
-        wo_load.wait()
+        if raw:
+            wo_load.wait()
         y_copies = [[None] * 4 for _ in range(GROUPS)]
 
         def project(heads, places):
@@ -570,13 +574,14 @@
     rows = x.shape[0] // GROUPS
     share = gains.shape[2] // 4
     n_group = rows * 4
-    f32, bf16, vmem, hbm = jnp.float32, jnp.bfloat16, pl.BlockSpec(memory_space=pltpu.VMEM), pl.BlockSpec(memory_space=pl.ANY)
+    f32, bf16, vmem, hbm = jnp.float32, jnp.bfloat16, pl.BlockSpec(memory_space=pltpu.VMEM), pl.BlockSpec(memory_space=pltpu.HBM)
     dma = pltpu.SemaphoreType.DMA
-    args, specs = [x, gains], [hbm, hbm]
+    args, specs = [x, gains], [hbm if post is None else vmem, hbm]
     raw = post is not None and post[0].ndim == 2
     n_stat = 4 * GROUPS
     n_misc = 5 + 3 * GROUPS
-    scratch = [pltpu.VMEM(x.shape, bf16), pltpu.VMEM(gains.shape, bf16), pltpu.VMEM((GROUPS, LANES, LANES), f32), pltpu.VMEM((n_stat, 8, LANES), f32), pltpu.VMEM((n_stat, 3, 8, LANES), f32), pltpu.VMEM((GROUPS, n_group, share), bf16),
+    scratch = [pltpu.VMEM(x.shape, bf16)] if post is None else []
+    scratch += [pltpu.VMEM(gains.shape, bf16), pltpu.VMEM((GROUPS, LANES, LANES), f32), pltpu.VMEM((n_stat, 8, LANES), f32), pltpu.VMEM((n_stat, 3, 8, LANES), f32), pltpu.VMEM((GROUPS, n_group, share), bf16),
                dma((n_stat, 3)), dma((n_stat, 3)), dma((n_misc,)), dma((n_misc,)), dma((10,))]
     if post is None:
         scratch.append(pltpu.VMEM(x.shape, bf16))
@@ -584,13 +589,13 @@
     if post is not None:
         residual, w_o, w_gate, w_up, w_down = post
         args += list(post)
-        specs += [hbm] * 5
+        specs += [hbm if raw else vmem] * 2 + [hbm] * 3
         ff = w_gate.shape[2]
         n_ff = ff // FF_CHUNK
         steps = GROUPS * n_ff
-        scratch += [pltpu.VMEM(residual.shape, bf16)] if raw else []
-        scratch += [pltpu.VMEM((GROUPS, n_group, share), bf16), pltpu.VMEM((3, GROUPS * rows, w_o.shape[1]), bf16)] + [pltpu.VMEM((GROUPS, n_group, share), f32)] * 4
-        scratch += [pltpu.VMEM(w_o.shape[1:], bf16), pltpu.VMEM((share, ff), bf16), pltpu.VMEM((share, ff), bf16), pltpu.VMEM((ff, share), bf16)]
+        scratch += [pltpu.VMEM(residual.shape, bf16), pltpu.VMEM((GROUPS, n_group, share), bf16), pltpu.VMEM(w_o.shape[1:], bf16)] if raw else []
+        scratch += [pltpu.VMEM((3, GROUPS * rows, w_o.shape[1]), bf16)] + [pltpu.VMEM((GROUPS, n_group, share), f32)] * 4
+        scratch += [pltpu.VMEM((share, ff), bf16), pltpu.VMEM((share, ff), bf16), pltpu.VMEM((ff, share), bf16)]
         scratch += [pltpu.VMEM((steps, 2 * rows, 2 * FF_CHUNK), f32)] * 3 + [pltpu.VMEM((steps, rows, 2 * FF_CHUNK), f32), pltpu.VMEM((steps, n_group, FF_CHUNK), bf16)]
         scratch += [dma((5 * GROUPS,)), dma((5 * GROUPS,)), dma((5, steps)), dma((5, steps))]
     if in_weights is not None:
@@ -609,7 +614,7 @@
     return pl.pallas_call(
         functools.partial(comm_kernel, cfg),
         out_shape=out_shape, in_specs=specs, out_specs=out_specs, scratch_shapes=scratch,
-        compiler_params=pltpu.CompilerParams(collective_id=collective_id, has_side_effects=True, vmem_limit_bytes=62 * 2**20),
+        compiler_params=pltpu.CompilerParams(collective_id=collective_id, has_side_effects=True, vmem_limit_bytes=int((62, 62, 49)[collective_id] * 2**20)),
         name=f"comm_{collective_id}",
     )(*args)
 

time: 333 us -> 331 us (level)
  no operation moved by 1% of the time
where the time goes in v10:
time: 331 us
  Pallas kernels  327 us (99%)
    pallas_call x3, Pallas kernels, comm(): pl.pallas_call(functools.partial(comm_kernel, cfg), out_shape=out_shape,...  275 us
    pallas_call x2, Pallas kernels, attend(): pl.pallas_call(functools.partial(attend_kernel, cache_len, n_rows, group,...  52.1 us

profile of v10, /device:TPU:0, one launch (start us, length us, event | category | flops | bytes accessed | tf_op | source)
XLA Modules:
  0.0 330.9 jit_solution(13288635803274947146)
XLA Ops:
  0.6 0.7 convert_element_type.10
  1.3 0.8 multiply_sine_fusion
  2.1 25.5 %comm_0.1.qkv_ref = f32[64,2048]{1,0:T(8,128)} custom-call(bf16[64,2560]{1,0:T(8,128)(2,1)} %bitcast.50, bf16[2,4,2560]{2,1,0:T(4,128)(2,1)} %refs_1_.5, bf16[2,640,4,256]{3,2,1,0:T(4,128)(2,1)} %refs_7_.1, bf16[2,640,2,256]{3,2,1,0:T(2,128)(2,1)} %refs_8_.1, bf16[2,640,2,256]{3,2,1,0:T(2,128)(2,1)} %refs_9_.1), custom_call_target="tpu_custom_call" | custom-call | tf_op jit(solution)/shard_map/comm_0/pallas_call | solution.py:614
  27.6 8.2 %attend_64.1 = (bf16[64,1024]{1,0:T(8,128)(2,1)}, bf16[64,256,128]{2,1,0:T(8,128)(2,1)}, bf16[64,256,128]{2,1,0:T(8,128)(2,1)}) custom-call(s32[64]{0:T(128)} %pos_ref.3, f32[64,2048]{1,0:T(8,128)} %comm_0.1.qkv_ref, f32[64,128]{1,0:T(8,128)} %get-tuple-element.22.cos_ref, f32[64,128]{1,0:T(8,128)} %get-tuple-element.21.sin_ref, ...), custom_call_target="tpu_custom_call" | custom-call | flops 67108864 | bytes 16777216 | tf_op jit(solution)/shard_map/attend_64/pallas_call | solution.py:143
  35.8 0.0 copy-start.4
  35.8 0.0 copy-start.5
  35.8 0.0 copy-start.6
  35.8 132.1 %comm_1.1 = (bf16[4,64,640]{2,1,0:T(8,128)(2,1)}, f32[64,2048]{1,0:T(8,128)}) custom-call(bf16[64,1024]{1,0:T(8,128)(2,1)} %get-tuple-element.13.refs_0_, bf16[2,4,2560]{2,1,0:T(4,128)(2,1)} %refs_1_.5, bf16[64,2560]{1,0:T(8,128)(2,1)} %bitcast.51, bf16[2,1024,640]{2,1,0:T(8,128)(2,1)} %bitcast.43, bf16[2,640,5120]{2,1,0:T(8,128)(2,1)} %refs_4_.5, ...), custom_call_target="tpu_custom_call" | custom-call | tf_op jit(solution)/shard_map/comm_1/pallas_call | solution.py:614
  167.9 0.0 copy-done.4
  167.9 0.0 copy-done.5
  167.9 0.0 copy-done.6
  167.9 0.0 copy-start.1
  167.9 1.0 copy-done.1
  169.0 0.0 copy-start
  169.0 0.0 copy-start.2
  169.0 0.0 copy-start.3
  169.0 43.9 %attend_512.1 = (bf16[64,1024]{1,0:T(8,128)(2,1)S(1)}, bf16[64,2048,128]{2,1,0:T(8,128)(2,1)}, bf16[64,2048,128]{2,1,0:T(8,128)(2,1)}) custom-call(s32[64]{0:T(128)S(1)} %copy-done.6, f32[64,2048]{1,0:T(8,128)S(1)} %copy-done.1, f32[64,128]{1,0:T(8,128)S(1)} %copy-done.5, f32[64,128]{1,0:T(8,128)S(1)} %copy-done.4, bf16[64,2048,128]{2,1,0:T(8,128)(2,1)} %bitcast.46, ...), custom_call_target="tpu_custom_call" | custom-call | flops 536870912 | bytes 134217728 | tf_op jit(solution)/shard_map/attend_512/pallas_call | solution.py:143
  212.9 0.0 copy-done
  212.9 0.0 copy-done.2
  212.9 0.0 copy-done.3
  212.9 117.3 %comm_2.1 = bf16[64,2560]{1,0:T(8,128)(2,1)S(1)} custom-call(bf16[64,1024]{1,0:T(8,128)(2,1)S(1)} %get-tuple-element.15.refs_0_, bf16[2,4,2560]{2,1,0:T(4,128)(2,1)S(1)} %copy-done.2, bf16[4,64,640]{2,1,0:T(8,128)(2,1)S(1)} %copy-done.3, bf16[2,1024,640]{2,1,0:T(8,128)(2,1)S(1)} %bitcast.44, bf16[2,640,5120]{2,1,0:T(8,128)(2,1)} %refs_4_.5, ...), custom_call_target="tpu_custom_call" | custom-call | tf_op jit(solution)/shard_map/comm_2/pallas_call | solution.py:614
  330.2 0.7 copy.28
  (1 shorter events, 0.0 us)
Async XLA Ops:
  35.8 132.1 %copy-start.4 = (f32[64,128]{1,0:T(8,128)S(1)}, f32[64,128]{1,0:T(8,128)}, u32[]{:S(2)}) copy-start(f32[64,128]{1,0:T(8,128)} %get-tuple-element.21.sin_ref) | copy-start | bytes 98308
  35.8 132.1 %copy-start.5 = (f32[64,128]{1,0:T(8,128)S(1)}, f32[64,128]{1,0:T(8,128)}, u32[]{:S(2)}) copy-start(f32[64,128]{1,0:T(8,128)} %get-tuple-element.22.cos_ref) | copy-start | bytes 98308
  35.8 132.1 %copy-start.6 = (s32[64]{0:T(128)S(1)}, s32[64]{0:T(128)}, u32[]{:S(2)}) copy-start(s32[64]{0:T(128)} %pos_ref.3) | copy-start | bytes 772
  167.9 1.0 copy-start.1
  169.0 43.9 %copy-start = (bf16[2,4,256,640]{3,2,1,0:T(8,128)(2,1)S(1)}, bf16[2,4,256,640]{3,2,1,0:T(8,128)(2,1)}, u32[]{:S(2)}) copy-start(bf16[2,4,256,640]{3,2,1,0:T(8,128)(2,1)} %param.23) | copy-start | bytes 7864324
  169.0 43.9 %copy-start.2 = (bf16[2,4,2560]{2,1,0:T(4,128)(2,1)S(1)}, bf16[2,4,2560]{2,1,0:T(4,128)(2,1)}, u32[]{:S(2)}) copy-start(bf16[2,4,2560]{2,1,0:T(4,128)(2,1)} %refs_1_.5) | copy-start | bytes 122884
  169.0 43.9 %copy-start.3 = (bf16[4,64,640]{2,1,0:T(8,128)(2,1)S(1)}, bf16[4,64,640]{2,1,0:T(8,128)(2,1)}, u32[]{:S(2)}) copy-start(bf16[4,64,640]{2,1,0:T(8,128)(2,1)} %get-tuple-element.16.refs_2_) | copy-start | bytes 983044

commit v11 on v10

--- a/solution.py
+++ b/solution.py
@@ -125,8 +125,8 @@
 def attend(qkv, tables, positions, k_cache, v_cache):
     n_rows, cache_len, kv_loc, head_dim = k_cache.shape
     halves = head_dim // LANES
-    group = 16 if cache_len <= 64 else 4
-    depth = 4 if cache_len <= 64 else 6
+    group = 8 if cache_len <= 64 else 4
+    depth = 8 if cache_len <= 64 else 6
     f32, bf16 = jnp.float32, jnp.bfloat16
 
     def flat(cache):
@@ -156,7 +156,7 @@
 
 
 FF_CHUNK = 512
-IN_FLIGHT = 2
+IN_FLIGHT = 4
 QKV_CHUNK = 1024
 MESH = pl.DeviceIdType.MESH
 
@@ -179,7 +179,7 @@
         qkv_ref = next(it)
     else:
         out_ref = next(it)
-    if not post:
+    if raw or not post:
         x_ref = next(it)
     g_ref, tcol, st_src, st_rcv, hp, st_ss, st_rs, misc_ss, misc_rs, ld_sem = (next(it) for _ in range(10))
     if not post:
@@ -217,7 +217,7 @@
         return copy
 
     early = [load(g_hbm, g_ref, ld_sem.at[8])]
-    if post:
+    if post and not raw:
         x_ref = x_any
     else:
         early.append(load(x_any, x_ref, ld_sem.at[7]))
@@ -576,11 +576,13 @@
     n_group = rows * 4
     f32, bf16, vmem, hbm = jnp.float32, jnp.bfloat16, pl.BlockSpec(memory_space=pltpu.VMEM), pl.BlockSpec(memory_space=pltpu.HBM)
     dma = pltpu.SemaphoreType.DMA
-    args, specs = [x, gains], [hbm if post is None else vmem, hbm]
+    args, specs = [x, gains], [hbm, hbm]
     raw = post is not None and post[0].ndim == 2
+    if post is not None and not raw:
+        specs[0] = vmem
     n_stat = 4 * GROUPS
     n_misc = 5 + 3 * GROUPS
-    scratch = [pltpu.VMEM(x.shape, bf16)] if post is None else []
+    scratch = [pltpu.VMEM(x.shape, bf16)] if raw or post is None else []
     scratch += [pltpu.VMEM(gains.shape, bf16), pltpu.VMEM((GROUPS, LANES, LANES), f32), pltpu.VMEM((n_stat, 8, LANES), f32), pltpu.VMEM((n_stat, 3, 8, LANES), f32), pltpu.VMEM((GROUPS, n_group, share), bf16),
                dma((n_stat, 3)), dma((n_stat, 3)), dma((n_misc,)), dma((n_misc,)), dma((10,))]
     if post is None:

time: 331 us -> 331 us (level)
  no operation moved by 1% of the time
where the time goes in v11:
time: 331 us
  Pallas kernels  327 us (99%)
    pallas_call x3, Pallas kernels, comm(): pl.pallas_call(functools.partial(comm_kernel, cfg), out_shape=out_shape,...  274 us
    pallas_call x2, Pallas kernels, attend(): pl.pallas_call(functools.partial(attend_kernel, cache_len, n_rows, group,...  52.9 us

profile of v11, /device:TPU:0, one launch (start us, length us, event | category | flops | bytes accessed | tf_op | source)
XLA Modules:
  0.0 330.9 jit_solution(11845771673478590378)
XLA Ops:
  0.6 0.7 convert_element_type.10
  1.3 0.8 multiply_sine_fusion
  2.1 25.5 %comm_0.1.qkv_ref = f32[64,2048]{1,0:T(8,128)} custom-call(bf16[64,2560]{1,0:T(8,128)(2,1)} %bitcast.50, bf16[2,4,2560]{2,1,0:T(4,128)(2,1)} %refs_1_.5, bf16[2,640,4,256]{3,2,1,0:T(4,128)(2,1)} %refs_7_.1, bf16[2,640,2,256]{3,2,1,0:T(2,128)(2,1)} %refs_8_.1, bf16[2,640,2,256]{3,2,1,0:T(2,128)(2,1)} %refs_9_.1), custom_call_target="tpu_custom_call" | custom-call | tf_op jit(solution)/shard_map/comm_0/pallas_call | solution.py:616
  27.6 9.0 %attend_64.1 = (bf16[64,1024]{1,0:T(8,128)(2,1)}, bf16[64,256,128]{2,1,0:T(8,128)(2,1)}, bf16[64,256,128]{2,1,0:T(8,128)(2,1)}) custom-call(s32[64]{0:T(128)} %pos_ref.3, f32[64,2048]{1,0:T(8,128)} %comm_0.1.qkv_ref, f32[64,128]{1,0:T(8,128)} %get-tuple-element.22.cos_ref, f32[64,128]{1,0:T(8,128)} %get-tuple-element.21.sin_ref, ...), custom_call_target="tpu_custom_call" | custom-call | flops 67108864 | bytes 16777216 | tf_op jit(solution)/shard_map/attend_64/pallas_call | solution.py:143
  36.7 0.0 copy-start.4
  36.7 0.0 copy-start.5
  36.7 0.0 copy-start.6
  36.7 131.2 %comm_1.1 = (bf16[4,64,640]{2,1,0:T(8,128)(2,1)}, f32[64,2048]{1,0:T(8,128)}) custom-call(bf16[64,1024]{1,0:T(8,128)(2,1)} %get-tuple-element.13.refs_0_, bf16[2,4,2560]{2,1,0:T(4,128)(2,1)} %refs_1_.5, bf16[64,2560]{1,0:T(8,128)(2,1)} %bitcast.51, bf16[2,1024,640]{2,1,0:T(8,128)(2,1)} %bitcast.43, bf16[2,640,5120]{2,1,0:T(8,128)(2,1)} %refs_4_.5, ...), custom_call_target="tpu_custom_call" | custom-call | tf_op jit(solution)/shard_map/comm_1/pallas_call | solution.py:616
  167.9 0.0 copy-done.4
  167.9 0.0 copy-done.5
  168.0 0.0 copy-done.6
  168.0 0.0 copy-start.1
  168.0 1.0 copy-done.1
  169.0 0.0 copy-start
  169.0 0.0 copy-start.2
  169.0 0.0 copy-start.3
  169.0 43.9 %attend_512.1 = (bf16[64,1024]{1,0:T(8,128)(2,1)S(1)}, bf16[64,2048,128]{2,1,0:T(8,128)(2,1)}, bf16[64,2048,128]{2,1,0:T(8,128)(2,1)}) custom-call(s32[64]{0:T(128)S(1)} %copy-done.6, f32[64,2048]{1,0:T(8,128)S(1)} %copy-done.1, f32[64,128]{1,0:T(8,128)S(1)} %copy-done.5, f32[64,128]{1,0:T(8,128)S(1)} %copy-done.4, bf16[64,2048,128]{2,1,0:T(8,128)(2,1)} %bitcast.46, ...), custom_call_target="tpu_custom_call" | custom-call | flops 536870912 | bytes 134217728 | tf_op jit(solution)/shard_map/attend_512/pallas_call | solution.py:143
  212.9 0.0 copy-done
  212.9 0.0 copy-done.2
  212.9 0.0 copy-done.3
  213.0 117.3 %comm_2.1 = bf16[64,2560]{1,0:T(8,128)(2,1)S(1)} custom-call(bf16[64,1024]{1,0:T(8,128)(2,1)S(1)} %get-tuple-element.15.refs_0_, bf16[2,4,2560]{2,1,0:T(4,128)(2,1)S(1)} %copy-done.2, bf16[4,64,640]{2,1,0:T(8,128)(2,1)S(1)} %copy-done.3, bf16[2,1024,640]{2,1,0:T(8,128)(2,1)S(1)} %bitcast.44, bf16[2,640,5120]{2,1,0:T(8,128)(2,1)} %refs_4_.5, ...), custom_call_target="tpu_custom_call" | custom-call | tf_op jit(solution)/shard_map/comm_2/pallas_call | solution.py:616
  330.2 0.7 copy.28
  (1 shorter events, 0.0 us)
Async XLA Ops:
  36.7 131.3 %copy-start.4 = (f32[64,128]{1,0:T(8,128)S(1)}, f32[64,128]{1,0:T(8,128)}, u32[]{:S(2)}) copy-start(f32[64,128]{1,0:T(8,128)} %get-tuple-element.21.sin_ref) | copy-start | bytes 98308
  36.7 131.3 %copy-start.5 = (f32[64,128]{1,0:T(8,128)S(1)}, f32[64,128]{1,0:T(8,128)}, u32[]{:S(2)}) copy-start(f32[64,128]{1,0:T(8,128)} %get-tuple-element.22.cos_ref) | copy-start | bytes 98308
  36.7 131.3 %copy-start.6 = (s32[64]{0:T(128)S(1)}, s32[64]{0:T(128)}, u32[]{:S(2)}) copy-start(s32[64]{0:T(128)} %pos_ref.3) | copy-start | bytes 772
  168.0 1.0 copy-start.1
  169.0 43.9 %copy-start = (bf16[2,4,256,640]{3,2,1,0:T(8,128)(2,1)S(1)}, bf16[2,4,256,640]{3,2,1,0:T(8,128)(2,1)}, u32[]{:S(2)}) copy-start(bf16[2,4,256,640]{3,2,1,0:T(8,128)(2,1)} %param.23) | copy-start | bytes 7864324
  169.0 43.9 %copy-start.2 = (bf16[2,4,2560]{2,1,0:T(4,128)(2,1)S(1)}, bf16[2,4,2560]{2,1,0:T(4,128)(2,1)}, u32[]{:S(2)}) copy-start(bf16[2,4,2560]{2,1,0:T(4,128)(2,1)} %refs_1_.5) | copy-start | bytes 122884
  169.0 43.9 %copy-start.3 = (bf16[4,64,640]{2,1,0:T(8,128)(2,1)S(1)}, bf16[4,64,640]{2,1,0:T(8,128)(2,1)}, u32[]{:S(2)}) copy-start(bf16[4,64,640]{2,1,0:T(8,128)(2,1)} %get-tuple-element.16.refs_2_) | copy-start | bytes 983044

commit v12 on v11

--- a/solution.py
+++ b/solution.py
@@ -125,8 +125,8 @@
 def attend(qkv, tables, positions, k_cache, v_cache):
     n_rows, cache_len, kv_loc, head_dim = k_cache.shape
     halves = head_dim // LANES
-    group = 8 if cache_len <= 64 else 4
-    depth = 8 if cache_len <= 64 else 6
+    group = 32 if cache_len <= 64 else 4
+    depth = 2 if cache_len <= 64 else 6
     f32, bf16 = jnp.float32, jnp.bfloat16
 
     def flat(cache):
@@ -293,23 +293,23 @@
     def q_partner(s):
         return remote(q_mine.at[s, pl.ds(0, rows)], q_x.at[s], q_ss.at[1, s], q_rs.at[1, s], part)
 
-    def start_qkv(h):
-        before = None
+    def finish_qkv(pending):
+        if pending is not None:
+            s, copy = pending
+            copy.wait_recv()
+            q_mine[s] = q_mine[s] + q_in[s]
+            q_partner(s).start()
+
+    def start_qkv(h, pending=None):
         for c in range(n_q):
             s = h * n_q + c
             sums = jnp.dot(hp[h], wi[:, c * QKV_CHUNK:(c + 1) * QKV_CHUNK], preferred_element_type=jnp.float32)
             q_out[s] = sums[:2 * rows]
             q_mine[s] = sums[2 * rows:]
             copy = send(q_out.at[s], q_in.at[s], q_ss.at[0, s], q_rs.at[0, s], sib)
-            if c >= 1:
-                before.wait_recv()
-                q_mine[s - 1] = q_mine[s - 1] + q_in[s - 1]
-                q_partner(s - 1).start()
-            before = copy
-        before.wait_recv()
-        s = h * n_q + n_q - 1
-        q_mine[s] = q_mine[s] + q_in[s]
-        q_partner(s).start()
+            finish_qkv(pending)
+            pending = s, copy
+        return pending
 
     def end_qkv():
         for h in range(GROUPS):
@@ -337,13 +337,15 @@
             inverse = lax.rsqrt(jnp.mean(value * value, axis=1, keepdims=True) + NORM_EPS)
             xn[mine_rows[h], :] = (value * inverse * (1.0 + g_ref[0, 0:1, :].astype(jnp.float32))).astype(jnp.bfloat16)
         copies = spread(xn, hp, 0)
+        pending = None
         relay_weights(0)
         relay_weights(1)
         for h in range(GROUPS):
             hp[h, OWN, :] = xn[mine_rows[h], my_cols]
             for copy in copies[h * 3:h * 3 + 3]:
                 copy.wait_recv()
-            start_qkv(h)
+            pending = start_qkv(h, pending)
+        finish_qkv(pending)
         end_qkv()
     else:
         head_cuts = (pl.ds(0, rows), pl.ds(rows, (GROUPS - 1) * rows))
@@ -538,7 +540,7 @@
             end_scales(h, 3, stats[h])
             for block in blocks:
                 hp[h, block, :] = scaled(h, block, hid_ref[h, block, :].astype(jnp.float32), 3).astype(jnp.bfloat16)
-            start_qkv(h)
+            finish_qkv(start_qkv(h))
 
         ff_sums(0)
         ff_sums(1)

time: 331 us -> 330 us (level)
  no operation moved by 1% of the time
where the time goes in v12:
time: 330 us
  Pallas kernels  326 us (99%)
    pallas_call x3, Pallas kernels, comm(): pl.pallas_call(functools.partial(comm_kernel, cfg), out_shape=out_shape,...  274 us
    pallas_call x2, Pallas kernels, attend(): pl.pallas_call(functools.partial(attend_kernel, cache_len, n_rows, group,...  52.3 us

profile of v12, /device:TPU:0, one launch (start us, length us, event | category | flops | bytes accessed | tf_op | source)
XLA Modules:
  0.0 330.3 jit_solution(5241623757693801769)
XLA Ops:
  0.6 0.7 convert_element_type.10
  1.3 0.8 multiply_sine_fusion
  2.1 25.5 %comm_0.1.qkv_ref = f32[64,2048]{1,0:T(8,128)} custom-call(bf16[64,2560]{1,0:T(8,128)(2,1)} %bitcast.50, bf16[2,4,2560]{2,1,0:T(4,128)(2,1)} %refs_1_.5, bf16[2,640,4,256]{3,2,1,0:T(4,128)(2,1)} %refs_7_.1, bf16[2,640,2,256]{3,2,1,0:T(2,128)(2,1)} %refs_8_.1, bf16[2,640,2,256]{3,2,1,0:T(2,128)(2,1)} %refs_9_.1), custom_call_target="tpu_custom_call" | custom-call | tf_op jit(solution)/shard_map/comm_0/pallas_call | solution.py:618
  27.6 8.4 %attend_64.1 = (bf16[64,1024]{1,0:T(8,128)(2,1)}, bf16[64,256,128]{2,1,0:T(8,128)(2,1)}, bf16[64,256,128]{2,1,0:T(8,128)(2,1)}) custom-call(s32[64]{0:T(128)} %pos_ref.3, f32[64,2048]{1,0:T(8,128)} %comm_0.1.qkv_ref, f32[64,128]{1,0:T(8,128)} %get-tuple-element.22.cos_ref, f32[64,128]{1,0:T(8,128)} %get-tuple-element.21.sin_ref, ...), custom_call_target="tpu_custom_call" | custom-call | flops 67108864 | bytes 16777216 | tf_op jit(solution)/shard_map/attend_64/pallas_call | solution.py:143
  36.0 0.0 copy-start.4
  36.0 0.0 copy-start.5
  36.0 0.0 copy-start.6
  36.0 131.2 %comm_1.1 = (bf16[4,64,640]{2,1,0:T(8,128)(2,1)}, f32[64,2048]{1,0:T(8,128)}) custom-call(bf16[64,1024]{1,0:T(8,128)(2,1)} %get-tuple-element.13.refs_0_, bf16[2,4,2560]{2,1,0:T(4,128)(2,1)} %refs_1_.5, bf16[64,2560]{1,0:T(8,128)(2,1)} %bitcast.51, bf16[2,1024,640]{2,1,0:T(8,128)(2,1)} %bitcast.43, bf16[2,640,5120]{2,1,0:T(8,128)(2,1)} %refs_4_.5, ...), custom_call_target="tpu_custom_call" | custom-call | tf_op jit(solution)/shard_map/comm_1/pallas_call | solution.py:618
  167.2 0.0 copy-done.4
  167.3 0.0 copy-done.5
  167.3 0.0 copy-done.6
  167.3 0.0 copy-start.1
  167.3 1.0 copy-done.1
  168.3 0.0 copy-start
  168.3 0.0 copy-start.2
  168.3 0.0 copy-start.3
  168.3 43.9 %attend_512.1 = (bf16[64,1024]{1,0:T(8,128)(2,1)S(1)}, bf16[64,2048,128]{2,1,0:T(8,128)(2,1)}, bf16[64,2048,128]{2,1,0:T(8,128)(2,1)}) custom-call(s32[64]{0:T(128)S(1)} %copy-done.6, f32[64,2048]{1,0:T(8,128)S(1)} %copy-done.1, f32[64,128]{1,0:T(8,128)S(1)} %copy-done.5, f32[64,128]{1,0:T(8,128)S(1)} %copy-done.4, bf16[64,2048,128]{2,1,0:T(8,128)(2,1)} %bitcast.46, ...), custom_call_target="tpu_custom_call" | custom-call | flops 536870912 | bytes 134217728 | tf_op jit(solution)/shard_map/attend_512/pallas_call | solution.py:143
  212.2 0.0 copy-done
  212.2 0.0 copy-done.2
  212.3 0.0 copy-done.3
  212.3 117.3 %comm_2.1 = bf16[64,2560]{1,0:T(8,128)(2,1)S(1)} custom-call(bf16[64,1024]{1,0:T(8,128)(2,1)S(1)} %get-tuple-element.15.refs_0_, bf16[2,4,2560]{2,1,0:T(4,128)(2,1)S(1)} %copy-done.2, bf16[4,64,640]{2,1,0:T(8,128)(2,1)S(1)} %copy-done.3, bf16[2,1024,640]{2,1,0:T(8,128)(2,1)S(1)} %bitcast.44, bf16[2,640,5120]{2,1,0:T(8,128)(2,1)} %refs_4_.5, ...), custom_call_target="tpu_custom_call" | custom-call | tf_op jit(solution)/shard_map/comm_2/pallas_call | solution.py:618
  329.5 0.7 copy.28
  (1 shorter events, 0.0 us)
Async XLA Ops:
  36.0 131.3 %copy-start.4 = (f32[64,128]{1,0:T(8,128)S(1)}, f32[64,128]{1,0:T(8,128)}, u32[]{:S(2)}) copy-start(f32[64,128]{1,0:T(8,128)} %get-tuple-element.21.sin_ref) | copy-start | bytes 98308
  36.0 131.3 %copy-start.5 = (f32[64,128]{1,0:T(8,128)S(1)}, f32[64,128]{1,0:T(8,128)}, u32[]{:S(2)}) copy-start(f32[64,128]{1,0:T(8,128)} %get-tuple-element.22.cos_ref) | copy-start | bytes 98308
  36.0 131.3 %copy-start.6 = (s32[64]{0:T(128)S(1)}, s32[64]{0:T(128)}, u32[]{:S(2)}) copy-start(s32[64]{0:T(128)} %pos_ref.3) | copy-start | bytes 772
  167.3 1.0 copy-start.1
  168.3 43.9 %copy-start = (bf16[2,4,256,640]{3,2,1,0:T(8,128)(2,1)S(1)}, bf16[2,4,256,640]{3,2,1,0:T(8,128)(2,1)}, u32[]{:S(2)}) copy-start(bf16[2,4,256,640]{3,2,1,0:T(8,128)(2,1)} %param.23) | copy-start | bytes 7864324
  168.3 43.9 %copy-start.2 = (bf16[2,4,2560]{2,1,0:T(4,128)(2,1)S(1)}, bf16[2,4,2560]{2,1,0:T(4,128)(2,1)}, u32[]{:S(2)}) copy-start(bf16[2,4,2560]{2,1,0:T(4,128)(2,1)} %refs_1_.5) | copy-start | bytes 122884
  168.3 43.9 %copy-start.3 = (bf16[4,64,640]{2,1,0:T(8,128)(2,1)S(1)}, bf16[4,64,640]{2,1,0:T(8,128)(2,1)}, u32[]{:S(2)}) copy-start(bf16[4,64,640]{2,1,0:T(8,128)(2,1)} %get-tuple-element.16.refs_2_) | copy-start | bytes 983044

commit v13 on v12

--- a/solution.py
+++ b/solution.py
@@ -125,8 +125,8 @@
 def attend(qkv, tables, positions, k_cache, v_cache):
     n_rows, cache_len, kv_loc, head_dim = k_cache.shape
     halves = head_dim // LANES
-    group = 32 if cache_len <= 64 else 4
-    depth = 2 if cache_len <= 64 else 6
+    group = 16 if cache_len <= 64 else 4
+    depth = 4 if cache_len <= 64 else 8
     f32, bf16 = jnp.float32, jnp.bfloat16
 
     def flat(cache):
@@ -148,7 +148,7 @@
         scratch_shapes=[pltpu.VMEM(block, bf16), pltpu.VMEM(block, bf16), pltpu.VMEM((n_rows, 8, LANES), f32), pltpu.VMEM((n_rows, 16, LANES), f32),
                         pltpu.VMEM((n_rows, 16, LANES), f32), pltpu.VMEM((n_rows, 8, LANES), f32), pltpu.VMEM((group, 8, n_cols), f32), pltpu.VMEM((group, 8, n_cols), bf16),
                         dma((2, depth)), dma((2, depth))],
-        compiler_params=pltpu.CompilerParams(vmem_limit_bytes=int((62 if cache_len <= 64 else 34) * 2**20)),
+        compiler_params=pltpu.CompilerParams(vmem_limit_bytes=int((62 if cache_len <= 64 else 42) * 2**20)),
         cost_estimate=pl.CostEstimate(flops=n_rows * 8 * n_cols * LANES * 4, bytes_accessed=4 * k_flat.size * 2, transcendentals=0),
         name=f"attend_{cache_len}",
     )(positions, qkv, *tables, k_flat, v_flat)

time: 330 us -> 330 us (level)
  no operation moved by 1% of the time
where the time goes in v13:
time: 330 us
  Pallas kernels  326 us (99%)
    pallas_call x3, Pallas kernels, comm(): pl.pallas_call(functools.partial(comm_kernel, cfg), out_shape=out_shape,...  274 us
    pallas_call x2, Pallas kernels, attend(): pl.pallas_call(functools.partial(attend_kernel, cache_len, n_rows, group,...  52.2 us

profile of v13, /device:TPU:0, one launch (start us, length us, event | category | flops | bytes accessed | tf_op | source)
XLA Modules:
  0.0 330.2 jit_solution(6929204456516406544)
XLA Ops:
  0.6 0.7 convert_element_type.10
  1.3 0.8 multiply_sine_fusion
  2.1 25.5 %comm_0.1.qkv_ref = f32[64,2048]{1,0:T(8,128)} custom-call(bf16[64,2560]{1,0:T(8,128)(2,1)} %bitcast.50, bf16[2,4,2560]{2,1,0:T(4,128)(2,1)} %refs_1_.5, bf16[2,640,4,256]{3,2,1,0:T(4,128)(2,1)} %refs_7_.1, bf16[2,640,2,256]{3,2,1,0:T(2,128)(2,1)} %refs_8_.1, bf16[2,640,2,256]{3,2,1,0:T(2,128)(2,1)} %refs_9_.1), custom_call_target="tpu_custom_call" | custom-call | tf_op jit(solution)/shard_map/comm_0/pallas_call | solution.py:618
  27.6 8.2 %attend_64.1 = (bf16[64,1024]{1,0:T(8,128)(2,1)}, bf16[64,256,128]{2,1,0:T(8,128)(2,1)}, bf16[64,256,128]{2,1,0:T(8,128)(2,1)}) custom-call(s32[64]{0:T(128)} %pos_ref.3, f32[64,2048]{1,0:T(8,128)} %comm_0.1.qkv_ref, f32[64,128]{1,0:T(8,128)} %get-tuple-element.22.cos_ref, f32[64,128]{1,0:T(8,128)} %get-tuple-element.21.sin_ref, ...), custom_call_target="tpu_custom_call" | custom-call | flops 67108864 | bytes 16777216 | tf_op jit(solution)/shard_map/attend_64/pallas_call | solution.py:143
  35.8 0.0 copy-start.4
  35.8 0.0 copy-start.5
  35.8 0.0 copy-start.6
  35.8 131.2 %comm_1.1 = (bf16[4,64,640]{2,1,0:T(8,128)(2,1)}, f32[64,2048]{1,0:T(8,128)}) custom-call(bf16[64,1024]{1,0:T(8,128)(2,1)} %get-tuple-element.13.refs_0_, bf16[2,4,2560]{2,1,0:T(4,128)(2,1)} %refs_1_.5, bf16[64,2560]{1,0:T(8,128)(2,1)} %bitcast.51, bf16[2,1024,640]{2,1,0:T(8,128)(2,1)} %bitcast.43, bf16[2,640,5120]{2,1,0:T(8,128)(2,1)} %refs_4_.5, ...), custom_call_target="tpu_custom_call" | custom-call | tf_op jit(solution)/shard_map/comm_1/pallas_call | solution.py:618
  167.1 0.0 copy-done.4
  167.1 0.0 copy-done.5
  167.1 0.0 copy-done.6
  167.1 0.0 copy-start.1
  167.1 1.0 copy-done.1
  168.1 0.0 copy-start
  168.1 0.0 copy-start.2
  168.1 0.0 copy-start.3
  168.1 44.0 %attend_512.1 = (bf16[64,1024]{1,0:T(8,128)(2,1)S(1)}, bf16[64,2048,128]{2,1,0:T(8,128)(2,1)}, bf16[64,2048,128]{2,1,0:T(8,128)(2,1)}) custom-call(s32[64]{0:T(128)S(1)} %copy-done.6, f32[64,2048]{1,0:T(8,128)S(1)} %copy-done.1, f32[64,128]{1,0:T(8,128)S(1)} %copy-done.5, f32[64,128]{1,0:T(8,128)S(1)} %copy-done.4, bf16[64,2048,128]{2,1,0:T(8,128)(2,1)} %bitcast.46, ...), custom_call_target="tpu_custom_call" | custom-call | flops 536870912 | bytes 134217728 | tf_op jit(solution)/shard_map/attend_512/pallas_call | solution.py:143
  212.1 0.0 copy-done
  212.1 0.0 copy-done.2
  212.2 0.0 copy-done.3
  212.2 117.3 %comm_2.1 = bf16[64,2560]{1,0:T(8,128)(2,1)S(1)} custom-call(bf16[64,1024]{1,0:T(8,128)(2,1)S(1)} %get-tuple-element.15.refs_0_, bf16[2,4,2560]{2,1,0:T(4,128)(2,1)S(1)} %copy-done.2, bf16[4,64,640]{2,1,0:T(8,128)(2,1)S(1)} %copy-done.3, bf16[2,1024,640]{2,1,0:T(8,128)(2,1)S(1)} %bitcast.44, bf16[2,640,5120]{2,1,0:T(8,128)(2,1)} %refs_4_.5, ...), custom_call_target="tpu_custom_call" | custom-call | tf_op jit(solution)/shard_map/comm_2/pallas_call | solution.py:618
  329.4 0.7 copy.28
  (1 shorter events, 0.0 us)
Async XLA Ops:
  35.8 131.3 %copy-start.4 = (f32[64,128]{1,0:T(8,128)S(1)}, f32[64,128]{1,0:T(8,128)}, u32[]{:S(2)}) copy-start(f32[64,128]{1,0:T(8,128)} %get-tuple-element.21.sin_ref) | copy-start | bytes 98308
  35.8 131.3 %copy-start.5 = (f32[64,128]{1,0:T(8,128)S(1)}, f32[64,128]{1,0:T(8,128)}, u32[]{:S(2)}) copy-start(f32[64,128]{1,0:T(8,128)} %get-tuple-element.22.cos_ref) | copy-start | bytes 98308
  35.8 131.3 %copy-start.6 = (s32[64]{0:T(128)S(1)}, s32[64]{0:T(128)}, u32[]{:S(2)}) copy-start(s32[64]{0:T(128)} %pos_ref.3) | copy-start | bytes 772
  167.1 1.0 copy-start.1
  168.1 44.0 %copy-start = (bf16[2,4,256,640]{3,2,1,0:T(8,128)(2,1)S(1)}, bf16[2,4,256,640]{3,2,1,0:T(8,128)(2,1)}, u32[]{:S(2)}) copy-start(bf16[2,4,256,640]{3,2,1,0:T(8,128)(2,1)} %param.23) | copy-start | bytes 7864324
  168.1 44.0 %copy-start.2 = (bf16[2,4,2560]{2,1,0:T(4,128)(2,1)S(1)}, bf16[2,4,2560]{2,1,0:T(4,128)(2,1)}, u32[]{:S(2)}) copy-start(bf16[2,4,2560]{2,1,0:T(4,128)(2,1)} %refs_1_.5) | copy-start | bytes 122884
  168.1 44.0 %copy-start.3 = (bf16[4,64,640]{2,1,0:T(8,128)(2,1)S(1)}, bf16[4,64,640]{2,1,0:T(8,128)(2,1)}, u32[]{:S(2)}) copy-start(bf16[4,64,640]{2,1,0:T(8,128)(2,1)} %get-tuple-element.16.refs_2_) | copy-start | bytes 983044
